TPU v7x, 256 devices: a whole 4x4x8 slice. The times are simulated.
256 devices in a mesh: gx: 4 (over z_hi), gy: 8 (over x, core), gz: 8 (over y, z_lo).
Axes of the slice: x: 4, y: 4, z: 8 (z_hi: 4, z_lo: 2; z = z_hi * 2 + z_lo), core: 2. Of those that a mesh axis runs over, the one named last changes fastest.
Arguments:
- order_real: float32 [128, 256, 1024], P('gz', 'gx', 'gy'), may hold values from -2.5 to 2.5
- order_imag: float32 [128, 256, 1024], P('gz', 'gx', 'gy'), may hold values from -2.5 to 2.5
- phase_z: float32 [128, 256, 1024], P('gz', 'gx', 'gy'), may hold values from -3.140625 to 3.140625
- phase_x: float32 [128, 256, 1024], P('gz', 'gx', 'gy'), may hold values from -3.140625 to 3.140625
- phase_y: float32 [128, 256, 1024], P('gz', 'gx', 'gy'), may hold values from -3.140625 to 3.140625
- material: int32 [128, 256, 1024], P('gz', 'gx', 'gy'), may hold values from 0 to 7
- levels: float32 [8], replicated, may hold values from -0.5 to 1.5
Outputs:
- final_real: float32 [128, 256, 1024], P('gz', 'gx', 'gy')
- final_imag: float32 [128, 256, 1024], P('gz', 'gx', 'gy')
- circulation: float32 [128, 256, 1024], P('gz', ('gx', 'gy'))
- current_flux: float32 [128, 256, 1024], P('gz', ('gx', 'gy'))
All inputs are finite; a program needn't handle non-finite values.
Results may differ from a plain program's by a relative error of at most 0.0003.
Values sent between devices are 32-bit elements; how exact they have to be, the bound alone decides.
No kernel may reach another device: no remote copies, remote signals or barrier semaphores. Data moves between devices by JAX's collectives and lax.ppermute only.
A program may use at most 64 MiB of HBM per device.

v0:
```python
import jax
import jax.numpy as jnp
from jax import lax
from jax.sharding import PartitionSpec as P

STEPS = 2
LEVELS = 8


time_step = 0.15


def passed_along(block, axis, distance):
    devices = range(lax.axis_size(axis))
    route = [(i - distance, i) for i in devices if i - distance in devices]
    return lax.ppermute(block, axis, route)


def with_halo(x, sides, width):
    edges = {}
    for axis, dim in sides:
        size, length = (lax.axis_size(axis), x.shape[dim])
        up = [(i, (i + 1) % size) for i in range(size - 1)]
        last = lax.slice_in_dim(x, length - width, length, axis=dim)
        initial = lax.slice_in_dim(x, 0, width, axis=dim)
        edges[dim] = (
            lax.ppermute(last, axis, up),
            lax.ppermute(initial, axis, [(b, a) for a, b in up]),
        )
    done = []
    for _, dim in sides:
        low, high = edges[dim]
        around = [(width, width) if d in done else (0, 0) for d in range(x.ndim)]
        x = jnp.concatenate([jnp.pad(low, around), x, jnp.pad(high, around)], axis=dim)
        done.append(dim)
    return x


def in_one_piece(arrays, axis, split_dim, concat_dim, along):
    ends, at = ([], 0)
    for a in arrays[:-1]:
        at += a.shape[along]
        ends.append(at)
    both = jnp.concatenate(arrays, axis=along)
    return tuple(
        jnp.split(
            lax.all_to_all(both, axis, split_axis=split_dim, concat_axis=concat_dim, tiled=True),
            ends,
            axis=along,
        )
    )


def inner(values, direction, offset):
    slicer = [slice(1, length - 1) for length in values.shape]
    length = values.shape[direction]
    slicer[direction] = slice(1 + offset, length - 1 + offset)
    return values[tuple(slicer)]


def advance(real_part, imag_part, cosines, sine_parts, epsilon):
    centre_real = inner(real_part, 0, 0)
    centre_imag = inner(imag_part, 0, 0)
    lap_real = -6.0 * centre_real
    lap_imag = -6.0 * centre_imag
    for direction in range(3):
        cosine = inner(cosines[direction], direction, 0)
        sine_part = inner(sine_parts[direction], direction, 0)
        ahead_real = inner(real_part, direction, 1)
        ahead_imag = inner(imag_part, direction, 1)
        lap_real = lap_real + cosine * ahead_real - sine_part * ahead_imag
        lap_imag = lap_imag + cosine * ahead_imag + sine_part * ahead_real
        cosine = inner(cosines[direction], direction, -1)
        sine_part = inner(sine_parts[direction], direction, -1)
        behind_real = inner(real_part, direction, -1)
        behind_imag = inner(imag_part, direction, -1)
        lap_real = lap_real + cosine * behind_real + sine_part * behind_imag
        lap_imag = lap_imag + cosine * behind_imag - sine_part * behind_real
    density = centre_real * centre_real + centre_imag * centre_imag
    new_real = centre_real + time_step * ((epsilon - density) * centre_real + lap_real)
    new_imag = centre_imag + time_step * ((epsilon - density) * centre_imag + lap_imag)
    return (new_real, new_imag)


def current(first_real, first_imag, second_real, second_imag, phase):
    cosine = jnp.cos(phase)
    sine_part = jnp.sin(phase)
    turned_real = cosine * second_real - sine_part * second_imag
    turned_imag = cosine * second_imag + sine_part * second_real
    return first_real * turned_imag - first_imag * turned_real


def analyse(upper_real, upper_imag, phase_along_x, phase_along_y):
    rows = phase_along_x.shape[1]
    cols = phase_along_y.shape[2]
    current_x = current(
        upper_real[:, :rows, :],
        upper_imag[:, :rows, :],
        upper_real[:, 1:, :],
        upper_imag[:, 1:, :],
        phase_along_x,
    )
    current_y = current(
        upper_real[:, :, :cols],
        upper_imag[:, :, :cols],
        upper_real[:, :, 1:],
        upper_imag[:, :, 1:],
        phase_along_y,
    )
    circulation = (
        current_x[:, :, :cols] + current_y[:, 1:, :] - current_x[:, :, 1:] - current_y[:, :rows, :]
    )
    return (circulation, current_x[:, :, :cols])


def prefix_sum(values):
    length = values.shape[-1]
    width = 128
    blocks = values.reshape(values.shape[:-1] + (length // width, width))
    triangle = (
        lax.broadcasted_iota(jnp.int32, (width, width), 0)
        <= lax.broadcasted_iota(jnp.int32, (width, width), 1)
    ).astype(jnp.float32)
    within = jnp.einsum("abcd,de->abce", blocks, triangle, precision=lax.Precision.HIGHEST)
    totals = within[..., -1]
    offsets = jnp.cumsum(totals, axis=-1) - totals
    return (within + offsets[..., None]).reshape(values.shape)


def extend_below(phase, below, direction):
    joined = jnp.concatenate([below, phase], axis=direction)
    widths = [(1, 1), (1, 1), (1, 1)]
    widths[direction] = (0, 1)
    return jnp.pad(joined, widths)


def shards(order_real, order_imag, phase_z, phase_x, phase_y, material, levels):
    epsilon = jnp.zeros(order_real.shape, jnp.float32)
    for level in range(LEVELS):
        epsilon = epsilon + jnp.where(material == level, levels[level], 0.0)
    below_z = passed_along(phase_z[-1:], "gz", 1)
    below_x = passed_along(phase_x[:, -1:], "gx", 1)
    below_y = passed_along(phase_y[:, :, -1:], "gy", 1)
    link_halo = [
        extend_below(phase_z, below_z, 0),
        extend_below(phase_x, below_x, 1),
        extend_below(phase_y, below_y, 2),
    ]
    cosines = [jnp.cos(phase) for phase in link_halo]
    sine_parts = [jnp.sin(phase) for phase in link_halo]
    real_part, imag_part = (order_real, order_imag)
    for turn in range(STEPS):
        padded = (
            with_halo(real_part, (("gx", 1), ("gy", 2), ("gz", 0)), 1),
            with_halo(imag_part, (("gx", 1), ("gy", 2), ("gz", 0)), 1),
        )
        real_part, imag_part = advance(padded[0], padded[1], cosines, sine_parts, epsilon)
    row_real, row_imag, row_phase_x, row_phase_y = in_one_piece(
        (real_part, imag_part, phase_x, phase_y), "gy", 1, 2, 0
    )
    following = passed_along(
        (row_real[:, :1], row_imag[:, :1], row_phase_y[:, :1]), ("gx", "gy"), -1
    )
    column_pad = ((0, 0), (0, 0), (0, 1))
    upper_real = jnp.pad(jnp.concatenate([row_real, following[0]], axis=1), column_pad)
    upper_imag = jnp.pad(jnp.concatenate([row_imag, following[1]], axis=1), column_pad)
    phase_along_x = jnp.pad(row_phase_x, column_pad)
    phase_along_y = jnp.concatenate([row_phase_y, following[2]], axis=1)
    circulation, current_x = analyse(upper_real, upper_imag, phase_along_x, phase_along_y)
    current_flux = prefix_sum(current_x)
    return (real_part, imag_part, circulation, current_flux)


def solution(mesh):
    in_specs = (
        P("gz", "gx", "gy"),
        P("gz", "gx", "gy"),
        P("gz", "gx", "gy"),
        P("gz", "gx", "gy"),
        P("gz", "gx", "gy"),
        P("gz", "gx", "gy"),
        P(),
    )
    out_specs = (
        P("gz", "gx", "gy"),
        P("gz", "gx", "gy"),
        P("gz", ("gx", "gy"), None),
        P("gz", ("gx", "gy"), None),
    )
    return jax.shard_map(shards, mesh=mesh, in_specs=in_specs, out_specs=out_specs, check_vma=False)
```

profile of v0, /device:TPU:79, one launch (start us, length us, event | category | flops | bytes accessed | tf_op | source)
XLA Modules:
  0.0 229.4 jit_solution(12253623082609452055)
XLA Ops:
  2.0 6.1 %collective-permute-start.7 = (f32[16,1,128]{2,0,1:T(8,128)S(1)}, f32[16,1,128]{2,0,1:T(8,128)S(1)}, u32[]{:S(2)}, u32[]{:S(2)}) collective-permute-start(f32[16,1,128]{2,0,1:T(8,128)S(1)} %get-tuple-element.40), channel_id=1, source_target_pairs={{0,64},{64,128},{128,192},{1,65},{65,129},{129,193},{2,66},{66,130... | collective-permute-start | bytes 24584 | tf_op jit(solution)/shard_map/ppermute | solution.py:27
  12.5 4.3 %collective-permute-start.9 = (f32[16,64,1]{2,0,1:T(8,128)S(1)}, f32[16,64,1]{2,0,1:T(8,128)S(1)}, u32[]{:S(2)}, u32[]{:S(2)}) collective-permute-start(f32[16,64,1]{2,0,1:T(8,128)S(1)} %get-tuple-element.37), channel_id=1, source_target_pairs={{8,0},{16,8},{24,16},{32,24},{40,32},{48,40},{56,48},{9,1},{17,9},... | collective-permute-start | bytes 12296 | tf_op jit(solution)/shard_map/ppermute | solution.py:28
  20.0 4.3 %collective-permute-start.4 = (f32[16,64,1]{2,0,1:T(8,128)S(1)}, f32[16,64,1]{2,0,1:T(8,128)S(1)}, u32[]{:S(2)}, u32[]{:S(2)}) collective-permute-start(f32[16,64,1]{2,0,1:T(8,128)S(1)} %get-tuple-element.39), channel_id=1, source_target_pairs={{8,0},{16,8},{24,16},{32,24},{40,32},{48,40},{56,48},{9,1},{17,9},... | collective-permute-start | bytes 12296 | tf_op jit(solution)/shard_map/ppermute | solution.py:28
  24.3 6.5 %fusion.31 = (f32[18,66,130]{2,0,1:T(8,128)S(1)}, f32[18,66,130]{2,0,1:T(8,128)S(1)}) fusion(f32[16,64,128]{2,0,1:T(8,128)S(1)} %copy.49, f32[16,64,1]{2,0,1:T(8,128)S(1)} %collective-permute-done.14), kind=kLoop, calls=%fused_computation.125 | loop fusion | flops 2471040 | bytes 1763904 | tf_op jit(solution)/shard_map/cos | solution.py:149
  33.6 3.6 %collective-permute-start.11 = (f32[1,64,128]{2,0,1:T(1,128)S(1)}, f32[1,64,128]{2,0,1:T(1,128)S(1)}, u32[]{:S(2)}, u32[]{:S(2)}) collective-permute-start(f32[1,64,128]{2,0,1:T(1,128)S(1)} %bitcast.57), channel_id=1, source_target_pairs={{0,1},{1,2},{2,3},{3,4},{4,5},{5,6},{6,7},{8,9},{9,10},{10,11},{11... | collective-permute-start | bytes 98312 | tf_op jit(solution)/shard_map/ppermute | solution.py:27
  48.0 4.4 %collective-permute-start.13 = (f32[16,1,128]{2,0,1:T(8,128)S(1)}, f32[16,1,128]{2,0,1:T(8,128)S(1)}, u32[]{:S(2)}, u32[]{:S(2)}) collective-permute-start(f32[16,1,128]{2,0,1:T(8,128)S(1)} %slice.395), channel_id=1, source_target_pairs={{0,64},{64,128},{128,192},{1,65},{65,129},{129,193},{2,66},{66,130... | collective-permute-start | bytes 24584 | tf_op jit(solution)/shard_map/ppermute | solution.py:16
  55.2 6.4 %fusion.29 = (f32[18,66,130]{2,0,1:T(8,128)S(1)}, f32[18,66,130]{2,0,1:T(8,128)S(1)}) fusion(f32[16,64,128]{2,0,1:T(8,128)S(1)} %copy.43, f32[16,1,128]{2,0,1:T(8,128)S(1)} %collective-permute-done.13), kind=kLoop, calls=%fused_computation.123 | loop fusion | flops 2471040 | bytes 1768000 | tf_op jit(solution)/shard_map/cos | solution.py:149
  63.9 4.7 %collective-permute-done.3 = f32[16,1,128]{2,0,1:T(8,128)S(1)} collective-permute-done((f32[16,1,128]{2,0,1:T(8,128)S(1)}, f32[16,1,128]{2,0,1:T(8,128)S(1)}, u32[]{:S(2)}, u32[]{:S(2)}) %collective-permute-start.3) | collective-permute-done | bytes 8224 | tf_op jit(solution)/shard_map/ppermute | solution.py:28
  68.6 3.5 %collective-permute-start.10 = (f32[1,64,128]{2,0,1:T(1,128)S(1)}, f32[1,64,128]{2,0,1:T(1,128)S(1)}, u32[]{:S(2)}, u32[]{:S(2)}) collective-permute-start(f32[1,64,128]{2,0,1:T(1,128)S(1)} %bitcast.54), channel_id=1, source_target_pairs={{1,0},{2,1},{3,2},{4,3},{5,4},{6,5},{7,6},{9,8},{10,9},{11,10},{12... | collective-permute-start | bytes 98312 | tf_op jit(solution)/shard_map/ppermute | solution.py:28
  72.1 6.7 %fusion.27 = (f32[18,66,130]{2,0,1:T(8,128)S(1)}, f32[18,66,130]{2,0,1:T(8,128)S(1)}) fusion(f32[16,64,128]{2,0,1:T(8,128)S(1)} %copy.28, f32[1,64,128]{2,0,1:T(1,128)S(1)} %collective-permute-done), kind=kLoop, calls=%fused_computation.120 | loop fusion | flops 2471040 | bytes 1792576 | tf_op jit(solution)/shard_map/cos | solution.py:149
  78.9 9.3 %multiply_add_fusion.2 = f32[16,64,128]{2,0,1:T(8,128)S(1)} fusion(f32[16,64,128]{2,0,1:T(8,128)S(1)} %copy.23, f32[16,64,128]{2,0,1:T(8,128)S(1)} %copy.51, f32[18,66,130]{2,0,1:T(8,128)S(1)} %get-tuple-element.13, f32[18,66,130]{2,0,1:T(8,128)S(1)} %get-tuple-element.12, f32[18,66,130]{2,0,1:T(8,128)S(1)} %get-tuple-element.19, ...), kind=kLoop, calls=%fused_computation.115 | loop fusion | flops 11010048 | bytes 9650720 | tf_op jit(solution)/shard_map/add | solution.py:81
  88.4 9.3 %multiply_add_fusion.3 = f32[16,64,128]{2,0,1:T(8,128)S(1)} fusion(f32[16,64,128]{2,0,1:T(8,128)S(1)} %copy.51, f32[16,64,128]{2,0,1:T(8,128)S(1)} %copy.23, f32[18,66,130]{2,0,1:T(8,128)S(1)} %get-tuple-element.13, f32[18,66,130]{2,0,1:T(8,128)S(1)} %get-tuple-element.12, f32[18,66,130]{2,0,1:T(8,128)S(1)} %get-tuple-element.19, ...), kind=kLoop, calls=%fused_computation.116 | loop fusion | flops 11010048 | bytes 9650720 | tf_op jit(solution)/shard_map/add | solution.py:80
  97.9 4.3 %collective-permute-start.16 = (f32[16,1,128]{2,0,1:T(8,128)S(1)}, f32[16,1,128]{2,0,1:T(8,128)S(1)}, u32[]{:S(2)}, u32[]{:S(2)}) collective-permute-start(f32[16,1,128]{2,0,1:T(8,128)S(1)} %get-tuple-element.30), channel_id=1, source_target_pairs={{0,64},{64,128},{128,192},{1,65},{65,129},{129,193},{2,66},{66,130... | collective-permute-start | bytes 24584 | tf_op jit(solution)/shard_map/ppermute | solution.py:27
  103.5 9.6 %collective-permute-start.23 = (f32[16,64,1]{2,0,1:T(8,128)S(1)}, f32[16,64,1]{2,0,1:T(8,128)S(1)}, u32[]{:S(2)}, u32[]{:S(2)}) collective-permute-start(f32[16,64,1]{2,0,1:T(8,128)S(1)} %get-tuple-element.25), channel_id=1, source_target_pairs={{8,0},{16,8},{24,16},{32,24},{40,32},{48,40},{56,48},{9,1},{17,9},... | collective-permute-start | bytes 12296 | tf_op jit(solution)/shard_map/ppermute | solution.py:28
  114.4 4.3 %collective-permute-start.18 = (f32[16,64,1]{2,0,1:T(8,128)S(1)}, f32[16,64,1]{2,0,1:T(8,128)S(1)}, u32[]{:S(2)}, u32[]{:S(2)}) collective-permute-start(f32[16,64,1]{2,0,1:T(8,128)S(1)} %get-tuple-element.27), channel_id=1, source_target_pairs={{8,0},{16,8},{24,16},{32,24},{40,32},{48,40},{56,48},{9,1},{17,9},... | collective-permute-start | bytes 12296 | tf_op jit(solution)/shard_map/ppermute | solution.py:28
  122.7 4.3 %collective-permute-start.24 = (f32[1,64,128]{2,0,1:T(1,128)S(1)}, f32[1,64,128]{2,0,1:T(1,128)S(1)}, u32[]{:S(2)}, u32[]{:S(2)}) collective-permute-start(f32[1,64,128]{2,0,1:T(1,128)S(1)} %get-tuple-element.21), channel_id=1, source_target_pairs={{1,0},{2,1},{3,2},{4,3},{5,4},{6,5},{7,6},{9,8},{10,9},{11,10},{12... | collective-permute-start | bytes 98312 | tf_op jit(solution)/shard_map/ppermute | solution.py:28
  129.0 4.1 %collective-permute-start.19 = (f32[1,64,128]{2,0,1:T(1,128)S(1)}, f32[1,64,128]{2,0,1:T(1,128)S(1)}, u32[]{:S(2)}, u32[]{:S(2)}) collective-permute-start(f32[1,64,128]{2,0,1:T(1,128)S(1)} %get-tuple-element.23), channel_id=1, source_target_pairs={{1,0},{2,1},{3,2},{4,3},{5,4},{6,5},{7,6},{9,8},{10,9},{11,10},{12... | collective-permute-start | bytes 98312 | tf_op jit(solution)/shard_map/ppermute | solution.py:28
  133.2 5.5 %collective-permute-start.21 = (f32[16,1,128]{2,0,1:T(8,128)S(1)}, f32[16,1,128]{2,0,1:T(8,128)S(1)}, u32[]{:S(2)}, u32[]{:S(2)}) collective-permute-start(f32[16,1,128]{2,0,1:T(8,128)S(1)} %get-tuple-element.28), channel_id=1, source_target_pairs={{0,64},{64,128},{128,192},{1,65},{65,129},{129,193},{2,66},{66,130... | collective-permute-start | bytes 24584 | tf_op jit(solution)/shard_map/ppermute | solution.py:27
  141.7 4.4 %collective-permute-done.22 = f32[16,1,128]{2,0,1:T(8,128)S(1)} collective-permute-done((f32[16,1,128]{2,0,1:T(8,128)S(1)}, f32[16,1,128]{2,0,1:T(8,128)S(1)}, u32[]{:S(2)}, u32[]{:S(2)}) %collective-permute-start.22) | collective-permute-done | bytes 8224 | tf_op jit(solution)/shard_map/ppermute | solution.py:28
  146.2 9.9 %multiply_add_fusion = f32[16,64,128]{2,0,1:T(8,128)S(1)} fusion(f32[16,64,128]{2,0,1:T(8,128)S(1)} %multiply_add_fusion.2, f32[16,64,128]{2,0,1:T(8,128)S(1)} %multiply_add_fusion.3, f32[18,66,130]{2,0,1:T(8,128)S(1)} %get-tuple-element.13, f32[18,66,130]{2,0,1:T(8,128)S(1)} %get-tuple-element.12, f32[18,66,130]{2,0,1:T(8,128)S(1)} %get-tuple-element.19, ...), kind=kLoop, calls=%fused_computation.112 | loop fusion | flops 13107200 | bytes 8569376 | tf_op jit(solution)/shard_map/add | solution.py:81
  156.1 9.9 %multiply_add_fusion.1 = f32[16,64,128]{2,0,1:T(8,128)S(1)} fusion(f32[16,64,128]{2,0,1:T(8,128)S(1)} %multiply_add_fusion.3, f32[16,64,128]{2,0,1:T(8,128)S(1)} %multiply_add_fusion.2, f32[18,66,130]{2,0,1:T(8,128)S(1)} %get-tuple-element.13, f32[18,66,130]{2,0,1:T(8,128)S(1)} %get-tuple-element.12, f32[18,66,130]{2,0,1:T(8,128)S(1)} %get-tuple-element.19, ...), kind=kLoop, calls=%fused_computation.113 | loop fusion | flops 13107200 | bytes 8569376 | tf_op jit(solution)/shard_map/add | solution.py:80
  166.4 33.8 %all_to_all.15 = f32[64,64,128]{2,0,1:T(8,128)S(1)} all-to-all(f32[64,64,128]{2,0,1:T(8,128)S(1)} %pad_maximum_fusion), channel_id=1, replica_groups=mesh['gx'=4,'gy'=8,'gz'=8] {'gy'}, dimensions={1} | all-to-all | bytes 4194304 | tf_op jit(solution)/shard_map/all_to_all | solution.py:47
  210.9 7.6 %collective-permute-done.27 = f32[16,1,1024]{2,1,0:T(1,128)S(1)} collective-permute-done((f32[16,1,1024]{2,1,0:T(1,128)S(1)}, f32[16,1,1024]{2,1,0:T(1,128)S(1)}, u32[]{:S(2)}, u32[]{:S(2)}) %collective-permute-start.27) | collective-permute-done | bytes 65568 | tf_op jit(solution)/shard_map/ppermute | solution.py:16
  220.9 4.3 %multiply_subtract_fusion = f32[16,9,1024]{2,1,0:T(8,128)S(1)} fusion(f32[16,9,1024]{2,1,0:T(8,128)S(1)} %pad_maximum_fusion.2, f32[16,9,1024]{2,1,0:T(8,128)S(1)} %pad_maximum_fusion.1, f32[16,1,1024]{2,1,0:T(1,128)S(1)} %collective-permute-done.29, f32[16,8,1024]{2,1,0:T(8,128)S(1)} %bitcast.46), kind=kLoop, calls=%fused_computation.32 | loop fusion | flops 1474560 | bytes 2359296 | tf_op jit(solution)/shard_map/sub | solution.py:90
  (114 shorter events, 56.8 us)
Async XLA Ops:
  2.0 40.7 %collective-permute-start.7 = (f32[16,1,128]{2,0,1:T(8,128)S(1)}, f32[16,1,128]{2,0,1:T(8,128)S(1)}, u32[]{:S(2)}, u32[]{:S(2)}) collective-permute-start(f32[16,1,128]{2,0,1:T(8,128)S(1)} %get-tuple-element.40), channel_id=1, source_target_pairs={{0,64},{64,128},{128,192},{1,65},{65,129},{129,193},{2,66},{66,130... | collective-permute-start | bytes 24584 | tf_op jit(solution)/shard_map/ppermute | solution.py:27
  9.7 10.4 %collective-permute-start.14 = (f32[16,64,1]{2,0,1:T(8,128)S(1)}, f32[16,64,1]{2,0,1:T(8,128)S(1)}, u32[]{:S(2)}, u32[]{:S(2)}) collective-permute-start(f32[16,64,1]{2,0,1:T(8,128)S(1)} %slice.400), channel_id=1, source_target_pairs={{0,8},{8,16},{16,24},{24,32},{32,40},{40,48},{48,56},{1,9},{9,17},... | collective-permute-start | bytes 12296 | tf_op jit(solution)/shard_map/ppermute | solution.py:16
  11.2 19.7 %collective-permute-start.6 = (f32[16,64,1]{2,0,1:T(8,128)S(1)}, f32[16,64,1]{2,0,1:T(8,128)S(1)}, u32[]{:S(2)}, u32[]{:S(2)}) collective-permute-start(f32[16,64,1]{2,0,1:T(8,128)S(1)} %get-tuple-element.36), channel_id=1, source_target_pairs={{0,8},{8,16},{16,24},{24,32},{32,40},{40,48},{48,56},{1,9},{9,17},... | collective-permute-start | bytes 12296 | tf_op jit(solution)/shard_map/ppermute | solution.py:27
  12.5 21.1 %collective-permute-start.9 = (f32[16,64,1]{2,0,1:T(8,128)S(1)}, f32[16,64,1]{2,0,1:T(8,128)S(1)}, u32[]{:S(2)}, u32[]{:S(2)}) collective-permute-start(f32[16,64,1]{2,0,1:T(8,128)S(1)} %get-tuple-element.37), channel_id=1, source_target_pairs={{8,0},{16,8},{24,16},{32,24},{40,32},{48,40},{56,48},{9,1},{17,9},... | collective-permute-start | bytes 12296 | tf_op jit(solution)/shard_map/ppermute | solution.py:28
  17.3 20.0 %collective-permute-start.1 = (f32[16,64,1]{2,0,1:T(8,128)S(1)}, f32[16,64,1]{2,0,1:T(8,128)S(1)}, u32[]{:S(2)}, u32[]{:S(2)}) collective-permute-start(f32[16,64,1]{2,0,1:T(8,128)S(1)} %get-tuple-element.38), channel_id=1, source_target_pairs={{0,8},{8,16},{16,24},{24,32},{32,40},{40,48},{48,56},{1,9},{9,17},... | collective-permute-start | bytes 12296 | tf_op jit(solution)/shard_map/ppermute | solution.py:27
  20.0 19.9 %collective-permute-start.4 = (f32[16,64,1]{2,0,1:T(8,128)S(1)}, f32[16,64,1]{2,0,1:T(8,128)S(1)}, u32[]{:S(2)}, u32[]{:S(2)}) collective-permute-start(f32[16,64,1]{2,0,1:T(8,128)S(1)} %get-tuple-element.39), channel_id=1, source_target_pairs={{8,0},{16,8},{24,16},{32,24},{40,32},{48,40},{56,48},{9,1},{17,9},... | collective-permute-start | bytes 12296 | tf_op jit(solution)/shard_map/ppermute | solution.py:28
  30.9 41.2 %collective-permute-start = (f32[1,64,128]{2,0,1:T(1,128)S(1)}, f32[1,64,128]{2,0,1:T(1,128)S(1)}, u32[]{:S(2)}, u32[]{:S(2)}) collective-permute-start(f32[1,64,128]{2,0,1:T(1,128)S(1)} %bitcast.53), channel_id=1, source_target_pairs={{0,1},{1,2},{2,3},{3,4},{4,5},{5,6},{6,7},{8,9},{9,10},{10,11},{11... | collective-permute-start | bytes 98312 | tf_op jit(solution)/shard_map/ppermute | solution.py:16
  33.6 45.3 %collective-permute-start.11 = (f32[1,64,128]{2,0,1:T(1,128)S(1)}, f32[1,64,128]{2,0,1:T(1,128)S(1)}, u32[]{:S(2)}, u32[]{:S(2)}) collective-permute-start(f32[1,64,128]{2,0,1:T(1,128)S(1)} %bitcast.57), channel_id=1, source_target_pairs={{0,1},{1,2},{2,3},{3,4},{4,5},{5,6},{6,7},{8,9},{9,10},{10,11},{11... | collective-permute-start | bytes 98312 | tf_op jit(solution)/shard_map/ppermute | solution.py:27
  37.3 41.6 %collective-permute-start.5 = (f32[1,64,128]{2,0,1:T(1,128)S(1)}, f32[1,64,128]{2,0,1:T(1,128)S(1)}, u32[]{:S(2)}, u32[]{:S(2)}) collective-permute-start(f32[1,64,128]{2,0,1:T(1,128)S(1)} %bitcast.56), channel_id=1, source_target_pairs={{1,0},{2,1},{3,2},{4,3},{5,4},{6,5},{7,6},{9,8},{10,9},{11,10},{12... | collective-permute-start | bytes 98312 | tf_op jit(solution)/shard_map/ppermute | solution.py:28
  39.9 39.0 %collective-permute-start.12 = (f32[1,64,128]{2,0,1:T(1,128)S(1)}, f32[1,64,128]{2,0,1:T(1,128)S(1)}, u32[]{:S(2)}, u32[]{:S(2)}) collective-permute-start(f32[1,64,128]{2,0,1:T(1,128)S(1)} %bitcast.55), channel_id=1, source_target_pairs={{0,1},{1,2},{2,3},{3,4},{4,5},{5,6},{6,7},{8,9},{9,10},{10,11},{11... | collective-permute-start | bytes 98312 | tf_op jit(solution)/shard_map/ppermute | solution.py:27
  68.6 10.3 %collective-permute-start.10 = (f32[1,64,128]{2,0,1:T(1,128)S(1)}, f32[1,64,128]{2,0,1:T(1,128)S(1)}, u32[]{:S(2)}, u32[]{:S(2)}) collective-permute-start(f32[1,64,128]{2,0,1:T(1,128)S(1)} %bitcast.54), channel_id=1, source_target_pairs={{1,0},{2,1},{3,2},{4,3},{5,4},{6,5},{7,6},{9,8},{10,9},{11,10},{12... | collective-permute-start | bytes 98312 | tf_op jit(solution)/shard_map/ppermute | solution.py:28
  97.9 31.0 %collective-permute-start.16 = (f32[16,1,128]{2,0,1:T(8,128)S(1)}, f32[16,1,128]{2,0,1:T(8,128)S(1)}, u32[]{:S(2)}, u32[]{:S(2)}) collective-permute-start(f32[16,1,128]{2,0,1:T(8,128)S(1)} %get-tuple-element.30), channel_id=1, source_target_pairs={{0,64},{64,128},{128,192},{1,65},{65,129},{129,193},{2,66},{66,130... | collective-permute-start | bytes 24584 | tf_op jit(solution)/shard_map/ppermute | solution.py:27
  102.2 16.6 %collective-permute-start.20 = (f32[16,64,1]{2,0,1:T(8,128)S(1)}, f32[16,64,1]{2,0,1:T(8,128)S(1)}, u32[]{:S(2)}, u32[]{:S(2)}) collective-permute-start(f32[16,64,1]{2,0,1:T(8,128)S(1)} %get-tuple-element.24), channel_id=1, source_target_pairs={{0,8},{8,16},{16,24},{24,32},{32,40},{40,48},{48,56},{1,9},{9,17},... | collective-permute-start | bytes 12296 | tf_op jit(solution)/shard_map/ppermute | solution.py:27
  103.5 17.2 %collective-permute-start.23 = (f32[16,64,1]{2,0,1:T(8,128)S(1)}, f32[16,64,1]{2,0,1:T(8,128)S(1)}, u32[]{:S(2)}, u32[]{:S(2)}) collective-permute-start(f32[16,64,1]{2,0,1:T(8,128)S(1)} %get-tuple-element.25), channel_id=1, source_target_pairs={{8,0},{16,8},{24,16},{32,24},{40,32},{48,40},{56,48},{9,1},{17,9},... | collective-permute-start | bytes 12296 | tf_op jit(solution)/shard_map/ppermute | solution.py:28
  113.1 9.5 %collective-permute-start.15 = (f32[16,64,1]{2,0,1:T(8,128)S(1)}, f32[16,64,1]{2,0,1:T(8,128)S(1)}, u32[]{:S(2)}, u32[]{:S(2)}) collective-permute-start(f32[16,64,1]{2,0,1:T(8,128)S(1)} %get-tuple-element.26), channel_id=1, source_target_pairs={{0,8},{8,16},{16,24},{24,32},{32,40},{40,48},{48,56},{1,9},{9,17},... | collective-permute-start | bytes 12296 | tf_op jit(solution)/shard_map/ppermute | solution.py:27
  114.4 12.5 %collective-permute-start.18 = (f32[16,64,1]{2,0,1:T(8,128)S(1)}, f32[16,64,1]{2,0,1:T(8,128)S(1)}, u32[]{:S(2)}, u32[]{:S(2)}) collective-permute-start(f32[16,64,1]{2,0,1:T(8,128)S(1)} %get-tuple-element.27), channel_id=1, source_target_pairs={{8,0},{16,8},{24,16},{32,24},{40,32},{48,40},{56,48},{9,1},{17,9},... | collective-permute-start | bytes 12296 | tf_op jit(solution)/shard_map/ppermute | solution.py:28
  118.8 14.4 %collective-permute-start.17 = (f32[16,1,128]{2,0,1:T(8,128)S(1)}, f32[16,1,128]{2,0,1:T(8,128)S(1)}, u32[]{:S(2)}, u32[]{:S(2)}) collective-permute-start(f32[16,1,128]{2,0,1:T(8,128)S(1)} %get-tuple-element.31), channel_id=1, source_target_pairs={{64,0},{128,64},{192,128},{65,1},{129,65},{193,129},{66,2},{130,66... | collective-permute-start | bytes 24584 | tf_op jit(solution)/shard_map/ppermute | solution.py:28
  120.7 25.4 %collective-permute-start.26 = (f32[1,64,128]{2,0,1:T(1,128)S(1)}, f32[1,64,128]{2,0,1:T(1,128)S(1)}, u32[]{:S(2)}, u32[]{:S(2)}) collective-permute-start(f32[1,64,128]{2,0,1:T(1,128)S(1)} %get-tuple-element.20), channel_id=1, source_target_pairs={{0,1},{1,2},{2,3},{3,4},{4,5},{5,6},{6,7},{8,9},{9,10},{10,11},{11... | collective-permute-start | bytes 98312 | tf_op jit(solution)/shard_map/ppermute | solution.py:27
  122.7 23.5 %collective-permute-start.24 = (f32[1,64,128]{2,0,1:T(1,128)S(1)}, f32[1,64,128]{2,0,1:T(1,128)S(1)}, u32[]{:S(2)}, u32[]{:S(2)}) collective-permute-start(f32[1,64,128]{2,0,1:T(1,128)S(1)} %get-tuple-element.21), channel_id=1, source_target_pairs={{1,0},{2,1},{3,2},{4,3},{5,4},{6,5},{7,6},{9,8},{10,9},{11,10},{12... | collective-permute-start | bytes 98312 | tf_op jit(solution)/shard_map/ppermute | solution.py:28
  126.9 19.2 %collective-permute-start.25 = (f32[1,64,128]{2,0,1:T(1,128)S(1)}, f32[1,64,128]{2,0,1:T(1,128)S(1)}, u32[]{:S(2)}, u32[]{:S(2)}) collective-permute-start(f32[1,64,128]{2,0,1:T(1,128)S(1)} %get-tuple-element.22), channel_id=1, source_target_pairs={{0,1},{1,2},{2,3},{3,4},{4,5},{5,6},{6,7},{8,9},{9,10},{10,11},{11... | collective-permute-start | bytes 98312 | tf_op jit(solution)/shard_map/ppermute | solution.py:27
  129.0 17.2 %collective-permute-start.19 = (f32[1,64,128]{2,0,1:T(1,128)S(1)}, f32[1,64,128]{2,0,1:T(1,128)S(1)}, u32[]{:S(2)}, u32[]{:S(2)}) collective-permute-start(f32[1,64,128]{2,0,1:T(1,128)S(1)} %get-tuple-element.23), channel_id=1, source_target_pairs={{1,0},{2,1},{3,2},{4,3},{5,4},{6,5},{7,6},{9,8},{10,9},{11,10},{12... | collective-permute-start | bytes 98312 | tf_op jit(solution)/shard_map/ppermute | solution.py:28
  200.7 10.1 %collective-permute-start.28 = (f32[16,1,1024]{2,1,0:T(1,128)S(1)}, f32[16,1,1024]{2,1,0:T(1,128)S(1)}, u32[]{:S(2)}, u32[]{:S(2)}) collective-permute-start(f32[16,1,1024]{2,1,0:T(1,128)S(1)} %slice.418), channel_id=1, source_target_pairs={{8,0},{16,8},{24,16},{32,24},{40,32},{48,40},{56,48},{64,56},{72,6... | collective-permute-start | bytes 196616 | tf_op jit(solution)/shard_map/ppermute | solution.py:16
  205.9 14.9 %collective-permute-start.29 = (f32[16,1,1024]{2,1,0:T(1,128)S(1)}, f32[16,1,1024]{2,1,0:T(1,128)S(1)}, u32[]{:S(2)}, u32[]{:S(2)}) collective-permute-start(f32[16,1,1024]{2,1,0:T(1,128)S(1)} %slice.420), channel_id=1, source_target_pairs={{8,0},{16,8},{24,16},{32,24},{40,32},{48,40},{56,48},{64,56},{72,6... | collective-permute-start | bytes 196616 | tf_op jit(solution)/shard_map/ppermute | solution.py:16
  208.1 10.5 %collective-permute-start.27 = (f32[16,1,1024]{2,1,0:T(1,128)S(1)}, f32[16,1,1024]{2,1,0:T(1,128)S(1)}, u32[]{:S(2)}, u32[]{:S(2)}) collective-permute-start(f32[16,1,1024]{2,1,0:T(1,128)S(1)} %slice.417), channel_id=1, source_target_pairs={{8,0},{16,8},{24,16},{32,24},{40,32},{48,40},{56,48},{64,56},{72,6... | collective-permute-start | bytes 196616 | tf_op jit(solution)/shard_map/ppermute | solution.py:16
  (12 other events, 74.8 us)
where the time goes:
time: 231 us; the launch traced here: 229 us
  starting transfers between devices  94.5 us (41%)
  other arithmetic  66.9 us (29%)
  blocking collectives  33.8 us (15%)
  waiting for transfers between devices  21 us (9%)
  local copies, waits for them, and re-layouts  11.3 us (5%)
    ppermute x12, starting transfers between devices, with_halo(): lax.ppermute(initial, axis, [(b, a) for a, b in up])  44.8 us
    ppermute x12, starting transfers between devices, with_halo(): lax.ppermute(last, axis, up)  34.5 us
    all_to_all x1, blocking collectives, in_one_piece(): lax.all_to_all(both, axis, split_axis=split_dim, concat_axis=concat_dim,...  33.8 us
    cos x3, other arithmetic, shards(): cosines = [jnp.cos(phase) for phase in link_halo]  19.7 us
    add x2, other arithmetic, advance(): centre_real + time_step * ((epsilon - density) * centre_real + lap_real)  19.2 us
    add x2, other arithmetic, advance(): centre_imag + time_step * ((epsilon - density) * centre_imag + lap_imag)  19.2 us
    ppermute x6, starting transfers between devices, passed_along(): return lax.ppermute(block, axis, route)  15.3 us
    ppermute x12, waiting for transfers between devices, with_halo(): lax.ppermute(initial, axis, [(b, a) for a, b in up])  9.16 us
  transfers between devices with their start and end apart: 30, of which 7 were waited for; matrix products, arithmetic and copies ran while one was open for 13% of the time, Pallas kernels for 0%

commit v1 on v0

v1 whole, which is shorter than its diff:
```python
import functools

import jax
import jax.numpy as jnp
from jax import lax
from jax.experimental import pallas as pl
from jax.experimental.pallas import tpu as pltpu
from jax.sharding import PartitionSpec as P

LEVELS = 8
time_step = 0.15

F32 = jnp.float32
LANES = 128
TILE = 8
NZ, NX, NY = 16, 64, 128
RX = NX + TILE
PR, PI, PX, PY, PZ, EP = range(6)

SIN = (1.0, -0.16666658222675323, 0.008333050645887852, -0.00019809069635812193, 2.6052216526295524e-06)
COS = (-0.5, 0.0416666604578495, -0.0013888651737943292, 2.4774621124379337e-05, -2.6298400257473986e-07)


def sincos(phase):
    half = phase * 0.5
    u = half * half
    s = SIN[4]
    for k in (3, 2, 1, 0):
        s = s * u + SIN[k]
    s = s * half
    c = COS[4]
    for k in (3, 2, 1, 0):
        c = c * u + COS[k]
    c = c * u + 1.0
    return (c - s) * (c + s), (s + s) * c


def iota(shape, dim):
    return lax.broadcasted_iota(jnp.int32, shape, dim)


def roll(v, shift, axis):
    return pltpu.roll(v, shift % v.shape[axis], axis)


def ahead_x(v):
    return pltpu.roll(v, RX - 1, 0)


def behind_x(v):
    return pltpu.roll(v, 1, 0)


def turned(c, s, r, i):
    return c * r - s * i, c * i + s * r


def turned_back(c, s, r, i):
    return c * r + s * i, c * i - s * r


def choose(index, cases):
    out = cases[-1][1]
    for test, value in cases[-2::-1]:
        out = jnp.where(test(index), value, out)
    return out


def place_low(index, r, i, c, s, others, own):
    wr, wi = turned_back(c, s, r, i)
    first = index == own
    return jnp.where(first, wr, r), jnp.where(first, wi, i)


def row_up(a, row):
    pr, pi, px, py, pz, ep = a
    c, s = sincos(px)
    wr, wi = turned_back(c, s, pr, pi)
    last = row == 6
    pr = jnp.where(last, wr, pr)
    pi = jnp.where(last, wi, pi)
    out = roll(pr, 2, 0)
    out = jnp.where(row >= 2, roll(pi, 4, 0), out)
    out = jnp.where(row == 4, roll(px, 5, 0), out)
    out = jnp.where(row == 5, roll(py, 6, 0), out)
    out = jnp.where(row == 6, roll(pz, 7, 0), out)
    return jnp.where(row == 7, ep, out)


def row_down(a, row):
    pr, pi, px, py, pz, ep = a
    first = jnp.where(row < 3, pr, jnp.where(row < 6, roll(pi, 3, 0), roll(px, 6, 0)))
    second = jnp.where(row < 2, py, jnp.where(row < 4, roll(pz, 2, 0), roll(ep, 4, 0)))
    return first, second


def pack_x(levels, pr, pi, px, py, pz, mat, ep, up, down):
    row = iota((TILE, LANES), 0)

    def body(z, carry):
        m = mat[z]
        e = jnp.full((NX, NY), levels[LEVELS - 1], F32)
        for k in range(LEVELS - 1):
            e = jnp.where(m == k, levels[k], e)
        ep[z] = e
        top = [q[z, NX - TILE:, :] for q in (pr, pi, px, py, pz)] + [e[NX - TILE:, :]]
        low = [q[z, :TILE, :] for q in (pr, pi, px, py, pz)] + [e[:TILE, :]]
        up[z] = row_up(top, row)
        first, second = row_down(low, row)
        down[z, :TILE, :] = first
        down[z, TILE:, :] = second
        return carry

    lax.fori_loop(0, NZ, body, 0)


def pack_y(pr, pi, px, py, pz, ep, lo, hi, halo, own, up, down):
    row = iota((TILE, LANES), 0)
    gx = lax.axis_index("gx")
    keep = jnp.where(row < 4, jnp.where(gx < lax.axis_size("gx") - 1, 1, 0), jnp.where(gx > 0, 1, 0)) > 0
    low_rows = row >= 6

    def unpack(z, carry):
        l = lo[z]
        a = hi[z, :TILE, :]
        b = hi[z, TILE:, :]
        zero = jnp.zeros_like(l)
        last = row == 7
        halo[PR, z] = jnp.where(keep, jnp.where(low_rows, roll(l, 6, 0), a), zero)
        halo[PI, z] = jnp.where(keep, jnp.where(low_rows, roll(l, 4, 0), roll(a, -3, 0)), zero)
        halo[PX, z] = jnp.where(last, roll(l, 3, 0), jnp.where(row < 2, roll(a, -6, 0), zero))
        halo[PY, z] = jnp.where(last, roll(l, 2, 0), jnp.where(row < 2, b, zero))
        halo[PZ, z] = jnp.where(last, roll(l, 1, 0), jnp.where(row < 2, roll(b, -2, 0), zero))
        halo[EP, z] = jnp.where(last, l, jnp.where(row < 2, roll(b, -4, 0), zero))
        return carry

    lax.fori_loop(0, NZ, unpack, 0)
    lane = iota((RX, LANES), 1)
    slot = lane % 8
    group = lane // 8
    columns = []
    for k, q in enumerate((pr, pi, px, py, pz, ep)):
        acc = jnp.zeros((RX, LANES), F32)
        for z in range(NZ):
            v = jnp.concatenate([q[z], halo[k, z]], axis=0)
            acc = jnp.where(group == z, roll(v, 8 * z - 126, 1), acc)
        own[k] = acc
        columns.append(acc)
    vr, vi, vx, vy, vz, ve = columns
    c, s = sincos(vy)
    wr, wi = turned_back(c, s, vr, vi)
    ur = jnp.where(slot == 0, wr, vr)
    ui = jnp.where(slot == 0, wi, vi)
    out = jnp.where(slot < 2, ur, roll(ui, 2, 1))
    out = jnp.where(slot == 4, roll(vx, 3, 1), out)
    out = jnp.where(slot == 5, roll(vy, 4, 1), out)
    out = jnp.where(slot == 6, roll(vz, 5, 1), out)
    out = jnp.where(slot == 7, roll(ve, 6, 1), out)
    up[...] = out
    down[0] = jnp.where(slot < 3, roll(vr, -2, 1), jnp.where(slot < 6, roll(vi, 1, 1), roll(vx, 4, 1)))
    down[1] = jnp.where(slot < 2, roll(vy, -2, 1), jnp.where(slot < 4, vz, roll(ve, 2, 1)))


def pack_z(pr, pi, px, py, pz, ep, halo, own, lo, hi, strip, up, down):
    lane = iota((RX, LANES), 1)
    slot = lane % 8
    group = lane // 8
    gy = lax.axis_index("gy")
    keep = jnp.where((slot >= 2) & (slot < 5), jnp.where(gy < lax.axis_size("gy") - 1, 1, 0),
                     jnp.where((slot >= 5) & (slot < 7), jnp.where(gy > 0, 1, 0), 1)) > 0
    l = lo[...]
    a = hi[0]
    b = hi[1]
    zero = jnp.zeros_like(l)

    def join(k, from_hi, from_lo):
        v = own[k]
        out = jnp.where(slot < 2, v, roll(v, 5, 1))
        out = jnp.where((slot >= 2) & (slot < 5), from_hi, out)
        return jnp.where((slot == 5) | (slot == 6), from_lo, out)

    one = slot == 6
    strip[PR] = jnp.where(keep, join(PR, roll(a, 2, 1), roll(l, 5, 1)), zero)
    strip[PI] = jnp.where(keep, join(PI, roll(a, -1, 1), roll(l, 3, 1)), zero)
    strip[PX] = join(PX, roll(a, -4, 1), jnp.where(one, roll(l, 2, 1), zero))
    strip[PY] = join(PY, roll(b, 2, 1), jnp.where(one, roll(l, 1, 1), zero))
    strip[PZ] = join(PZ, b, jnp.where(one, l, zero))
    strip[EP] = join(EP, roll(b, -2, 1), jnp.where(one, roll(l, -1, 1), zero))

    def layer(k, z):
        q = (pr, pi, px, py, pz, ep)[k]
        return jnp.concatenate([q[z], halo[k, z]], axis=0)

    c, s = sincos(layer(PZ, 14))
    up[0], up[1] = turned_back(c, s, layer(PR, 14), layer(PI, 14))
    for k in range(6):
        up[2 + k] = layer(k, 15)
    down[0] = layer(PR, 1)
    down[1] = layer(PI, 1)
    for k in range(6):
        down[2 + k] = layer(k, 0)
    c, s = sincos(strip[PZ])
    wr, wi = turned_back(c, s, strip[PR], strip[PI])
    out = jnp.where(group == 0, roll(wr, -8 * 14, 1), roll(wi, -8 * 13, 1))
    for k in range(6):
        out = jnp.where(group == 2 + k, roll(strip[k], 8 * (2 + k - 15), 1), out)
    up[8] = out
    out = jnp.where(group == 0, roll(strip[PR], -8, 1), strip[PI])
    for k in range(6):
        out = jnp.where(group == 2 + k, roll(strip[k], 8 * (2 + k), 1), out)
    down[8] = out


def advance_layer(centre, above, below_turned, trig, edge, epsilon, lane):
    r, i = centre
    cz, sz, cx, sx, cy, sy = trig
    lap_r = -6.0 * r + below_turned[0]
    lap_i = -6.0 * i + below_turned[1]
    t = turned(cz, sz, *above)
    lap_r, lap_i = lap_r + t[0], lap_i + t[1]
    t = turned(cx, sx, ahead_x(r), ahead_x(i))
    lap_r, lap_i = lap_r + t[0], lap_i + t[1]
    t = turned_back(cx, sx, r, i)
    lap_r, lap_i = lap_r + behind_x(t[0]), lap_i + behind_x(t[1])
    w = turned_back(cy, sy, r, i)
    fr, fi = r, i
    wr, wi = w
    if edge is not None:
        fr, fi = jnp.where(lane == 0, edge[0], r), jnp.where(lane == 0, edge[1], i)
        wr, wi = jnp.where(lane == 127, edge[0], wr), jnp.where(lane == 127, edge[1], wi)
    t = turned(cy, sy, roll(fr, -1, 1), roll(fi, -1, 1))
    lap_r, lap_i = lap_r + t[0], lap_i + t[1]
    lap_r, lap_i = lap_r + roll(wr, 1, 1), lap_i + roll(wi, 1, 1)
    gain = epsilon - (r * r + i * i)
    return r + time_step * (gain * r + lap_r), i + time_step * (gain * i + lap_i)


def compute(pr, pi, px, py, pz, ep, halo, strip, zlo, zhi, final_r, final_i, out,
            ar, ai, br, bi, trig, eps, nr, ni, mr, mi, ntrig, neps, er, ei, jx_edge):
    lane = iota((RX, LANES), 1)
    row = iota((RX, LANES), 0)
    slot = lane % 8
    group = lane // 8
    gx, gy, gz = (lax.axis_index(a) for a in ("gx", "gy", "gz"))

    def on(test):
        return jnp.where(test, 1, 0)

    x_hi, x_lo = on(gx < lax.axis_size("gx") - 1), on(gx > 0)
    y_hi, y_lo = on(gy < lax.axis_size("gy") - 1), on(gy > 0)
    z_hi, z_lo = on(gz < lax.axis_size("gz") - 1), on(gz > 0)
    keep_x = jnp.where(row < NX, 1, jnp.where(row < NX + 4, x_hi, x_lo))
    keep_xy = keep_x * jnp.where((slot >= 2) & (slot < 5), y_hi, jnp.where((slot >= 5) & (slot < 7), y_lo, 1))
    keep_z = jnp.where(group < 8, z_hi, z_lo)
    zero = jnp.zeros((RX, LANES), F32)

    def fill(z, carry):
        def layer(q, k):
            return jnp.concatenate([q[z], halo[k, z]], axis=0)

        ar[z + 2] = layer(pr, PR)
        ai[z + 2] = layer(pi, PI)
        for n, (q, k) in enumerate(((pz, PZ), (px, PX), (py, PY))):
            trig[2 * n, z + 2], trig[2 * n + 1, z + 2] = sincos(layer(q, k))
        eps[z + 2] = layer(ep, EP)
        return carry

    lax.fori_loop(0, NZ, fill, 0)
    for src, keep, outer, inner in ((zlo, z_lo, 0, 1), (zhi, z_hi, 19, 18)):
        ok = jnp.broadcast_to(keep, (RX, LANES)) > 0
        ar[outer] = jnp.where(ok, src[0], zero)
        ai[outer] = jnp.where(ok, src[1], zero)
        ar[inner] = jnp.where(ok, src[2], zero)
        ai[inner] = jnp.where(ok, src[3], zero)
        for n, k in enumerate((PZ, PX, PY)):
            trig[2 * n, inner], trig[2 * n + 1, inner] = sincos(src[2 + k])
        eps[inner] = src[2 + EP]
    trig[0, 0] = zero + 1.0
    trig[1, 0] = zero
    lo8 = zlo[8]
    hi8 = zhi[8]

    def beyond(k, outer):
        v = jnp.where(group == 0, roll(hi8, -8 * (2 + k), 1), roll(lo8, 8 * (15 - 2 - k), 1))
        if outer is not None:
            v = jnp.where(group == 1, roll(hi8, 8 * (1 - outer), 1), v)
            v = jnp.where(group == 14, roll(lo8, 8 * (14 - outer), 1), v)
        return v

    nr[0] = strip[PR]
    ni[0] = strip[PI]
    nr[1] = jnp.where(keep_z > 0, beyond(PR, 0), zero)
    ni[1] = jnp.where(keep_z > 0, beyond(PI, 1), zero)
    for n, k in enumerate((PZ, PX, PY)):
        ntrig[2 * n, 0], ntrig[2 * n + 1, 0] = sincos(strip[k])
        v = beyond(k, None)
        if k == PZ:
            v = jnp.where(group == 14, zero, v)
        ntrig[2 * n, 1], ntrig[2 * n + 1, 1] = sincos(v)
    neps[0] = strip[EP]
    neps[1] = beyond(EP, None)

    def edges(sr, si):
        for h in range(2):
            w = turned_back(ntrig[4, h], ntrig[5, h], sr[h], si[h])
            er[h] = jnp.where(slot == 1, roll(w[0], -5, 1), sr[h])
            ei[h] = jnp.where(slot == 1, roll(w[1], -5, 1), si[h])

    def step_strips(sr, si, halves):
        w = [turned_back(ntrig[0, h], ntrig[1, h], sr[h], si[h]) for h in range(2)]
        wr = [roll(v[0], 8, 1) for v in w]
        wi = [roll(v[1], 8, 1) for v in w]
        fr = [roll(sr[h], -8, 1) for h in range(2)]
        fi = [roll(si[h], -8, 1) for h in range(2)]
        results = []
        for h in halves:
            g = 1 - h
            below = (jnp.where(group == 0, wr[g], wr[h]), jnp.where(group == 0, wi[g], wi[h]))
            above = (jnp.where(group == 15, fr[g], fr[h]), jnp.where(group == 15, fi[g], fi[h]))
            v = advance_layer((sr[h], si[h]), above, below, [ntrig[k, h] for k in range(6)], None, neps[h], lane)
            keep = keep_xy if h == 0 else keep_xy * keep_z
            results.append([jnp.where(keep > 0, u, zero) for u in v])
        return results

    def step_layer(sr, si, k):
        inside = (k >= 2) & (k < 18)
        half = jnp.where(inside, 0, 1)
        shift = (126 - 8 * ((k + 14) % 16)) % 128
        edge = (pltpu.roll(er[half], shift, 1), pltpu.roll(ei[half], shift, 1))
        below = turned_back(trig[0, k - 1], trig[1, k - 1], sr[k - 1], si[k - 1])
        v = advance_layer((sr[k], si[k]), (sr[k + 1], si[k + 1]), below, [trig[n, k] for n in range(6)],
                          edge, eps[k], lane)
        return v, inside

    edges(nr, ni)

    def first(k, carry):
        v, inside = step_layer(ar, ai, k)
        ok = keep_x * jnp.where(inside, 1, jnp.where(k < 2, z_lo, z_hi)) > 0
        br[k] = jnp.where(ok, v[0], zero)
        bi[k] = jnp.where(ok, v[1], zero)
        return carry

    lax.fori_loop(1, 19, first, 0)
    for h, v in enumerate(step_strips(nr, ni, (0, 1))):
        mr[h], mi[h] = v
    edges(mr, mi)

    def second(k, carry):
        v, _ = step_layer(br, bi, k)
        ok = keep_x > 0
        ar[k] = jnp.where(ok, v[0], zero)
        ai[k] = jnp.where(ok, v[1], zero)
        final_r[k - 2] = v[0][:NX]
        final_i[k - 2] = v[1][:NX]
        return carry

    lax.fori_loop(2, 18, second, 0)
    (sr, si), = step_strips(mr, mi, (0,))
    nr[0] = sr
    ni[0] = si
    t = turned(ntrig[2, 0], ntrig[3, 0], ahead_x(sr), ahead_x(si))
    jx_edge[...] = sr * t[1] - si * t[0]
    triangle = jnp.where(iota((LANES, LANES), 0) <= iota((LANES, LANES), 1), 1.0, 0.0).astype(F32)

    def analyse(z, carry):
        r, i = ar[z + 2], ai[z + 2]
        shift = (126 - 8 * z) % 128
        t = turned(trig[2, z + 2], trig[3, z + 2], ahead_x(r), ahead_x(i))
        jx = r * t[1] - i * t[0]
        fr = jnp.where(lane == 0, pltpu.roll(nr[0], shift, 1), r)
        fi = jnp.where(lane == 0, pltpu.roll(ni[0], shift, 1), i)
        t = turned(trig[4, z + 2], trig[5, z + 2], roll(fr, -1, 1), roll(fi, -1, 1))
        jy = r * t[1] - i * t[0]
        jx_next = roll(jnp.where(lane == 0, pltpu.roll(jx_edge[...], shift, 1), jx), -1, 1)
        circulation = (jx + ahead_x(jy) - jx_next - jy)[:NX]
        sums = jnp.dot(jx[:NX], triangle, precision=lax.Precision.HIGHEST, preferred_element_type=F32)
        for j in range(NX // TILE):
            out[j, z] = circulation[j * TILE:(j + 1) * TILE]
            out[j, NZ + z] = sums[j * TILE:(j + 1) * TILE]
        return carry

    lax.fori_loop(0, NZ, analyse, 0)


def finish(got, circulation, flux):
    def body(z, carry):
        before = jnp.zeros((TILE, 1), F32)
        for j in range(got.shape[0]):
            circulation[z, :, j * LANES:(j + 1) * LANES] = got[j, z]
            v = got[j, NZ + z]
            flux[z, :, j * LANES:(j + 1) * LANES] = v + before
            before = before + v[:, LANES - 1:]
        return carry

    lax.fori_loop(0, NZ, body, 0)


def spec(*shape):
    return jax.ShapeDtypeStruct(shape, F32)


def call(body, outs, *args, scratch=(), smem=0):
    memory = [pl.BlockSpec(memory_space=pltpu.SMEM if k < smem else pltpu.VMEM) for k in range(len(args))]
    return pl.pallas_call(
        body, out_shape=outs, in_specs=memory, scratch_shapes=list(scratch),
        out_specs=jax.tree.map(lambda _: pl.BlockSpec(memory_space=pltpu.VMEM), outs), name=body.__name__,
        compiler_params=pltpu.CompilerParams(vmem_limit_bytes=48 * 2**20),
    )(*args)


def exchange(up, down, axis):
    size = lax.axis_size(axis)
    forward = [(k, (k + 1) % size) for k in range(size)]
    return lax.ppermute(up, axis, forward), lax.ppermute(down, axis, [(b, a) for a, b in forward])


def shards(pr, pi, pz, px, py, material, levels):
    layers = lambda n: pltpu.VMEM((n, RX, LANES), F32)
    ep, up, down = call(pack_x, (spec(NZ, NX, NY), spec(NZ, TILE, LANES), spec(NZ, 2 * TILE, LANES)),
                        levels, pr, pi, px, py, pz, material, smem=1)
    lo, hi = exchange(up, down, "gx")
    fields = (pr, pi, px, py, pz, ep)
    halo, own, up, down = call(
        pack_y, (spec(6, NZ, TILE, LANES), spec(6, RX, LANES), spec(RX, LANES), spec(2, RX, LANES)), *fields, lo, hi)
    lo, hi = exchange(up, down, "gy")
    strip, up, down = call(pack_z, (spec(6, RX, LANES), spec(9, RX, LANES), spec(9, RX, LANES)),
                           *fields, halo, own, lo, hi)
    lo, hi = exchange(up, down, "gz")
    parts = lax.axis_size("gy")
    final_r, final_i, out = call(
        compute, (spec(NZ, NX, NY), spec(NZ, NX, NY), spec(parts, 2 * NZ, TILE, LANES)),
        *fields, halo, strip, lo, hi,
        scratch=[layers(20)] * 4 + [pltpu.VMEM((6, 20, RX, LANES), F32), layers(20)] + [layers(2)] * 4
        + [pltpu.VMEM((6, 2, RX, LANES), F32), layers(2), layers(2), layers(2), pltpu.VMEM((RX, LANES), F32)])
    got = lax.all_to_all(out, "gy", 0, 0, tiled=True)
    circulation, flux = call(finish, (spec(NZ, TILE, parts * LANES), spec(NZ, TILE, parts * LANES)), got)
    return final_r, final_i, circulation, flux


def solution(mesh):
    block = P("gz", "gx", "gy")
    slab = P("gz", ("gx", "gy"), None)
    return jax.shard_map(shards, mesh=mesh, in_specs=(block,) * 6 + (P(),),
                         out_specs=(block, block, slab, slab), check_vma=False)
```

time: 231 us -> 81.4 us (0.35)
  the two profiles are of different devices: /device:TPU:79 before, /device:TPU:1 now
where the time goes in v1:
time: 81.4 us; the launch traced here: 81 us
  blocking collectives  22.7 us (28%)
  waiting for transfers between devices  18.7 us (23%)
  Pallas kernels  18.3 us (22%)
  starting transfers between devices  13.6 us (17%)
  local copies, waits for them, and re-layouts  6.91 us (8%)
    all_to_all x1, blocking collectives, shards(): got = lax.all_to_all(out, 'gy', 0, 0, tiled=True)  22.7 us
    pallas_call x5, Pallas kernels, call(): pl.pallas_call(body, out_shape=outs, in_specs=memory, scratch_shapes=list...  18.3 us
    ppermute x3, waiting for transfers between devices, exchange(): lax.ppermute(up, axis, forward)  12.3 us
    ppermute x3, starting transfers between devices, exchange(): lax.ppermute(down, axis, [(b, a) for a, b in forward])  11 us
    unnamed x24, local copies, waits for them, and re-layouts  6.91 us
    ppermute x3, waiting for transfers between devices, exchange(): lax.ppermute(down, axis, [(b, a) for a, b in forward])  6.4 us
    ppermute x3, starting transfers between devices, exchange(): lax.ppermute(up, axis, forward)  2.6 us
  transfers between devices with their start and end apart: 6, of which 5 were waited for; matrix products, arithmetic and copies ran while one was open for 0% of the time, Pallas kernels for 0%

profile of v1, /device:TPU:1, one launch (start us, length us, event | category | flops | bytes accessed | tf_op | source)
XLA Modules:
  0.0 81.0 jit_solution(14416384956727037742)
XLA Ops:
  0.6 1.0 %copy-done = f32[16,64,128]{2,1,0:T(8,128)S(1)} copy-done((f32[16,64,128]{2,1,0:T(8,128)S(1)}, f32[16,64,128]{2,1,0:T(8,128)}, u32[]{:S(2)}) %copy-start) | copy-done | bytes 524312
  1.7 1.0 %copy-done.2 = f32[16,64,128]{2,1,0:T(8,128)S(1)} copy-done((f32[16,64,128]{2,1,0:T(8,128)S(1)}, f32[16,64,128]{2,1,0:T(8,128)}, u32[]{:S(2)}) %copy-start.2) | copy-done | bytes 524312
  2.7 1.0 %copy-done.4 = f32[16,64,128]{2,1,0:T(8,128)S(1)} copy-done((f32[16,64,128]{2,1,0:T(8,128)S(1)}, f32[16,64,128]{2,1,0:T(8,128)}, u32[]{:S(2)}) %copy-start.4) | copy-done | bytes 524312
  3.8 1.0 %copy-done.6 = f32[16,64,128]{2,1,0:T(8,128)S(1)} copy-done((f32[16,64,128]{2,1,0:T(8,128)S(1)}, f32[16,64,128]{2,1,0:T(8,128)}, u32[]{:S(2)}) %copy-start.6) | copy-done | bytes 524312
  4.8 1.0 %copy-done.8 = f32[16,64,128]{2,1,0:T(8,128)S(1)} copy-done((f32[16,64,128]{2,1,0:T(8,128)S(1)}, f32[16,64,128]{2,1,0:T(8,128)}, u32[]{:S(2)}) %copy-start.8) | copy-done | bytes 524312
  5.8 1.0 %copy-done.10 = s32[16,64,128]{2,1,0:T(8,128)S(1)} copy-done((s32[16,64,128]{2,1,0:T(8,128)S(1)}, s32[16,64,128]{2,1,0:T(8,128)}, u32[]{:S(2)}) %copy-start.10) | copy-done | bytes 524312
  6.9 0.7 copy-done.11
  7.6 1.1 %pack_x.1 = (f32[16,64,128]{2,1,0:T(8,128)S(1)}, f32[16,8,128]{2,1,0:T(8,128)S(1)}, f32[16,16,128]{2,1,0:T(8,128)S(1)}) custom-call(f32[8]{0:T(128)S(1)} %copy-done.11, f32[16,64,128]{2,1,0:T(8,128)S(1)} %copy-done, f32[16,64,128]{2,1,0:T(8,128)S(1)} %copy-done.2, f32[16,64,128]{2,1,0:T(8,128)S(1)} %copy-done.4, f32[16,64,128]{2,1,0:T(8,128)S(1)} %copy-done.6, ...), custom_call_target="tpu_custom_call" | custom-call | tf_op jit(solution)/shard_map/pack_x/pallas_call | solution.py:405
  8.7 6.9 %collective-permute-start.1 = (f32[16,16,128]{2,1,0:T(8,128)S(1)}, f32[16,16,128]{2,1,0:T(8,128)S(1)}, u32[]{:S(2)}, u32[]{:S(2)}) collective-permute-start(f32[16,16,128]{2,1,0:T(8,128)S(1)} %get-tuple-element.21), channel_id=1, source_target_pairs={{64,0},{128,64},{192,128},{0,192},{65,1},{129,65},{193,129},{1,193... | collective-permute-start | bytes 393224 | tf_op jit(solution)/shard_map/ppermute | solution.py:415
  15.6 0.0 collective-permute-start
  15.6 5.9 %collective-permute-done.lo = f32[16,8,128]{2,1,0:T(8,128)S(1)} collective-permute-done((f32[16,8,128]{2,1,0:T(8,128)S(1)}, f32[16,8,128]{2,1,0:T(8,128)S(1)}, u32[]{:S(2)}, u32[]{:S(2)}) %collective-permute-start) | collective-permute-done | bytes 65568 | tf_op jit(solution)/shard_map/ppermute | solution.py:415
  21.6 1.2 %pack_y.1 = (f32[6,16,8,128]{3,2,1,0:T(8,128)S(1)}, f32[6,72,128]{2,1,0:T(8,128)S(1)}, f32[72,128]{1,0:T(8,128)S(1)}, f32[2,72,128]{2,1,0:T(8,128)S(1)}) custom-call(f32[16,64,128]{2,1,0:T(8,128)S(1)} %copy-done.1, f32[16,64,128]{2,1,0:T(8,128)S(1)} %copy-done.3, f32[16,64,128]{2,1,0:T(8,128)S(1)} %copy-done.5, f32[16,64,128]{2,1,0:T(8,128)S(1)} %copy-done.7, ...), custom_call_target="tpu_custom_call" | custom-call | tf_op jit(solution)/shard_map/pack_y/pallas_call | solution.py:405
  22.8 1.6 %collective-permute-start.3 = (f32[2,72,128]{2,1,0:T(8,128)S(1)}, f32[2,72,128]{2,1,0:T(8,128)S(1)}, u32[]{:S(2)}, u32[]{:S(2)}) collective-permute-start(f32[2,72,128]{2,1,0:T(8,128)S(1)} %get-tuple-element.25), channel_id=1, source_target_pairs={{8,0},{16,8},{24,16},{32,24},{40,32},{48,40},{56,48},{0,56},{9,1},... | collective-permute-start | bytes 221192 | tf_op jit(solution)/shard_map/ppermute | solution.py:415
  24.4 1.1 %collective-permute-start.2 = (f32[72,128]{1,0:T(8,128)S(1)}, f32[72,128]{1,0:T(8,128)S(1)}, u32[]{:S(2)}, u32[]{:S(2)}) collective-permute-start(f32[72,128]{1,0:T(8,128)S(1)} %get-tuple-element.24), channel_id=1, source_target_pairs={{0,8},{8,16},{16,24},{24,32},{32,40},{40,48},{48,56},{56,0},{1,9},... | collective-permute-start | bytes 110600 | tf_op jit(solution)/shard_map/ppermute | solution.py:415
  25.5 1.1 %collective-permute-done.2.lo = f32[72,128]{1,0:T(8,128)S(1)} collective-permute-done((f32[72,128]{1,0:T(8,128)S(1)}, f32[72,128]{1,0:T(8,128)S(1)}, u32[]{:S(2)}, u32[]{:S(2)}) %collective-permute-start.2) | collective-permute-done | bytes 36896 | tf_op jit(solution)/shard_map/ppermute | solution.py:415
  26.6 1.0 %collective-permute-done.3.hi = f32[2,72,128]{2,1,0:T(8,128)S(1)} collective-permute-done((f32[2,72,128]{2,1,0:T(8,128)S(1)}, f32[2,72,128]{2,1,0:T(8,128)S(1)}, u32[]{:S(2)}, u32[]{:S(2)}) %collective-permute-start.3) | collective-permute-done | bytes 73760 | tf_op jit(solution)/shard_map/ppermute | solution.py:415
  27.5 0.4 pack_z.1
  28.0 1.5 %collective-permute-start.4 = (f32[9,72,128]{2,1,0:T(8,128)S(1)}, f32[9,72,128]{2,1,0:T(8,128)S(1)}, u32[]{:S(2)}, u32[]{:S(2)}) collective-permute-start(f32[9,72,128]{2,1,0:T(8,128)S(1)} %get-tuple-element.27), channel_id=1, source_target_pairs={{0,1},{1,2},{2,3},{3,4},{4,5},{5,6},{6,7},{7,0},{8,9},{9,10},{10,1... | collective-permute-start | bytes 995336 | tf_op jit(solution)/shard_map/ppermute | solution.py:415
  29.4 2.5 %collective-permute-start.5 = (f32[9,72,128]{2,1,0:T(8,128)S(1)}, f32[9,72,128]{2,1,0:T(8,128)S(1)}, u32[]{:S(2)}, u32[]{:S(2)}) collective-permute-start(f32[9,72,128]{2,1,0:T(8,128)S(1)} %get-tuple-element.28), channel_id=1, source_target_pairs={{1,0},{2,1},{3,2},{4,3},{5,4},{6,5},{7,6},{0,7},{9,8},{10,9},{11,1... | collective-permute-start | bytes 995336 | tf_op jit(solution)/shard_map/ppermute | solution.py:415
  32.0 5.3 %collective-permute-done.4.zlo = f32[9,72,128]{2,1,0:T(8,128)S(1)} collective-permute-done((f32[9,72,128]{2,1,0:T(8,128)S(1)}, f32[9,72,128]{2,1,0:T(8,128)S(1)}, u32[]{:S(2)}, u32[]{:S(2)}) %collective-permute-start.4) | collective-permute-done | bytes 331808 | tf_op jit(solution)/shard_map/ppermute | solution.py:415
  37.3 5.5 %collective-permute-done.5.zhi = f32[9,72,128]{2,1,0:T(8,128)S(1)} collective-permute-done((f32[9,72,128]{2,1,0:T(8,128)S(1)}, f32[9,72,128]{2,1,0:T(8,128)S(1)}, u32[]{:S(2)}, u32[]{:S(2)}) %collective-permute-start.5) | collective-permute-done | bytes 331808 | tf_op jit(solution)/shard_map/ppermute | solution.py:415
  42.7 13.4 %compute.1 = (f32[16,64,128]{2,1,0:T(8,128)}, f32[16,64,128]{2,1,0:T(8,128)}, f32[8,32,8,128]{3,2,1,0:T(8,128)S(1)}) custom-call(f32[16,64,128]{2,1,0:T(8,128)S(1)} %copy-done.1, f32[16,64,128]{2,1,0:T(8,128)S(1)} %copy-done.3, f32[16,64,128]{2,1,0:T(8,128)S(1)} %copy-done.5, f32[16,64,128]{2,1,0:T(8,128)S(1)} %copy-done.7, f32[16,64,128]{2,1,0:T(8,128)S(1)} %copy-done.9, ...), custom_call_target="tpu_custom_call" | custom-call | tf_op jit(solution)/shard_map/compute/pallas_call | solution.py:405
  56.1 22.7 %all_to_all.5.got = f32[8,32,8,128]{3,2,1,0:T(8,128)S(1)} all-to-all(f32[8,32,8,128]{3,2,1,0:T(8,128)S(1)} %get-tuple-element.31), channel_id=1, replica_groups=mesh['gx'=4,'gy'=8,'gz'=8] {'gy'}, dimensions={0} | all-to-all | bytes 2097152 | tf_op jit(solution)/shard_map/all_to_all | solution.py:436
  78.8 2.2 %finish.1 = (f32[16,8,1024]{2,1,0:T(8,128)}, f32[16,8,1024]{2,1,0:T(8,128)}) custom-call(f32[8,32,8,128]{3,2,1,0:T(8,128)S(1)} %all_to_all.5.got), custom_call_target="tpu_custom_call" | custom-call | tf_op jit(solution)/shard_map/finish/pallas_call | solution.py:405
  (18 shorter events, 0.0 us)
Async XLA Ops:
  0.6 1.0 %copy-start = (f32[16,64,128]{2,1,0:T(8,128)S(1)}, f32[16,64,128]{2,1,0:T(8,128)}, u32[]{:S(2)}) copy-start(f32[16,64,128]{2,1,0:T(8,128)} %pr.7) | copy-start | bytes 1572868
  1.7 1.0 %copy-start.2 = (f32[16,64,128]{2,1,0:T(8,128)S(1)}, f32[16,64,128]{2,1,0:T(8,128)}, u32[]{:S(2)}) copy-start(f32[16,64,128]{2,1,0:T(8,128)} %pi.7) | copy-start | bytes 1572868
  2.7 1.0 %copy-start.4 = (f32[16,64,128]{2,1,0:T(8,128)S(1)}, f32[16,64,128]{2,1,0:T(8,128)}, u32[]{:S(2)}) copy-start(f32[16,64,128]{2,1,0:T(8,128)} %px.7) | copy-start | bytes 1572868
  3.8 1.0 %copy-start.6 = (f32[16,64,128]{2,1,0:T(8,128)S(1)}, f32[16,64,128]{2,1,0:T(8,128)}, u32[]{:S(2)}) copy-start(f32[16,64,128]{2,1,0:T(8,128)} %py.7) | copy-start | bytes 1572868
  4.8 1.0 %copy-start.8 = (f32[16,64,128]{2,1,0:T(8,128)S(1)}, f32[16,64,128]{2,1,0:T(8,128)}, u32[]{:S(2)}) copy-start(f32[16,64,128]{2,1,0:T(8,128)} %pz.7) | copy-start | bytes 1572868
  5.8 1.0 %copy-start.10 = (s32[16,64,128]{2,1,0:T(8,128)S(1)}, s32[16,64,128]{2,1,0:T(8,128)}, u32[]{:S(2)}) copy-start(s32[16,64,128]{2,1,0:T(8,128)} %mat.1) | copy-start | bytes 1572868
  6.9 0.7 copy-start.11
  7.5 14.0 %copy-start.1 = (f32[16,64,128]{2,1,0:T(8,128)S(1)}, f32[16,64,128]{2,1,0:T(8,128)}, u32[]{:S(2)}) copy-start(f32[16,64,128]{2,1,0:T(8,128)} %pr.7) | copy-start | bytes 1572868
  7.5 14.0 %copy-start.3 = (f32[16,64,128]{2,1,0:T(8,128)S(1)}, f32[16,64,128]{2,1,0:T(8,128)}, u32[]{:S(2)}) copy-start(f32[16,64,128]{2,1,0:T(8,128)} %pi.7) | copy-start | bytes 1572868
  7.5 14.0 %copy-start.5 = (f32[16,64,128]{2,1,0:T(8,128)S(1)}, f32[16,64,128]{2,1,0:T(8,128)}, u32[]{:S(2)}) copy-start(f32[16,64,128]{2,1,0:T(8,128)} %px.7) | copy-start | bytes 1572868
  7.5 14.0 %copy-start.7 = (f32[16,64,128]{2,1,0:T(8,128)S(1)}, f32[16,64,128]{2,1,0:T(8,128)}, u32[]{:S(2)}) copy-start(f32[16,64,128]{2,1,0:T(8,128)} %py.7) | copy-start | bytes 1572868
  7.6 14.0 %copy-start.9 = (f32[16,64,128]{2,1,0:T(8,128)S(1)}, f32[16,64,128]{2,1,0:T(8,128)}, u32[]{:S(2)}) copy-start(f32[16,64,128]{2,1,0:T(8,128)} %pz.7) | copy-start | bytes 1572868
  8.7 12.8 %collective-permute-start.1 = (f32[16,16,128]{2,1,0:T(8,128)S(1)}, f32[16,16,128]{2,1,0:T(8,128)S(1)}, u32[]{:S(2)}, u32[]{:S(2)}) collective-permute-start(f32[16,16,128]{2,1,0:T(8,128)S(1)} %get-tuple-element.21), channel_id=1, source_target_pairs={{64,0},{128,64},{192,128},{0,192},{65,1},{129,65},{193,129},{1,193... | collective-permute-start | bytes 393224 | tf_op jit(solution)/shard_map/ppermute | solution.py:415
  15.6 5.9 %collective-permute-start = (f32[16,8,128]{2,1,0:T(8,128)S(1)}, f32[16,8,128]{2,1,0:T(8,128)S(1)}, u32[]{:S(2)}, u32[]{:S(2)}) collective-permute-start(f32[16,8,128]{2,1,0:T(8,128)S(1)} %get-tuple-element.20), channel_id=1, source_target_pairs={{0,64},{64,128},{128,192},{192,0},{1,65},{65,129},{129,193},{193,1... | collective-permute-start | bytes 196616 | tf_op jit(solution)/shard_map/ppermute | solution.py:415
  22.8 4.7 %collective-permute-start.3 = (f32[2,72,128]{2,1,0:T(8,128)S(1)}, f32[2,72,128]{2,1,0:T(8,128)S(1)}, u32[]{:S(2)}, u32[]{:S(2)}) collective-permute-start(f32[2,72,128]{2,1,0:T(8,128)S(1)} %get-tuple-element.25), channel_id=1, source_target_pairs={{8,0},{16,8},{24,16},{32,24},{40,32},{48,40},{56,48},{0,56},{9,1},... | collective-permute-start | bytes 221192 | tf_op jit(solution)/shard_map/ppermute | solution.py:415
  24.4 2.2 %collective-permute-start.2 = (f32[72,128]{1,0:T(8,128)S(1)}, f32[72,128]{1,0:T(8,128)S(1)}, u32[]{:S(2)}, u32[]{:S(2)}) collective-permute-start(f32[72,128]{1,0:T(8,128)S(1)} %get-tuple-element.24), channel_id=1, source_target_pairs={{0,8},{8,16},{16,24},{24,32},{32,40},{40,48},{48,56},{56,0},{1,9},... | collective-permute-start | bytes 110600 | tf_op jit(solution)/shard_map/ppermute | solution.py:415
  28.0 9.3 %collective-permute-start.4 = (f32[9,72,128]{2,1,0:T(8,128)S(1)}, f32[9,72,128]{2,1,0:T(8,128)S(1)}, u32[]{:S(2)}, u32[]{:S(2)}) collective-permute-start(f32[9,72,128]{2,1,0:T(8,128)S(1)} %get-tuple-element.27), channel_id=1, source_target_pairs={{0,1},{1,2},{2,3},{3,4},{4,5},{5,6},{6,7},{7,0},{8,9},{9,10},{10,1... | collective-permute-start | bytes 995336 | tf_op jit(solution)/shard_map/ppermute | solution.py:415
  29.4 13.3 %collective-permute-start.5 = (f32[9,72,128]{2,1,0:T(8,128)S(1)}, f32[9,72,128]{2,1,0:T(8,128)S(1)}, u32[]{:S(2)}, u32[]{:S(2)}) collective-permute-start(f32[9,72,128]{2,1,0:T(8,128)S(1)} %get-tuple-element.28), channel_id=1, source_target_pairs={{1,0},{2,1},{3,2},{4,3},{5,4},{6,5},{7,6},{0,7},{9,8},{10,9},{11,1... | collective-permute-start | bytes 995336 | tf_op jit(solution)/shard_map/ppermute | solution.py:415

commit v2 on v1

v2 whole, which is shorter than its diff:
```python
import jax
import jax.numpy as jnp
from jax import lax
from jax.experimental import pallas as pl
from jax.experimental.pallas import tpu as pltpu
from jax.sharding import PartitionSpec as P


LEVELS = 8
time_step = 0.15

F32 = jnp.float32
LANES = 128
TILE = 8
NZ, NX, NY = 16, 64, 128
RX = NX + TILE
PR, PI, PX, PY, PZ, EP = range(6)

SIN = (1.0, -0.16666658222675323, 0.008333050645887852, -0.00019809069635812193, 2.6052216526295524e-06)
COS = (-0.5, 0.0416666604578495, -0.0013888651737943292, 2.4774621124379337e-05, -2.6298400257473986e-07)


def sincos(phase):
    half = phase * 0.5
    u = half * half
    s = SIN[4]
    for k in (3, 2, 1, 0):
        s = s * u + SIN[k]
    s = s * half
    c = COS[4]
    for k in (3, 2, 1, 0):
        c = c * u + COS[k]
    c = c * u + 1.0
    return (c - s) * (c + s), (s + s) * c


def iota(shape, dim):
    return lax.broadcasted_iota(jnp.int32, shape, dim)


def roll(v, shift, axis):
    return pltpu.roll(v, shift % v.shape[axis], axis)


def ahead_x(v):
    return pltpu.roll(v, RX - 1, 0)


def behind_x(v):
    return pltpu.roll(v, 1, 0)


def turned(c, s, r, i):
    return c * r - s * i, c * i + s * r


def turned_back(c, s, r, i):
    return c * r + s * i, c * i - s * r


def row_up(a, row):
    pr, pi, px, py, pz, ep = a
    c, s = sincos(px)
    wr, wi = turned_back(c, s, pr, pi)
    last = row == 6
    pr = jnp.where(last, wr, pr)
    pi = jnp.where(last, wi, pi)
    out = roll(pr, 2, 0)
    out = jnp.where(row >= 2, roll(pi, 4, 0), out)
    out = jnp.where(row == 4, roll(px, 5, 0), out)
    out = jnp.where(row == 5, roll(py, 6, 0), out)
    out = jnp.where(row == 6, roll(pz, 7, 0), out)
    return jnp.where(row == 7, ep, out)


def row_down(a, row):
    pr, pi, px, py, pz, ep = a
    first = jnp.where(row < 3, pr, jnp.where(row < 6, roll(pi, 3, 0), roll(px, 6, 0)))
    second = jnp.where(row < 2, py, jnp.where(row < 4, roll(pz, 2, 0), roll(ep, 4, 0)))
    return first, second


def scaled_levels(levels):
    return [1.0 + time_step * (levels[k] - 6.0) for k in range(LEVELS)]


def material_gain(m, values):
    e = jnp.full(m.shape, values[LEVELS - 1], F32)
    for k in range(LEVELS - 1):
        e = jnp.where(m == k, values[k], e)
    return e


def start_copies(pairs, sems):
    copies = [pltpu.make_async_copy(a, b, sems.at[n]) for n, (a, b) in enumerate(pairs)]
    for copy in copies:
        copy.start()
    return copies


def pack_x(levels_in, pr, pi, px, py, pz, mat, up, down, levels, top, low, top_mat, low_mat, sems):
    fields = (pr, pi, px, py, pz)
    pairs = [(levels_in, levels)]
    pairs += [(q.at[:, pl.ds(NX - TILE, TILE), :], top.at[k]) for k, q in enumerate(fields)]
    pairs += [(q.at[:, pl.ds(0, TILE), :], low.at[k]) for k, q in enumerate(fields)]
    pairs += [(mat.at[:, pl.ds(NX - TILE, TILE), :], top_mat), (mat.at[:, pl.ds(0, TILE), :], low_mat)]
    for copy in start_copies(pairs, sems):
        copy.wait()
    row = iota((TILE, LANES), 0)
    values = scaled_levels(levels)

    def body(z, carry):
        up[z] = row_up([top[k, z] for k in range(5)] + [material_gain(top_mat[z], values)], row)
        first, second = row_down([low[k, z] for k in range(5)] + [material_gain(low_mat[z], values)], row)
        down[z, :TILE, :] = first
        down[z, TILE:, :] = second
        return carry

    lax.fori_loop(0, NZ, body, 0, unroll=2)


def prepare(levels_in, pr_in, pi_in, px_in, py_in, pz_in, mat_in, pr, pi, ep, trig, own, up, down,
            levels, px, py, pz, mat, sems):
    pairs = [(levels_in, levels), (mat_in, mat), (pz_in, pz), (px_in, px), (py_in, py), (pr_in, pr), (pi_in, pi)]
    copies = start_copies(pairs, sems)
    copies[0].wait()
    copies[1].wait()
    values = scaled_levels(levels)

    def gains(z, carry):
        ep[z] = material_gain(mat[z], values)
        return carry

    lax.fori_loop(0, NZ, gains, 0)
    for n, q in enumerate((pz, px, py)):
        copies[2 + n].wait()

        def angles(z, carry):
            trig[2 * n, z], trig[2 * n + 1, z] = sincos(q[z])
            return carry

        lax.fori_loop(0, NZ, angles, 0)
    copies[5].wait()
    copies[6].wait()
    group = iota((NX, LANES), 1) // 8
    for k, q in enumerate((pr, pi, px, py, pz, ep)):
        acc = jnp.zeros((NX, LANES), F32)
        for z in range(NZ):
            acc = jnp.where(group == z, roll(q[z], 8 * z - 126, 1), acc)
        own[k] = acc
    up[0], up[1] = turned_back(trig[0, 14], trig[1, 14], pr[14], pi[14])
    down[0] = pr[1]
    down[1] = pi[1]
    for k, q in enumerate((pr, pi, px, py, pz, ep)):
        up[2 + k] = q[15]
        down[2 + k] = q[0]


def pack_y(own_in, lo, hi, halo, own, up, down):
    row = iota((TILE, LANES), 0)
    gx = lax.axis_index("gx")
    keep = jnp.where(row < 4, jnp.where(gx < lax.axis_size("gx") - 1, 1, 0), jnp.where(gx > 0, 1, 0)) > 0
    low_rows = row >= 6
    last = row == 7
    group = iota((TILE, LANES), 1) // 8
    acc = [jnp.zeros((TILE, LANES), F32) for _ in range(6)]
    for z in range(NZ):
        l = lo[z]
        a = hi[z, :TILE, :]
        b = hi[z, TILE:, :]
        zero = jnp.zeros_like(l)
        tiles = (
            jnp.where(keep, jnp.where(low_rows, roll(l, 6, 0), a), zero),
            jnp.where(keep, jnp.where(low_rows, roll(l, 4, 0), roll(a, -3, 0)), zero),
            jnp.where(last, roll(l, 3, 0), jnp.where(row < 2, roll(a, -6, 0), zero)),
            jnp.where(last, roll(l, 2, 0), jnp.where(row < 2, b, zero)),
            jnp.where(last, roll(l, 1, 0), jnp.where(row < 2, roll(b, -2, 0), zero)),
            jnp.where(last, l, jnp.where(row < 2, roll(b, -4, 0), zero)),
        )
        for k, tile in enumerate(tiles):
            halo[k, z] = tile
            acc[k] = jnp.where(group == z, roll(tile, 8 * z - 126, 1), acc[k])
    columns = []
    for k in range(6):
        v = jnp.concatenate([own_in[k], acc[k]], axis=0)
        own[k] = v
        columns.append(v)
    slot = iota((RX, LANES), 1) % 8
    vr, vi, vx, vy, vz, ve = columns
    c, s = sincos(vy)
    wr, wi = turned_back(c, s, vr, vi)
    ur = jnp.where(slot == 0, wr, vr)
    ui = jnp.where(slot == 0, wi, vi)
    out = jnp.where(slot < 2, ur, roll(ui, 2, 1))
    out = jnp.where(slot == 4, roll(vx, 3, 1), out)
    out = jnp.where(slot == 5, roll(vy, 4, 1), out)
    out = jnp.where(slot == 6, roll(vz, 5, 1), out)
    out = jnp.where(slot == 7, roll(ve, 6, 1), out)
    up[...] = out
    down[0] = jnp.where(slot < 3, roll(vr, -2, 1), jnp.where(slot < 6, roll(vi, 1, 1), roll(vx, 4, 1)))
    down[1] = jnp.where(slot < 2, roll(vy, -2, 1), jnp.where(slot < 4, vz, roll(ve, 2, 1)))


def tall(q, h, z):
    return jnp.concatenate([q[z], h[z]], axis=0)


def angles_at(trig, trig_halo, n, z):
    return jnp.concatenate([trig[n, z], trig_halo[n, z]], axis=0)


def advance(centre, above, below_turned, trig, edge, gain, lane):
    r, i = centre
    cz, sz, cx, sx, cy, sy = trig
    t = turned(cx, sx, ahead_x(r), ahead_x(i))
    w = turned_back(cx, sx, r, i)
    sum_r, sum_i = t[0] + behind_x(w[0]), t[1] + behind_x(w[1])
    if below_turned is not None:
        sum_r, sum_i = sum_r + below_turned[0], sum_i + below_turned[1]
    if above is not None:
        t = turned(cz, sz, *above)
        sum_r, sum_i = sum_r + t[0], sum_i + t[1]
    fr, fi = r, i
    wr, wi = turned_back(cy, sy, r, i)
    if edge is not None:
        fr, fi = jnp.where(lane == 0, edge[0], r), jnp.where(lane == 0, edge[1], i)
        wr, wi = jnp.where(lane == 127, edge[0], wr), jnp.where(lane == 127, edge[1], wi)
    t = turned(cy, sy, roll(fr, -1, 1), roll(fi, -1, 1))
    sum_r, sum_i = sum_r + t[0] + roll(wr, 1, 1), sum_i + t[1] + roll(wi, 1, 1)
    gain = gain - time_step * (r * r + i * i)
    return gain * r + time_step * sum_r, gain * i + time_step * sum_i


def begin(pr, pi, ep, trig, halo, trig_halo, br, bi):
    lane = iota((RX, LANES), 1)
    zero = jnp.zeros((RX, LANES), F32)

    def angles(z, carry):
        for n, k in enumerate((PZ, PX, PY)):
            trig_halo[2 * n, z], trig_halo[2 * n + 1, z] = sincos(halo[k, z])
        return carry

    lax.fori_loop(0, NZ, angles, 0)
    none = (zero, zero)

    def layer(z):
        return tall(pr, halo.at[PR], z), tall(pi, halo.at[PI], z)

    def one(z, above, below):
        t = [angles_at(trig, trig_halo, n, z) for n in range(6)]
        if below is not None:
            below = turned_back(angles_at(trig, trig_halo, 0, below), angles_at(trig, trig_halo, 1, below),
                                *layer(below))
        if above is not None:
            above = layer(above)
        br[z], bi[z] = advance(layer(z), above, below, t, none, tall(ep, halo.at[EP], z), lane)

    one(0, 1, None)

    def body(z, carry):
        one(z, z + 1, z - 1)
        return carry

    lax.fori_loop(1, NZ - 1, body, 0)
    one(NZ - 1, None, NZ - 2)


def pack_edges(trig_halo, halo, own, lo, hi, strip, up, down):
    lane = iota((RX, LANES), 1)
    slot = lane % 8
    group = lane // 8
    gy = lax.axis_index("gy")
    keep = jnp.where((slot >= 2) & (slot < 5), jnp.where(gy < lax.axis_size("gy") - 1, 1, 0),
                     jnp.where((slot >= 5) & (slot < 7), jnp.where(gy > 0, 1, 0), 1)) > 0
    l = lo[...]
    a = hi[0]
    b = hi[1]
    zero = jnp.zeros_like(l)

    def join(k, from_hi, from_lo):
        v = own[k]
        out = jnp.where(slot < 2, v, roll(v, 5, 1))
        out = jnp.where((slot >= 2) & (slot < 5), from_hi, out)
        return jnp.where((slot == 5) | (slot == 6), from_lo, out)

    one = slot == 6
    strip[PR] = jnp.where(keep, join(PR, roll(a, 2, 1), roll(l, 5, 1)), zero)
    strip[PI] = jnp.where(keep, join(PI, roll(a, -1, 1), roll(l, 3, 1)), zero)
    strip[PX] = join(PX, roll(a, -4, 1), jnp.where(one, roll(l, 2, 1), zero))
    strip[PY] = join(PY, roll(b, 2, 1), jnp.where(one, roll(l, 1, 1), zero))
    strip[PZ] = join(PZ, b, jnp.where(one, l, zero))
    strip[EP] = join(EP, roll(b, -2, 1), jnp.where(one, roll(l, -1, 1), zero))
    up[0], up[1] = turned_back(trig_halo[0, 14], trig_halo[1, 14], halo[PR, 14], halo[PI, 14])
    down[0] = halo[PR, 1]
    down[1] = halo[PI, 1]
    for k in range(6):
        up[2 + k] = halo[k, 15]
        down[2 + k] = halo[k, 0]
    c, s = sincos(strip[PZ])
    wr, wi = turned_back(c, s, strip[PR], strip[PI])
    out = jnp.where(group == 0, roll(wr, -8 * 14, 1), roll(wi, -8 * 13, 1))
    for k in range(6):
        out = jnp.where(group == 2 + k, roll(strip[k], 8 * (2 + k - 15), 1), out)
    for t in range(RX // TILE):
        up[8 + t] = out[t * TILE:(t + 1) * TILE]
    out = jnp.where(group == 0, roll(strip[PR], -8, 1), strip[PI])
    for k in range(6):
        out = jnp.where(group == 2 + k, roll(strip[k], 8 * (2 + k), 1), out)
    for t in range(RX // TILE):
        down[8 + t] = out[t * TILE:(t + 1) * TILE]


def shift_of(group):
    return (126 - 8 * group) % 128


def on(test):
    return jnp.where(test, 1, 0)


def inside_masks():
    row = iota((RX, LANES), 0)
    slot = iota((RX, LANES), 1) % 8
    gx, gy = lax.axis_index("gx"), lax.axis_index("gy")
    keep_x = jnp.where(row < NX, 1, jnp.where(row < NX + 4, on(gx < lax.axis_size("gx") - 1), on(gx > 0)))
    keep_y = jnp.where((slot >= 2) & (slot < 5), on(gy < lax.axis_size("gy") - 1),
                       jnp.where((slot >= 5) & (slot < 7), on(gy > 0), 1))
    return keep_x, keep_x * keep_y


def edge_columns(slot, ntrig, r, i):
    wr, wi = turned_back(ntrig[4], ntrig[5], r, i)
    return jnp.where(slot == 1, roll(wr, -5, 1), r), jnp.where(slot == 1, roll(wi, -5, 1), i)


def analyse(z, r, i, trig_x, trig_y, columns, jx_column, lane, triangle, out):
    shift = shift_of(z)
    t = turned(*trig_x, ahead_x(r), ahead_x(i))
    jx = r * t[1] - i * t[0]
    fr = jnp.where(lane == 0, roll_by(columns[0], shift), r)
    fi = jnp.where(lane == 0, roll_by(columns[1], shift), i)
    t = turned(*trig_y, roll(fr, -1, 1), roll(fi, -1, 1))
    jy = r * t[1] - i * t[0]
    jx_next = roll(jnp.where(lane == 0, roll_by(jx_column, shift), jx), -1, 1)
    circulation = (jx + ahead_x(jy) - jx_next - jy)[:NX]
    sums = jnp.dot(jx[:NX], triangle, precision=lax.Precision.HIGHEST, preferred_element_type=F32)
    for j in range(NX // TILE):
        out[j, z] = circulation[j * TILE:(j + 1) * TILE]
        out[j, NZ + z] = sums[j * TILE:(j + 1) * TILE]


def roll_by(v, shift):
    return pltpu.roll(v, shift, 1)


def triangle_of():
    return jnp.where(iota((LANES, LANES), 0) <= iota((LANES, LANES), 1), 1.0, 0.0).astype(F32)


def interior(pr_in, pi_in, ep, trig, halo, trig_halo, strip, ntrig, cr, ci, final_r, final_i, out,
             er, ei, nr, ni, jx_edge):
    lane = iota((RX, LANES), 1)
    slot = lane % 8
    keep_x, keep_xy = inside_masks()
    zero = jnp.zeros((RX, LANES), F32)
    for n, k in enumerate((PZ, PX, PY)):
        ntrig[2 * n], ntrig[2 * n + 1] = sincos(strip[k])
    nt = lambda: [ntrig[n] for n in range(6)]
    er[...], ei[...] = edge_columns(slot, ntrig, strip[PR], strip[PI])

    def fix(z, carry):
        shift = shift_of(z)
        xr, xi = roll_by(er[...], shift), roll_by(ei[...], shift)
        cy, sy = angles_at(trig, trig_halo, 4, z), angles_at(trig, trig_halo, 5, z)
        hr, hi = turned(cy, sy, roll(xr, -1, 1), roll(xi, -1, 1))
        lr, li = roll(xr, 1, 1), roll(xi, 1, 1)
        r = pr_in[z] + time_step * jnp.where(lane == 127, hr, jnp.where(lane == 0, lr, zero))
        i = pi_in[z] + time_step * jnp.where(lane == 127, hi, jnp.where(lane == 0, li, zero))
        cr[z] = jnp.where(keep_x > 0, r, zero)
        ci[z] = jnp.where(keep_x > 0, i, zero)
        return carry

    lax.fori_loop(0, NZ, fix, 0)

    def strips(r, i):
        w = turned_back(ntrig[0], ntrig[1], r, i)
        v = advance((r, i), (roll(r, -8, 1), roll(i, -8, 1)), (roll(w[0], 8, 1), roll(w[1], 8, 1)), nt(), None,
                    strip[EP], lane)
        return jnp.where(keep_xy > 0, v[0], zero), jnp.where(keep_xy > 0, v[1], zero)

    mr, mi = strips(strip[PR], strip[PI])
    er[...], ei[...] = edge_columns(slot, ntrig, mr, mi)
    r, i = strips(mr, mi)
    nr[...] = r
    ni[...] = i
    t = turned(ntrig[2], ntrig[3], ahead_x(r), ahead_x(i))
    jx_edge[...] = r * t[1] - i * t[0]
    triangle = triangle_of()

    def second(z, carry):
        last_layer(z, (cr[z], ci[z]), (cr[z + 1], ci[z + 1]), (cr[z - 1], ci[z - 1]), ep, trig, halo, trig_halo,
                   (er[...], ei[...]), (nr[...], ni[...]), jx_edge[...], keep_x, lane, triangle,
                   final_r, final_i, out, None)
        return carry

    lax.fori_loop(2, NZ - 2, second, 0)


def last_layer(z, centre, above, below, ep, trig, halo, trig_halo, edges, columns, jx_column, keep_x, lane,
               triangle, final_r, final_i, out, below_turned):
    t = [angles_at(trig, trig_halo, n, z) for n in range(6)]
    if below_turned is None:
        below_turned = turned_back(angles_at(trig, trig_halo, 0, z - 1), angles_at(trig, trig_halo, 1, z - 1), *below)
    shift = shift_of(z)
    edge = roll_by(edges[0], shift), roll_by(edges[1], shift)
    r, i = advance(centre, above, below_turned, t, edge, tall(ep, halo.at[EP], z), lane)
    zero = jnp.zeros((RX, LANES), F32)
    r = jnp.where(keep_x > 0, r, zero)
    i = jnp.where(keep_x > 0, i, zero)
    final_r[z] = r[:NX]
    final_i[z] = i[:NX]
    analyse(z, r, i, t[2:4], t[4:6], columns, jx_column, lane, triangle, out)


def boundary(pr, pi, ep, trig, halo, trig_halo, strip, ntrig0, cr, ci, some_r, some_i, some_out,
             zlo, zhi, elo, ehi, final_r, final_i, out, ntrig1):
    lane = iota((RX, LANES), 1)
    slot = lane % 8
    group = lane // 8
    keep_x, keep_xy = inside_masks()
    gz = lax.axis_index("gz")
    z_hi, z_lo = on(gz < lax.axis_size("gz") - 1), on(gz > 0)
    keep_z = jnp.where(group < 8, z_hi, z_lo)
    zero = jnp.zeros((RX, LANES), F32)
    final_r[2:NZ - 2] = some_r[2:NZ - 2]
    final_i[2:NZ - 2] = some_i[2:NZ - 2]
    for j in range(NX // TILE):
        out[j, 2:NZ - 2] = some_out[j, 2:NZ - 2]
        out[j, NZ + 2:2 * NZ - 2] = some_out[j, NZ + 2:2 * NZ - 2]
    lo8 = jnp.concatenate([elo[8 + t] for t in range(RX // TILE)], axis=0)
    hi8 = jnp.concatenate([ehi[8 + t] for t in range(RX // TILE)], axis=0)

    def beyond(k, outer):
        v = jnp.where(group == 0, roll(hi8, -8 * (2 + k), 1), roll(lo8, 8 * (15 - 2 - k), 1))
        if outer is not None:
            v = jnp.where(group == 1, roll(hi8, 8 * (1 - outer), 1), v)
            v = jnp.where(group == 14, roll(lo8, 8 * (14 - outer), 1), v)
        return v

    for n, k in enumerate((PZ, PX, PY)):
        v = beyond(k, None)
        if k == PZ:
            v = jnp.where(group == 14, zero, v)
        ntrig1[2 * n], ntrig1[2 * n + 1] = sincos(v)
    trigs = (ntrig0, ntrig1)
    gains = (strip[EP], beyond(EP, None))

    def step_strips(halves, wanted):
        w = [turned_back(trigs[h][0], trigs[h][1], *halves[h]) for h in range(2)]
        results = []
        for h in wanted:
            g = 1 - h
            below = [jnp.where(group == 0, roll(w[g][n], 8, 1), roll(w[h][n], 8, 1)) for n in range(2)]
            above = [jnp.where(group == 15, roll(halves[g][n], -8, 1), roll(halves[h][n], -8, 1)) for n in range(2)]
            v = advance(halves[h], above, below, [trigs[h][n] for n in range(6)], None, gains[h], lane)
            keep = keep_xy if h == 0 else keep_xy * keep_z
            results.append([jnp.where(keep > 0, u, zero) for u in v])
        return results

    halves = ((strip[PR], strip[PI]),
              (jnp.where(keep_z > 0, beyond(PR, 0), zero), jnp.where(keep_z > 0, beyond(PI, 1), zero)))
    beyond_edge = edge_columns(slot, ntrig1, *halves[1])
    middle = step_strips(halves, (0, 1))
    edges = edge_columns(slot, ntrig0, *middle[0])
    (columns,) = step_strips(middle, (0,))
    t = turned(ntrig0[2], ntrig0[3], ahead_x(columns[0]), ahead_x(columns[1]))
    jx_column = columns[0] * t[1] - columns[1] * t[0]

    ok_lo = jnp.broadcast_to(z_lo, (RX, LANES)) > 0
    ok_hi = jnp.broadcast_to(z_hi, (RX, LANES)) > 0

    def got(main, tiles, n):
        return jnp.concatenate([main[n], tiles[n]], axis=0)

    def angles(main, tiles):
        found = []
        for k in (PZ, PX, PY):
            found += list(sincos(got(main, tiles, 2 + k)))
        return found

    def own(z):
        return tall(pr, halo.at[PR], z), tall(pi, halo.at[PI], z)

    def masked(ok, v):
        return tuple(jnp.where(ok, u, zero) for u in v)

    def at(z, n):
        return angles_at(trig, trig_halo, n, z)

    t_lo = angles(zlo, elo)
    outer = masked(ok_lo, (got(zlo, elo, 0), got(zlo, elo, 1)))
    inner = masked(ok_lo, (got(zlo, elo, 2), got(zlo, elo, 3)))
    edge = roll_by(beyond_edge[0], shift_of(15)), roll_by(beyond_edge[1], shift_of(15))
    v = masked(ok_lo & (keep_x > 0), advance(inner, own(0), outer, t_lo, edge, got(zlo, elo, 2 + EP), lane))
    w = turned_back(t_lo[0], t_lo[1], *inner)
    first = masked(keep_x > 0, (cr[0] + time_step * w[0], ci[0] + time_step * w[1]))
    below = turned_back(t_lo[0], t_lo[1], *v)
    triangle = triangle_of()
    common = (ep, trig, halo, trig_halo, edges, columns, jx_column, keep_x, lane, triangle, final_r, final_i, out)
    last_layer(0, first, (cr[1], ci[1]), None, *common, below)
    last_layer(1, (cr[1], ci[1]), (cr[2], ci[2]), first, *common, None)
    t_hi = angles(zhi, ehi)
    outer = masked(ok_hi, (got(zhi, ehi, 0), got(zhi, ehi, 1)))
    inner = masked(ok_hi, (got(zhi, ehi, 2), got(zhi, ehi, 3)))
    edge = roll_by(beyond_edge[0], shift_of(0)), roll_by(beyond_edge[1], shift_of(0))
    below = turned_back(at(15, 0), at(15, 1), *own(15))
    v = masked(ok_hi & (keep_x > 0), advance(inner, outer, below, t_hi, edge, got(zhi, ehi, 2 + EP), lane))
    w = turned(at(15, 0), at(15, 1), *inner)
    final = masked(keep_x > 0, (cr[15] + time_step * w[0], ci[15] + time_step * w[1]))
    last_layer(14, (cr[14], ci[14]), final, (cr[13], ci[13]), *common, None)
    last_layer(15, final, v, (cr[14], ci[14]), *common, None)


def finish(got, circulation, flux):
    def body(z, carry):
        before = jnp.zeros((TILE, 1), F32)
        for j in range(got.shape[0]):
            circulation[z, :, j * LANES:(j + 1) * LANES] = got[j, z]
            v = got[j, NZ + z]
            flux[z, :, j * LANES:(j + 1) * LANES] = v + before
            before = before + v[:, LANES - 1:]
        return carry

    lax.fori_loop(0, NZ, body, 0)


def spec(*shape):
    return jax.ShapeDtypeStruct(shape, F32)


def call(body, outs, *args, scratch=(), hbm=0, room=32 * 2**20):
    memory = [pl.BlockSpec(memory_space=pltpu.HBM if k < hbm else pltpu.VMEM) for k in range(len(args))]
    return pl.pallas_call(
        body, out_shape=outs, in_specs=memory, scratch_shapes=list(scratch),
        out_specs=jax.tree.map(lambda _: pl.BlockSpec(memory_space=pltpu.VMEM), outs),
        compiler_params=pltpu.CompilerParams(vmem_limit_bytes=room),
    )(*args)


def exchange(up, down, axis):
    size = lax.axis_size(axis)
    forward = [(k, (k + 1) % size) for k in range(size)]
    lo = lax.ppermute(up, axis, forward)
    hi = lax.ppermute(down, axis, [(b, a) for a, b in forward])
    return lo, hi


def program(pr_in, pi_in, pz_in, px_in, py_in, material, levels):
    parts = lax.axis_size("gy")
    raw = (levels, pr_in, pi_in, px_in, py_in, pz_in, material)
    raw = tuple(pltpu.with_memory_space_constraint(a, pltpu.HBM) for a in raw)
    edge = spec(NZ, TILE, LANES)
    block, tall_block, strip_like = spec(NZ, NX, NY), spec(NZ, RX, LANES), spec(RX, LANES)
    scratch = lambda s, dtype=F32: pltpu.VMEM(s.shape, dtype)
    up, down = call(pack_x, (edge, spec(NZ, 2 * TILE, LANES)), *raw, hbm=7, scratch=[
        pltpu.SMEM((LEVELS,), F32), pltpu.VMEM((5, NZ, TILE, LANES), F32), pltpu.VMEM((5, NZ, TILE, LANES), F32),
        scratch(edge, jnp.int32), scratch(edge, jnp.int32), pltpu.SemaphoreType.DMA((13,))])
    lo, hi = exchange(up, down, "gx")
    pr, pi, ep, trig, own, zup, zdown = call(
        prepare, (block, block, block, spec(6, NZ, NX, NY), spec(6, NX, LANES), spec(8, NX, NY), spec(8, NX, NY)),
        *raw, hbm=7, scratch=[pltpu.SMEM((LEVELS,), F32), scratch(block), scratch(block), scratch(block),
                              scratch(block, jnp.int32), pltpu.SemaphoreType.DMA((7,))])
    zlo, zhi = exchange(zup, zdown, "gz")
    halo, own, up, down = call(
        pack_y, (spec(6, NZ, TILE, LANES), spec(6, RX, LANES), strip_like, spec(2, RX, LANES)), own, lo, hi)
    lo, hi = exchange(up, down, "gy")
    trig_halo, br, bi = call(begin, (spec(6, NZ, TILE, LANES), tall_block, tall_block), pr, pi, ep, trig, halo)
    strip, up, down = call(pack_edges, (spec(6, RX, LANES), spec(17, TILE, LANES), spec(17, TILE, LANES)),
                           trig_halo, halo, own, lo, hi)
    elo, ehi = exchange(up, down, "gz")
    out = spec(parts, 2 * NZ, TILE, LANES)
    ntrig, cr, ci, some_r, some_i, some_out = call(
        interior, (spec(6, RX, LANES), tall_block, tall_block, block, block, out),
        br, bi, ep, trig, halo, trig_halo, strip, scratch=[scratch(strip_like)] * 5)
    final_r, final_i, out = call(
        boundary, (block, block, out), pr, pi, ep, trig, halo, trig_halo, strip, ntrig, cr, ci,
        some_r, some_i, some_out, zlo, zhi, elo, ehi, scratch=[pltpu.VMEM((6, RX, LANES), F32)])
    got = lax.all_to_all(out, "gy", 0, 0, tiled=True)
    circulation, flux = call(finish, (spec(NZ, TILE, parts * LANES), spec(NZ, TILE, parts * LANES)), got)
    return final_r, final_i, circulation, flux


def solution(mesh):
    block = P("gz", "gx", "gy")
    slab = P("gz", ("gx", "gy"), None)
    return jax.shard_map(program, mesh=mesh, in_specs=(block,) * 6 + (P(),),
                         out_specs=(block, block, slab, slab), check_vma=False)
```

time: 81.4 us -> 71.5 us (0.88)
  local copies, waits for them, and re-layouts: 6.91 us -> 0 us
  waiting for transfers between devices: 18.7 us -> 11.9 us
  starting transfers between devices: 13.6 us -> 17.5 us
  Pallas kernels: 18.3 us -> 21.2 us
  blocking collectives: 22.7 us -> 20 us
    unnamed x24 -> x0, local copies, waits for them, and re-layouts: 6.91 us -> none
    ppermute x6 -> x8, waiting for transfers between devices: 18.7 us -> 11.9 us  [the longest x4 11.9 us: exchange(): lo = lax.ppermute(up, axis, forward)]
    ppermute x6 -> x8, starting transfers between devices: 13.6 us -> 17.5 us  [the longest x4 15.4 us: exchange(): hi = lax.ppermute(down, axis, [(b, a) for a, b in forward])]
    pallas_call x5 -> x8, Pallas kernels: 18.3 us -> 21.2 us  [call(): pl.pallas_call(body, out_shape=outs, in_specs=memory, scratch_shapes=list...]
    all_to_all x1, blocking collectives: 22.7 us -> 20 us  [program(): got = lax.all_to_all(out, 'gy', 0, 0, tiled=True)]
  transfers between devices with their start and end apart: 6 -> 8, of which waited for: 5 -> 1; matrix products, arithmetic and copies ran while one was open for 0% -> 0% of each run, Pallas kernels for 0% -> 20%
where the time goes in v2:
time: 71.5 us; the launch traced here: 71.3 us
  Pallas kernels  21.2 us (30%)
  blocking collectives  20 us (28%)
  starting transfers between devices  17.5 us (24%)
  waiting for transfers between devices  11.9 us (17%)
  between operations  0.74 us (1%)
    pallas_call x8, Pallas kernels, call(): pl.pallas_call(body, out_shape=outs, in_specs=memory, scratch_shapes=list...  21.2 us
    all_to_all x1, blocking collectives, program(): got = lax.all_to_all(out, 'gy', 0, 0, tiled=True)  20 us
    ppermute x4, starting transfers between devices, exchange(): hi = lax.ppermute(down, axis, [(b, a) for a, b in forward])  15.4 us
    ppermute x4, waiting for transfers between devices, exchange(): lo = lax.ppermute(up, axis, forward)  11.9 us
    ppermute x4, starting transfers between devices, exchange(): lo = lax.ppermute(up, axis, forward)  2.02 us
  transfers between devices with their start and end apart: 8, of which 1 were waited for; matrix products, arithmetic and copies ran while one was open for 0% of the time, Pallas kernels for 20%

profile of v2, /device:TPU:1, one launch (start us, length us, event | category | flops | bytes accessed | tf_op | source)
XLA Modules:
  0.0 71.3 jit_solution(2906288945799805845)
XLA Ops:
  0.6 1.5 %shard_map.103 = (f32[16,8,128]{2,1,0:T(8,128)S(1)}, f32[16,16,128]{2,1,0:T(8,128)S(1)}) custom-call(f32[8]{0:T(128)} %levels_in.3, f32[16,64,128]{2,1,0:T(8,128)} %pr.1, f32[16,64,128]{2,1,0:T(8,128)} %pi.1, f32[16,64,128]{2,1,0:T(8,128)} %px.1, f32[16,64,128]{2,1,0:T(8,128)} %py.1, f32[16,64,128]{2,1,0:T(8,128)} %pz.1, s32[16,64,128]{2,1,0:T(8,128)} %mat.1), custom_call_target="tpu_custom_call" | custom-call | tf_op jit(solution)/shard_map/pallas_call | solution.py:543
  2.1 6.9 %collective-permute-start.1 = (f32[16,16,128]{2,1,0:T(8,128)S(1)}, f32[16,16,128]{2,1,0:T(8,128)S(1)}, u32[]{:S(2)}, u32[]{:S(2)}) collective-permute-start(f32[16,16,128]{2,1,0:T(8,128)S(1)} %get-tuple-element.40), channel_id=1, source_target_pairs={{64,0},{128,64},{192,128},{0,192},{65,1},{129,65},{193,129},{1,193... | collective-permute-start | bytes 393224 | tf_op jit(solution)/shard_map/ppermute | solution.py:554
  9.1 3.9 %shard_map.102 = (f32[16,64,128]{2,1,0:T(8,128)S(1)}, f32[16,64,128]{2,1,0:T(8,128)S(1)}, f32[16,64,128]{2,1,0:T(8,128)S(1)}, f32[6,16,64,128]{3,2,1,0:T(8,128)S...) custom-call(f32[8]{0:T(128)} %levels_in.3, f32[16,64,128]{2,1,0:T(8,128)} %pr.1, ...), custom_call_target="tpu_custom_call" | custom-call | tf_op jit(solution)/shard_map/pallas_call | solution.py:543
  13.0 0.8 %collective-permute-start.4 = (f32[8,64,128]{2,1,0:T(8,128)S(1)}, f32[8,64,128]{2,1,0:T(8,128)S(1)}, u32[]{:S(2)}, u32[]{:S(2)}) collective-permute-start(f32[8,64,128]{2,1,0:T(8,128)S(1)} %get-tuple-element.55), channel_id=1, source_target_pairs={{0,1},{1,2},{2,3},{3,4},{4,5},{5,6},{6,7},{7,0},{8,9},{9,10},{10,1... | collective-permute-start | bytes 786440 | tf_op jit(solution)/shard_map/ppermute | solution.py:553
  13.8 2.8 %collective-permute-start.5 = (f32[8,64,128]{2,1,0:T(8,128)S(1)}, f32[8,64,128]{2,1,0:T(8,128)S(1)}, u32[]{:S(2)}, u32[]{:S(2)}) collective-permute-start(f32[8,64,128]{2,1,0:T(8,128)S(1)} %get-tuple-element.56), channel_id=1, source_target_pairs={{1,0},{2,1},{3,2},{4,3},{5,4},{6,5},{7,6},{0,7},{9,8},{10,9},{11,1... | collective-permute-start | bytes 786440 | tf_op jit(solution)/shard_map/ppermute | solution.py:554
  16.7 0.0 collective-permute-start
  16.7 11.9 %collective-permute-done.lo = f32[16,8,128]{2,1,0:T(8,128)S(1)} collective-permute-done((f32[16,8,128]{2,1,0:T(8,128)S(1)}, f32[16,8,128]{2,1,0:T(8,128)S(1)}, u32[]{:S(2)}, u32[]{:S(2)}) %collective-permute-start) | collective-permute-done | bytes 65568 | tf_op jit(solution)/shard_map/ppermute | solution.py:553
  28.6 0.0 collective-permute-done.1.hi
  28.6 0.3 shard_map.104
  28.9 2.1 %collective-permute-start.3 = (f32[2,72,128]{2,1,0:T(8,128)S(1)}, f32[2,72,128]{2,1,0:T(8,128)S(1)}, u32[]{:S(2)}, u32[]{:S(2)}) collective-permute-start(f32[2,72,128]{2,1,0:T(8,128)S(1)} %get-tuple-element.45), channel_id=1, source_target_pairs={{8,0},{16,8},{24,16},{32,24},{40,32},{48,40},{56,48},{0,56},{9,1},... | collective-permute-start | bytes 221192 | tf_op jit(solution)/shard_map/ppermute | solution.py:554
  31.0 1.1 %collective-permute-start.2 = (f32[72,128]{1,0:T(8,128)S(1)}, f32[72,128]{1,0:T(8,128)S(1)}, u32[]{:S(2)}, u32[]{:S(2)}) collective-permute-start(f32[72,128]{1,0:T(8,128)S(1)} %get-tuple-element.44), channel_id=1, source_target_pairs={{0,8},{8,16},{16,24},{24,32},{32,40},{40,48},{48,56},{56,0},{1,9},... | collective-permute-start | bytes 110600 | tf_op jit(solution)/shard_map/ppermute | solution.py:553
  32.2 2.1 %shard_map.105 = (f32[6,16,8,128]{3,2,1,0:T(8,128)S(1)}, f32[16,72,128]{2,1,0:T(8,128)S(1)}, f32[16,72,128]{2,1,0:T(8,128)S(1)}) custom-call(f32[16,64,128]{2,1,0:T(8,128)S(1)} %get-tuple-element.34.pr, f32[16,64,128]{2,1,0:T(8,128)S(1)} %get-tuple-element.35.pi, f32[16,64,128]{2,1,0:T(8,128)S(1)} %get-tuple-element.36.ep, ...), custom_call_target="tpu_custom_call" | custom-call | tf_op jit(solution)/shard_map/pallas_call | solution.py:543
  34.3 0.0 collective-permute-done.2.lo
  34.3 0.0 collective-permute-done.3.hi
  34.3 0.4 shard_map.106
  34.7 0.1 collective-permute-start.6
  34.8 3.6 %collective-permute-start.7 = (f32[17,8,128]{2,1,0:T(8,128)S(1)}, f32[17,8,128]{2,1,0:T(8,128)S(1)}, u32[]{:S(2)}, u32[]{:S(2)}) collective-permute-start(f32[17,8,128]{2,1,0:T(8,128)S(1)} %get-tuple-element.58), channel_id=1, source_target_pairs={{1,0},{2,1},{3,2},{4,3},{5,4},{6,5},{7,6},{0,7},{9,8},{10,9},{11,1... | collective-permute-start | bytes 208904 | tf_op jit(solution)/shard_map/ppermute | solution.py:554
  38.4 7.7 %shard_map.107 = (f32[6,72,128]{2,1,0:T(8,128)S(1)}, f32[16,72,128]{2,1,0:T(8,128)S(1)}, f32[16,72,128]{2,1,0:T(8,128)S(1)}, f32[16,64,128]{2,1,0:T(8,128)S(1)},...) custom-call(f32[16,72,128]{2,1,0:T(8,128)S(1)} %get-tuple-element.47.pr_in, ...), custom_call_target="tpu_custom_call" | custom-call | tf_op jit(solution)/shard_map/pallas_call | solution.py:543
  46.1 0.0 collective-permute-done.4.zlo
  46.1 0.0 collective-permute-done.5.zhi
  46.1 0.0 collective-permute-done.7.ehi
  46.1 3.0 %shard_map.108 = (f32[16,64,128]{2,1,0:T(8,128)}, f32[16,64,128]{2,1,0:T(8,128)}, f32[8,32,8,128]{3,2,1,0:T(8,128)S(1)}) custom-call(f32[16,64,128]{2,1,0:T(8,128)S(1)} %get-tuple-element.34.pr, f32[16,64,128]{2,1,0:T(8,128)S(1)} %get-tuple-element.35.pi, f32[16,64,128]{2,1,0:T(8,128)S(1)} %get-tuple-element.36.ep, ...), custom_call_target="tpu_custom_call" | custom-call | tf_op jit(solution)/shard_map/pallas_call | solution.py:543
  49.1 20.0 %all_to_all.5.got = f32[8,32,8,128]{3,2,1,0:T(8,128)S(1)} all-to-all(f32[8,32,8,128]{3,2,1,0:T(8,128)S(1)} %get-tuple-element.61), channel_id=1, replica_groups=mesh['gx'=4,'gy'=8,'gz'=8] {'gy'}, dimensions={0} | all-to-all | bytes 2097152 | tf_op jit(solution)/shard_map/all_to_all | solution.py:588
  69.1 2.2 %shard_map.109 = (f32[16,8,1024]{2,1,0:T(8,128)}, f32[16,8,1024]{2,1,0:T(8,128)}) custom-call(f32[8,32,8,128]{3,2,1,0:T(8,128)S(1)} %all_to_all.5.got), custom_call_target="tpu_custom_call" | custom-call | tf_op jit(solution)/shard_map/pallas_call | solution.py:543
  (1 shorter events, 0.0 us)
Async XLA Ops:
  2.1 26.4 %collective-permute-start.1 = (f32[16,16,128]{2,1,0:T(8,128)S(1)}, f32[16,16,128]{2,1,0:T(8,128)S(1)}, u32[]{:S(2)}, u32[]{:S(2)}) collective-permute-start(f32[16,16,128]{2,1,0:T(8,128)S(1)} %get-tuple-element.40), channel_id=1, source_target_pairs={{64,0},{128,64},{192,128},{0,192},{65,1},{129,65},{193,129},{1,193... | collective-permute-start | bytes 393224 | tf_op jit(solution)/shard_map/ppermute | solution.py:554
  13.0 33.1 %collective-permute-start.4 = (f32[8,64,128]{2,1,0:T(8,128)S(1)}, f32[8,64,128]{2,1,0:T(8,128)S(1)}, u32[]{:S(2)}, u32[]{:S(2)}) collective-permute-start(f32[8,64,128]{2,1,0:T(8,128)S(1)} %get-tuple-element.55), channel_id=1, source_target_pairs={{0,1},{1,2},{2,3},{3,4},{4,5},{5,6},{6,7},{7,0},{8,9},{9,10},{10,1... | collective-permute-start | bytes 786440 | tf_op jit(solution)/shard_map/ppermute | solution.py:553
  13.8 32.3 %collective-permute-start.5 = (f32[8,64,128]{2,1,0:T(8,128)S(1)}, f32[8,64,128]{2,1,0:T(8,128)S(1)}, u32[]{:S(2)}, u32[]{:S(2)}) collective-permute-start(f32[8,64,128]{2,1,0:T(8,128)S(1)} %get-tuple-element.56), channel_id=1, source_target_pairs={{1,0},{2,1},{3,2},{4,3},{5,4},{6,5},{7,6},{0,7},{9,8},{10,9},{11,1... | collective-permute-start | bytes 786440 | tf_op jit(solution)/shard_map/ppermute | solution.py:554
  16.7 11.9 %collective-permute-start = (f32[16,8,128]{2,1,0:T(8,128)S(1)}, f32[16,8,128]{2,1,0:T(8,128)S(1)}, u32[]{:S(2)}, u32[]{:S(2)}) collective-permute-start(f32[16,8,128]{2,1,0:T(8,128)S(1)} %get-tuple-element.39), channel_id=1, source_target_pairs={{0,64},{64,128},{128,192},{192,0},{1,65},{65,129},{129,193},{193,1... | collective-permute-start | bytes 196616 | tf_op jit(solution)/shard_map/ppermute | solution.py:553
  28.9 5.4 %collective-permute-start.3 = (f32[2,72,128]{2,1,0:T(8,128)S(1)}, f32[2,72,128]{2,1,0:T(8,128)S(1)}, u32[]{:S(2)}, u32[]{:S(2)}) collective-permute-start(f32[2,72,128]{2,1,0:T(8,128)S(1)} %get-tuple-element.45), channel_id=1, source_target_pairs={{8,0},{16,8},{24,16},{32,24},{40,32},{48,40},{56,48},{0,56},{9,1},... | collective-permute-start | bytes 221192 | tf_op jit(solution)/shard_map/ppermute | solution.py:554
  31.0 3.2 %collective-permute-start.2 = (f32[72,128]{1,0:T(8,128)S(1)}, f32[72,128]{1,0:T(8,128)S(1)}, u32[]{:S(2)}, u32[]{:S(2)}) collective-permute-start(f32[72,128]{1,0:T(8,128)S(1)} %get-tuple-element.44), channel_id=1, source_target_pairs={{0,8},{8,16},{16,24},{24,32},{32,40},{40,48},{48,56},{56,0},{1,9},... | collective-permute-start | bytes 110600 | tf_op jit(solution)/shard_map/ppermute | solution.py:553
  34.7 11.4 %collective-permute-start.6 = (f32[17,8,128]{2,1,0:T(8,128)S(1)}, f32[17,8,128]{2,1,0:T(8,128)S(1)}, u32[]{:S(2)}, u32[]{:S(2)}) collective-permute-start(f32[17,8,128]{2,1,0:T(8,128)S(1)} %get-tuple-element.57), channel_id=1, source_target_pairs={{0,1},{1,2},{2,3},{3,4},{4,5},{5,6},{6,7},{7,0},{8,9},{9,10},{10,1... | collective-permute-start | bytes 208904 | tf_op jit(solution)/shard_map/ppermute | solution.py:553
  34.8 11.3 %collective-permute-start.7 = (f32[17,8,128]{2,1,0:T(8,128)S(1)}, f32[17,8,128]{2,1,0:T(8,128)S(1)}, u32[]{:S(2)}, u32[]{:S(2)}) collective-permute-start(f32[17,8,128]{2,1,0:T(8,128)S(1)} %get-tuple-element.58), channel_id=1, source_target_pairs={{1,0},{2,1},{3,2},{4,3},{5,4},{6,5},{7,6},{0,7},{9,8},{10,9},{11,1... | collective-permute-start | bytes 208904 | tf_op jit(solution)/shard_map/ppermute | solution.py:554

commit v3 on v2

--- a/solution.py
+++ b/solution.py
@@ -15,6 +15,8 @@
 NZ, NX, NY = 16, 64, 128
 RX = NX + TILE
 PR, PI, PX, PY, PZ, EP = range(6)
+EARLY = ()
+LATE = (4, 3, 5, 2, 6, 1, 7)
 
 SIN = (1.0, -0.16666658222675323, 0.008333050645887852, -0.00019809069635812193, 2.6052216526295524e-06)
 COS = (-0.5, 0.0416666604578495, -0.0013888651737943292, 2.4774621124379337e-05, -2.6298400257473986e-07)
@@ -333,7 +335,7 @@
     return jnp.where(slot == 1, roll(wr, -5, 1), r), jnp.where(slot == 1, roll(wi, -5, 1), i)
 
 
-def analyse(z, r, i, trig_x, trig_y, columns, jx_column, lane, triangle, out):
+def analyse(z, r, i, trig_x, trig_y, columns, jx_column, lane, triangle, out, spot, gap):
     shift = shift_of(z)
     t = turned(*trig_x, ahead_x(r), ahead_x(i))
     jx = r * t[1] - i * t[0]
@@ -345,8 +347,9 @@
     circulation = (jx + ahead_x(jy) - jx_next - jy)[:NX]
     sums = jnp.dot(jx[:NX], triangle, precision=lax.Precision.HIGHEST, preferred_element_type=F32)
     for j in range(NX // TILE):
-        out[j, z] = circulation[j * TILE:(j + 1) * TILE]
-        out[j, NZ + z] = sums[j * TILE:(j + 1) * TILE]
+        away = (j + out.shape[0] - lax.axis_index("gy")) % out.shape[0]
+        out[away, spot] = circulation[j * TILE:(j + 1) * TILE]
+        out[away, spot + gap] = sums[j * TILE:(j + 1) * TILE]
 
 
 def roll_by(v, shift):
@@ -380,7 +383,8 @@
         ci[z] = jnp.where(keep_x > 0, i, zero)
         return carry
 
-    lax.fori_loop(0, NZ, fix, 0)
+    for z in range(NZ):
+        fix(z, 0)
 
     def strips(r, i):
         w = turned_back(ntrig[0], ntrig[1], r, i)
@@ -400,14 +404,15 @@
     def second(z, carry):
         last_layer(z, (cr[z], ci[z]), (cr[z + 1], ci[z + 1]), (cr[z - 1], ci[z - 1]), ep, trig, halo, trig_halo,
                    (er[...], ei[...]), (nr[...], ni[...]), jx_edge[...], keep_x, lane, triangle,
-                   final_r, final_i, out, None)
+                   final_r, final_i, out, None, z - 2, NZ - 4)
         return carry
 
-    lax.fori_loop(2, NZ - 2, second, 0)
+    for z in range(2, NZ - 2):
+        second(z, 0)
 
 
 def last_layer(z, centre, above, below, ep, trig, halo, trig_halo, edges, columns, jx_column, keep_x, lane,
-               triangle, final_r, final_i, out, below_turned):
+               triangle, final_r, final_i, out, below_turned, spot, gap):
     t = [angles_at(trig, trig_halo, n, z) for n in range(6)]
     if below_turned is None:
         below_turned = turned_back(angles_at(trig, trig_halo, 0, z - 1), angles_at(trig, trig_halo, 1, z - 1), *below)
@@ -419,10 +424,10 @@
     i = jnp.where(keep_x > 0, i, zero)
     final_r[z] = r[:NX]
     final_i[z] = i[:NX]
-    analyse(z, r, i, t[2:4], t[4:6], columns, jx_column, lane, triangle, out)
-
-
-def boundary(pr, pi, ep, trig, halo, trig_halo, strip, ntrig0, cr, ci, some_r, some_i, some_out,
+    analyse(z, r, i, t[2:4], t[4:6], columns, jx_column, lane, triangle, out, spot, gap)
+
+
+def boundary(pr, pi, ep, trig, halo, trig_halo, strip, ntrig0, cr, ci, some_r, some_i, middle_out,
              zlo, zhi, elo, ehi, final_r, final_i, out, ntrig1):
     lane = iota((RX, LANES), 1)
     slot = lane % 8
@@ -432,11 +437,10 @@
     z_hi, z_lo = on(gz < lax.axis_size("gz") - 1), on(gz > 0)
     keep_z = jnp.where(group < 8, z_hi, z_lo)
     zero = jnp.zeros((RX, LANES), F32)
+    for away in range(out.shape[0]):
+        out[away, 8:] = middle_out[away]
     final_r[2:NZ - 2] = some_r[2:NZ - 2]
     final_i[2:NZ - 2] = some_i[2:NZ - 2]
-    for j in range(NX // TILE):
-        out[j, 2:NZ - 2] = some_out[j, 2:NZ - 2]
-        out[j, NZ + 2:2 * NZ - 2] = some_out[j, NZ + 2:2 * NZ - 2]
     lo8 = jnp.concatenate([elo[8 + t] for t in range(RX // TILE)], axis=0)
     hi8 = jnp.concatenate([ehi[8 + t] for t in range(RX // TILE)], axis=0)
 
@@ -507,8 +511,8 @@
     below = turned_back(t_lo[0], t_lo[1], *v)
     triangle = triangle_of()
     common = (ep, trig, halo, trig_halo, edges, columns, jx_column, keep_x, lane, triangle, final_r, final_i, out)
-    last_layer(0, first, (cr[1], ci[1]), None, *common, below)
-    last_layer(1, (cr[1], ci[1]), (cr[2], ci[2]), first, *common, None)
+    last_layer(0, first, (cr[1], ci[1]), None, *common, below, 0, 4)
+    last_layer(1, (cr[1], ci[1]), (cr[2], ci[2]), first, *common, None, 1, 4)
     t_hi = angles(zhi, ehi)
     outer = masked(ok_hi, (got(zhi, ehi, 0), got(zhi, ehi, 1)))
     inner = masked(ok_hi, (got(zhi, ehi, 2), got(zhi, ehi, 3)))
@@ -517,33 +521,62 @@
     v = masked(ok_hi & (keep_x > 0), advance(inner, outer, below, t_hi, edge, got(zhi, ehi, 2 + EP), lane))
     w = turned(at(15, 0), at(15, 1), *inner)
     final = masked(keep_x > 0, (cr[15] + time_step * w[0], ci[15] + time_step * w[1]))
-    last_layer(14, (cr[14], ci[14]), final, (cr[13], ci[13]), *common, None)
-    last_layer(15, final, v, (cr[14], ci[14]), *common, None)
-
-
-def finish(got, circulation, flux):
-    def body(z, carry):
+    last_layer(14, (cr[14], ci[14]), final, (cr[13], ci[13]), *common, None, 2, 4)
+    last_layer(15, final, v, (cr[14], ci[14]), *common, None, 3, 4)
+
+
+ENDS = (0, 1, NZ - 2, NZ - 1)
+
+
+def finish(*refs):
+    parts = lax.axis_size("gy")
+    got, (circulation, flux, ends, middle, full_c, full_f, sems) = refs[:-7], refs[-7:]
+    me = lax.axis_index("gy")
+    for k in range(parts):
+        source = (me + parts - k) % parts
+        if k in EARLY:
+            ends[source] = got[len(EARLY) + k][...]
+            middle[source] = got[EARLY.index(k)][...]
+        else:
+            ends[source] = got[len(EARLY) + k][:8]
+            middle[source] = got[len(EARLY) + k][8:]
+
+    def layer(pieces, spot, gap, z):
         before = jnp.zeros((TILE, 1), F32)
-        for j in range(got.shape[0]):
-            circulation[z, :, j * LANES:(j + 1) * LANES] = got[j, z]
-            v = got[j, NZ + z]
-            flux[z, :, j * LANES:(j + 1) * LANES] = v + before
+        for j in range(parts):
+            full_c[z, :, j * LANES:(j + 1) * LANES] = pieces[j, spot]
+            v = pieces[j, spot + gap]
+            full_f[z, :, j * LANES:(j + 1) * LANES] = v + before
             before = before + v[:, LANES - 1:]
-        return carry
-
-    lax.fori_loop(0, NZ, body, 0)
+
+    copies = []
+
+    def send(first):
+        for a, b in ((full_c, circulation), (full_f, flux)):
+            copies.append(pltpu.make_async_copy(a.at[pl.ds(first, 4)], b.at[pl.ds(first, 4)], sems.at[len(copies)]))
+            copies[-1].start()
+
+    for first in (4, 8, 0, 12):
+        for z in range(first, first + 4):
+            if z in ENDS:
+                layer(ends, ENDS.index(z), 4, z)
+            else:
+                layer(middle, z - 2, NZ - 4, z)
+        send(first)
+    for copy in copies:
+        copy.wait()
 
 
 def spec(*shape):
     return jax.ShapeDtypeStruct(shape, F32)
 
 
-def call(body, outs, *args, scratch=(), hbm=0, room=32 * 2**20):
+def call(body, outs, *args, scratch=(), hbm=0, hbm_out=False):
     memory = [pl.BlockSpec(memory_space=pltpu.HBM if k < hbm else pltpu.VMEM) for k in range(len(args))]
     return pl.pallas_call(
         body, out_shape=outs, in_specs=memory, scratch_shapes=list(scratch),
-        out_specs=jax.tree.map(lambda _: pl.BlockSpec(memory_space=pltpu.VMEM), outs),
-        compiler_params=pltpu.CompilerParams(vmem_limit_bytes=room),
+        out_specs=jax.tree.map(lambda _: pl.BlockSpec(memory_space=pltpu.HBM if hbm_out else pltpu.VMEM), outs),
+        compiler_params=pltpu.CompilerParams(vmem_limit_bytes=32 * 2**20),
     )(*args)
 
 
@@ -553,6 +586,11 @@
     lo = lax.ppermute(up, axis, forward)
     hi = lax.ppermute(down, axis, [(b, a) for a, b in forward])
     return lo, hi
+
+
+def ahead(value, k):
+    size = lax.axis_size("gy")
+    return lax.ppermute(value, "gy", [(i, (i + k) % size) for i in range(size)])
 
 
 def program(pr_in, pi_in, pz_in, px_in, py_in, material, levels):
@@ -578,15 +616,19 @@
     strip, up, down = call(pack_edges, (spec(6, RX, LANES), spec(17, TILE, LANES), spec(17, TILE, LANES)),
                            trig_halo, halo, own, lo, hi)
     elo, ehi = exchange(up, down, "gz")
-    out = spec(parts, 2 * NZ, TILE, LANES)
-    ntrig, cr, ci, some_r, some_i, some_out = call(
-        interior, (spec(6, RX, LANES), tall_block, tall_block, block, block, out),
+    ntrig, cr, ci, some_r, some_i, out = call(
+        interior, (spec(6, RX, LANES), tall_block, tall_block, block, block, spec(parts, 2 * NZ - 8, TILE, LANES)),
         br, bi, ep, trig, halo, trig_halo, strip, scratch=[scratch(strip_like)] * 5)
+    got = [ahead(out[k], k) for k in EARLY]
     final_r, final_i, out = call(
-        boundary, (block, block, out), pr, pi, ep, trig, halo, trig_halo, strip, ntrig, cr, ci,
-        some_r, some_i, some_out, zlo, zhi, elo, ehi, scratch=[pltpu.VMEM((6, RX, LANES), F32)])
-    got = lax.all_to_all(out, "gy", 0, 0, tiled=True)
-    circulation, flux = call(finish, (spec(NZ, TILE, parts * LANES), spec(NZ, TILE, parts * LANES)), got)
+        boundary, (block, block, spec(parts, 2 * NZ, TILE, LANES)), pr, pi, ep, trig, halo, trig_halo, strip, ntrig, cr, ci,
+        some_r, some_i, out, zlo, zhi, elo, ehi, scratch=[pltpu.VMEM((6, RX, LANES), F32)])
+    late = {k: ahead(out[k, :8] if k in EARLY else out[k], k) for k in LATE}
+    got += [out[0]] + [late[k] for k in range(1, parts)]
+    slab = spec(NZ, TILE, parts * LANES)
+    circulation, flux = call(finish, (slab, slab), *got, hbm_out=True, scratch=[
+        pltpu.VMEM((parts, 8, TILE, LANES), F32), pltpu.VMEM((parts, 2 * NZ - 8, TILE, LANES), F32),
+        scratch(slab), scratch(slab), pltpu.SemaphoreType.DMA((8,))])
     return final_r, final_i, circulation, flux
 
 

time: 71.5 us -> 65.2 us (0.912)
  the two profiles are of different devices: /device:TPU:1 before, /device:TPU:8 now
where the time goes in v3:
time: 65.2 us; the launch traced here: 65 us
  waiting for transfers between devices  27.7 us (42%)
  starting transfers between devices  18.6 us (29%)
  Pallas kernels  17.7 us (27%)
  between operations  0.9 us (1%)
    pallas_call x8, Pallas kernels, call(): pl.pallas_call(body, out_shape=outs, in_specs=memory, scratch_shapes=list...  17.7 us
    ppermute x4, waiting for transfers between devices, exchange(): lo = lax.ppermute(up, axis, forward)  16.2 us
    ppermute x4, starting transfers between devices, exchange(): hi = lax.ppermute(down, axis, [(b, a) for a, b in forward])  12 us
    ppermute x7, waiting for transfers between devices, ahead(): return lax.ppermute(value, 'gy', [(i, (i + k) % size) for i in range(size)])  11.5 us
    ppermute x7, starting transfers between devices, ahead(): return lax.ppermute(value, 'gy', [(i, (i + k) % size) for i in range(size)])  5.4 us
  transfers between devices with their start and end apart: 15, of which 8 were waited for; matrix products, arithmetic and copies ran while one was open for 0% of the time, Pallas kernels for 19%

profile of v3, /device:TPU:8, one launch (start us, length us, event | category | flops | bytes accessed | tf_op | source)
XLA Modules:
  0.0 65.0 jit_solution(15508352369113488369)
XLA Ops:
  0.6 1.5 %shard_map.103 = (f32[16,8,128]{2,1,0:T(8,128)S(1)}, f32[16,16,128]{2,1,0:T(8,128)S(1)}) custom-call(f32[8]{0:T(128)} %levels_in.3, f32[16,64,128]{2,1,0:T(8,128)} %pr.1, f32[16,64,128]{2,1,0:T(8,128)} %pi.1, f32[16,64,128]{2,1,0:T(8,128)} %px.1, f32[16,64,128]{2,1,0:T(8,128)} %py.1, f32[16,64,128]{2,1,0:T(8,128)} %pz.1, s32[16,64,128]{2,1,0:T(8,128)} %mat.1), custom_call_target="tpu_custom_call" | custom-call | tf_op jit(solution)/shard_map/pallas_call | solution.py:576
  2.1 6.4 %collective-permute-start.1 = (f32[16,16,128]{2,1,0:T(8,128)S(1)}, f32[16,16,128]{2,1,0:T(8,128)S(1)}, u32[]{:S(2)}, u32[]{:S(2)}) collective-permute-start(f32[16,16,128]{2,1,0:T(8,128)S(1)} %get-tuple-element.40), channel_id=1, source_target_pairs={{64,0},{128,64},{192,128},{0,192},{65,1},{129,65},{193,129},{1,193... | collective-permute-start | bytes 393224 | tf_op jit(solution)/shard_map/ppermute | solution.py:587
  8.5 3.9 %shard_map.102 = (f32[16,64,128]{2,1,0:T(8,128)S(1)}, f32[16,64,128]{2,1,0:T(8,128)S(1)}, f32[16,64,128]{2,1,0:T(8,128)S(1)}, f32[6,16,64,128]{3,2,1,0:T(8,128)S...) custom-call(f32[8]{0:T(128)} %levels_in.3, f32[16,64,128]{2,1,0:T(8,128)} %pr.1, ...), custom_call_target="tpu_custom_call" | custom-call | tf_op jit(solution)/shard_map/pallas_call | solution.py:576
  12.5 1.1 %collective-permute-start.4 = (f32[8,64,128]{2,1,0:T(8,128)S(1)}, f32[8,64,128]{2,1,0:T(8,128)S(1)}, u32[]{:S(2)}, u32[]{:S(2)}) collective-permute-start(f32[8,64,128]{2,1,0:T(8,128)S(1)} %get-tuple-element.55), channel_id=1, source_target_pairs={{0,1},{1,2},{2,3},{3,4},{4,5},{5,6},{6,7},{7,0},{8,9},{9,10},{10,1... | collective-permute-start | bytes 786440 | tf_op jit(solution)/shard_map/ppermute | solution.py:586
  13.6 1.9 %collective-permute-start.5 = (f32[8,64,128]{2,1,0:T(8,128)S(1)}, f32[8,64,128]{2,1,0:T(8,128)S(1)}, u32[]{:S(2)}, u32[]{:S(2)}) collective-permute-start(f32[8,64,128]{2,1,0:T(8,128)S(1)} %get-tuple-element.56), channel_id=1, source_target_pairs={{1,0},{2,1},{3,2},{4,3},{5,4},{6,5},{7,6},{0,7},{9,8},{10,9},{11,1... | collective-permute-start | bytes 786440 | tf_op jit(solution)/shard_map/ppermute | solution.py:587
  15.5 13.7 %collective-permute-done.lo = f32[16,8,128]{2,1,0:T(8,128)S(1)} collective-permute-done((f32[16,8,128]{2,1,0:T(8,128)S(1)}, f32[16,8,128]{2,1,0:T(8,128)S(1)}, u32[]{:S(2)}, u32[]{:S(2)}) %collective-permute-start) | collective-permute-done | bytes 65568 | tf_op jit(solution)/shard_map/ppermute | solution.py:586
  29.2 0.3 shard_map.104
  29.5 0.8 %collective-permute-start.3 = (f32[2,72,128]{2,1,0:T(8,128)S(1)}, f32[2,72,128]{2,1,0:T(8,128)S(1)}, u32[]{:S(2)}, u32[]{:S(2)}) collective-permute-start(f32[2,72,128]{2,1,0:T(8,128)S(1)} %get-tuple-element.45), channel_id=1, source_target_pairs={{8,0},{16,8},{24,16},{32,24},{40,32},{48,40},{56,48},{0,56},{9,1},... | collective-permute-start | bytes 221192 | tf_op jit(solution)/shard_map/ppermute | solution.py:587
  30.3 2.1 %shard_map.105 = (f32[6,16,8,128]{3,2,1,0:T(8,128)S(1)}, f32[16,72,128]{2,1,0:T(8,128)S(1)}, f32[16,72,128]{2,1,0:T(8,128)S(1)}) custom-call(f32[16,64,128]{2,1,0:T(8,128)S(1)} %get-tuple-element.34.pr, f32[16,64,128]{2,1,0:T(8,128)S(1)} %get-tuple-element.35.pi, f32[16,64,128]{2,1,0:T(8,128)S(1)} %get-tuple-element.36.ep, ...), custom_call_target="tpu_custom_call" | custom-call | tf_op jit(solution)/shard_map/pallas_call | solution.py:576
  32.4 2.5 %collective-permute-done.2.lo = f32[72,128]{1,0:T(8,128)S(1)} collective-permute-done((f32[72,128]{1,0:T(8,128)S(1)}, f32[72,128]{1,0:T(8,128)S(1)}, u32[]{:S(2)}, u32[]{:S(2)}) %collective-permute-start.2) | collective-permute-done | bytes 36896 | tf_op jit(solution)/shard_map/ppermute | solution.py:586
  34.9 0.4 shard_map.106
  35.4 2.9 %collective-permute-start.7 = (f32[17,8,128]{2,1,0:T(8,128)S(1)}, f32[17,8,128]{2,1,0:T(8,128)S(1)}, u32[]{:S(2)}, u32[]{:S(2)}) collective-permute-start(f32[17,8,128]{2,1,0:T(8,128)S(1)} %get-tuple-element.58), channel_id=1, source_target_pairs={{1,0},{2,1},{3,2},{4,3},{5,4},{6,5},{7,6},{0,7},{9,8},{10,9},{11,1... | collective-permute-start | bytes 208904 | tf_op jit(solution)/shard_map/ppermute | solution.py:587
  38.4 5.3 %shard_map.107 = (f32[6,72,128]{2,1,0:T(8,128)S(1)}, f32[16,72,128]{2,1,0:T(8,128)S(1)}, f32[16,72,128]{2,1,0:T(8,128)S(1)}, f32[16,64,128]{2,1,0:T(8,128)S(1)},...) custom-call(f32[16,72,128]{2,1,0:T(8,128)S(1)} %get-tuple-element.47.pr_in, ...), custom_call_target="tpu_custom_call" | custom-call | tf_op jit(solution)/shard_map/pallas_call | solution.py:576
  43.7 2.9 %shard_map.108 = (f32[16,64,128]{2,1,0:T(8,128)}, f32[16,64,128]{2,1,0:T(8,128)}, f32[8,32,8,128]{3,2,1,0:T(8,128)S(1)}) custom-call(f32[16,64,128]{2,1,0:T(8,128)S(1)} %get-tuple-element.34.pr, f32[16,64,128]{2,1,0:T(8,128)S(1)} %get-tuple-element.35.pi, f32[16,64,128]{2,1,0:T(8,128)S(1)} %get-tuple-element.36.ep, ...), custom_call_target="tpu_custom_call" | custom-call | tf_op jit(solution)/shard_map/pallas_call | solution.py:576
  46.8 0.9 %collective-permute-start.13 = (f32[32,8,128]{2,1,0:T(8,128)S(1)}, f32[32,8,128]{2,1,0:T(8,128)S(1)}, u32[]{:S(2)}, u32[]{:S(2)}) collective-permute-start(f32[32,8,128]{2,1,0:T(8,128)S(1)} %get-tuple-element.65), channel_id=1, source_target_pairs={{0,48},{8,56},{16,0},{24,8},{32,16},{40,24},{48,32},{56,40},{1,49}... | collective-permute-start | bytes 393224 | tf_op jit(solution)/shard_map/ppermute | solution.py:593
  47.6 0.5 collective-permute-start.12
  48.2 2.7 %collective-permute-start.11 = (f32[32,8,128]{2,1,0:T(8,128)S(1)}, f32[32,8,128]{2,1,0:T(8,128)S(1)}, u32[]{:S(2)}, u32[]{:S(2)}) collective-permute-start(f32[32,8,128]{2,1,0:T(8,128)S(1)} %get-tuple-element.67), channel_id=1, source_target_pairs={{0,32},{8,40},{16,48},{24,56},{32,0},{40,8},{48,16},{56,24},{1,33}... | collective-permute-start | bytes 393224 | tf_op jit(solution)/shard_map/ppermute | solution.py:593
  50.9 1.2 %collective-permute-start.9 = (f32[32,8,128]{2,1,0:T(8,128)S(1)}, f32[32,8,128]{2,1,0:T(8,128)S(1)}, u32[]{:S(2)}, u32[]{:S(2)}) collective-permute-start(f32[32,8,128]{2,1,0:T(8,128)S(1)} %get-tuple-element.69), channel_id=1, source_target_pairs={{0,16},{8,24},{16,32},{24,40},{32,48},{40,56},{48,0},{56,8},{1,17}... | collective-permute-start | bytes 393224 | tf_op jit(solution)/shard_map/ppermute | solution.py:593
  52.2 1.4 %collective-permute-done.13.refs_6_ = f32[32,8,128]{2,1,0:T(8,128)S(1)} collective-permute-done((f32[32,8,128]{2,1,0:T(8,128)S(1)}, f32[32,8,128]{2,1,0:T(8,128)S(1)}, u32[]{:S(2)}, u32[]{:S(2)}) %collective-permute-start.13) | collective-permute-done | bytes 131104 | tf_op jit(solution)/shard_map/ppermute | solution.py:593
  53.5 1.4 %collective-permute-done.12.refs_5_ = f32[32,8,128]{2,1,0:T(8,128)S(1)} collective-permute-done((f32[32,8,128]{2,1,0:T(8,128)S(1)}, f32[32,8,128]{2,1,0:T(8,128)S(1)}, u32[]{:S(2)}, u32[]{:S(2)}) %collective-permute-start.12) | collective-permute-done | bytes 131104 | tf_op jit(solution)/shard_map/ppermute | solution.py:593
  54.9 3.0 %collective-permute-done.11.refs_4_ = f32[32,8,128]{2,1,0:T(8,128)S(1)} collective-permute-done((f32[32,8,128]{2,1,0:T(8,128)S(1)}, f32[32,8,128]{2,1,0:T(8,128)S(1)}, u32[]{:S(2)}, u32[]{:S(2)}) %collective-permute-start.11) | collective-permute-done | bytes 131104 | tf_op jit(solution)/shard_map/ppermute | solution.py:593
  57.9 0.4 collective-permute-done.10.refs_3_
  58.3 5.3 %collective-permute-done.9.refs_2_ = f32[32,8,128]{2,1,0:T(8,128)S(1)} collective-permute-done((f32[32,8,128]{2,1,0:T(8,128)S(1)}, f32[32,8,128]{2,1,0:T(8,128)S(1)}, u32[]{:S(2)}, u32[]{:S(2)}) %collective-permute-start.9) | collective-permute-done | bytes 131104 | tf_op jit(solution)/shard_map/ppermute | solution.py:593
  63.7 1.2 %shard_map.109 = (f32[16,8,1024]{2,1,0:T(8,128)}, f32[16,8,1024]{2,1,0:T(8,128)}) custom-call(f32[32,8,128]{2,1,0:T(8,128)S(1)} %get-tuple-element.71.refs_0_, f32[32,8,128]{2,1,0:T(8,128)S(1)} %collective-permute-done.8.refs_1_, f32[32,8,128]{2,1,0:T(8,128)S(1)} %collective-permute-done.9.refs_2_, f32[32,8,128]{2,1,0:T(8,128)S(1)} %collective-permute-done.10.refs_3_, ...), custom_call_target="tpu_custom_call" | custom-call | tf_op jit(solution)/shard_map/pallas_call | solution.py:576
  (15 shorter events, 0.3 us)
Async XLA Ops:
  2.1 27.0 %collective-permute-start.1 = (f32[16,16,128]{2,1,0:T(8,128)S(1)}, f32[16,16,128]{2,1,0:T(8,128)S(1)}, u32[]{:S(2)}, u32[]{:S(2)}) collective-permute-start(f32[16,16,128]{2,1,0:T(8,128)S(1)} %get-tuple-element.40), channel_id=1, source_target_pairs={{64,0},{128,64},{192,128},{0,192},{65,1},{129,65},{193,129},{1,193... | collective-permute-start | bytes 393224 | tf_op jit(solution)/shard_map/ppermute | solution.py:587
  12.5 31.2 %collective-permute-start.4 = (f32[8,64,128]{2,1,0:T(8,128)S(1)}, f32[8,64,128]{2,1,0:T(8,128)S(1)}, u32[]{:S(2)}, u32[]{:S(2)}) collective-permute-start(f32[8,64,128]{2,1,0:T(8,128)S(1)} %get-tuple-element.55), channel_id=1, source_target_pairs={{0,1},{1,2},{2,3},{3,4},{4,5},{5,6},{6,7},{7,0},{8,9},{9,10},{10,1... | collective-permute-start | bytes 786440 | tf_op jit(solution)/shard_map/ppermute | solution.py:586
  13.6 30.1 %collective-permute-start.5 = (f32[8,64,128]{2,1,0:T(8,128)S(1)}, f32[8,64,128]{2,1,0:T(8,128)S(1)}, u32[]{:S(2)}, u32[]{:S(2)}) collective-permute-start(f32[8,64,128]{2,1,0:T(8,128)S(1)} %get-tuple-element.56), channel_id=1, source_target_pairs={{1,0},{2,1},{3,2},{4,3},{5,4},{6,5},{7,6},{0,7},{9,8},{10,9},{11,1... | collective-permute-start | bytes 786440 | tf_op jit(solution)/shard_map/ppermute | solution.py:587
  15.5 13.7 %collective-permute-start = (f32[16,8,128]{2,1,0:T(8,128)S(1)}, f32[16,8,128]{2,1,0:T(8,128)S(1)}, u32[]{:S(2)}, u32[]{:S(2)}) collective-permute-start(f32[16,8,128]{2,1,0:T(8,128)S(1)} %get-tuple-element.39), channel_id=1, source_target_pairs={{0,64},{64,128},{128,192},{192,0},{1,65},{65,129},{129,193},{193,1... | collective-permute-start | bytes 196616 | tf_op jit(solution)/shard_map/ppermute | solution.py:586
  29.5 5.4 %collective-permute-start.3 = (f32[2,72,128]{2,1,0:T(8,128)S(1)}, f32[2,72,128]{2,1,0:T(8,128)S(1)}, u32[]{:S(2)}, u32[]{:S(2)}) collective-permute-start(f32[2,72,128]{2,1,0:T(8,128)S(1)} %get-tuple-element.45), channel_id=1, source_target_pairs={{8,0},{16,8},{24,16},{32,24},{40,32},{48,40},{56,48},{0,56},{9,1},... | collective-permute-start | bytes 221192 | tf_op jit(solution)/shard_map/ppermute | solution.py:587
  30.3 4.6 %collective-permute-start.2 = (f32[72,128]{1,0:T(8,128)S(1)}, f32[72,128]{1,0:T(8,128)S(1)}, u32[]{:S(2)}, u32[]{:S(2)}) collective-permute-start(f32[72,128]{1,0:T(8,128)S(1)} %get-tuple-element.44), channel_id=1, source_target_pairs={{0,8},{8,16},{16,24},{24,32},{32,40},{40,48},{48,56},{56,0},{1,9},... | collective-permute-start | bytes 110600 | tf_op jit(solution)/shard_map/ppermute | solution.py:586
  35.4 8.3 %collective-permute-start.6 = (f32[17,8,128]{2,1,0:T(8,128)S(1)}, f32[17,8,128]{2,1,0:T(8,128)S(1)}, u32[]{:S(2)}, u32[]{:S(2)}) collective-permute-start(f32[17,8,128]{2,1,0:T(8,128)S(1)} %get-tuple-element.57), channel_id=1, source_target_pairs={{0,1},{1,2},{2,3},{3,4},{4,5},{5,6},{6,7},{7,0},{8,9},{9,10},{10,1... | collective-permute-start | bytes 208904 | tf_op jit(solution)/shard_map/ppermute | solution.py:586
  35.4 8.3 %collective-permute-start.7 = (f32[17,8,128]{2,1,0:T(8,128)S(1)}, f32[17,8,128]{2,1,0:T(8,128)S(1)}, u32[]{:S(2)}, u32[]{:S(2)}) collective-permute-start(f32[17,8,128]{2,1,0:T(8,128)S(1)} %get-tuple-element.58), channel_id=1, source_target_pairs={{1,0},{2,1},{3,2},{4,3},{5,4},{6,5},{7,6},{0,7},{9,8},{10,9},{11,1... | collective-permute-start | bytes 208904 | tf_op jit(solution)/shard_map/ppermute | solution.py:587
  46.7 4.2 %collective-permute-start.14 = (f32[32,8,128]{2,1,0:T(8,128)S(1)}, f32[32,8,128]{2,1,0:T(8,128)S(1)}, u32[]{:S(2)}, u32[]{:S(2)}) collective-permute-start(f32[32,8,128]{2,1,0:T(8,128)S(1)} %get-tuple-element.64), channel_id=1, source_target_pairs={{0,56},{8,0},{16,8},{24,16},{32,24},{40,32},{48,40},{56,48},{1,57}... | collective-permute-start | bytes 393224 | tf_op jit(solution)/shard_map/ppermute | solution.py:593
  46.8 6.8 %collective-permute-start.13 = (f32[32,8,128]{2,1,0:T(8,128)S(1)}, f32[32,8,128]{2,1,0:T(8,128)S(1)}, u32[]{:S(2)}, u32[]{:S(2)}) collective-permute-start(f32[32,8,128]{2,1,0:T(8,128)S(1)} %get-tuple-element.65), channel_id=1, source_target_pairs={{0,48},{8,56},{16,0},{24,8},{32,16},{40,24},{48,32},{56,40},{1,49}... | collective-permute-start | bytes 393224 | tf_op jit(solution)/shard_map/ppermute | solution.py:593
  47.6 7.3 %collective-permute-start.12 = (f32[32,8,128]{2,1,0:T(8,128)S(1)}, f32[32,8,128]{2,1,0:T(8,128)S(1)}, u32[]{:S(2)}, u32[]{:S(2)}) collective-permute-start(f32[32,8,128]{2,1,0:T(8,128)S(1)} %get-tuple-element.66), channel_id=1, source_target_pairs={{0,40},{8,48},{16,56},{24,0},{32,8},{40,16},{48,24},{56,32},{1,41}... | collective-permute-start | bytes 393224 | tf_op jit(solution)/shard_map/ppermute | solution.py:593
  48.2 9.8 %collective-permute-start.11 = (f32[32,8,128]{2,1,0:T(8,128)S(1)}, f32[32,8,128]{2,1,0:T(8,128)S(1)}, u32[]{:S(2)}, u32[]{:S(2)}) collective-permute-start(f32[32,8,128]{2,1,0:T(8,128)S(1)} %get-tuple-element.67), channel_id=1, source_target_pairs={{0,32},{8,40},{16,48},{24,56},{32,0},{40,8},{48,16},{56,24},{1,33}... | collective-permute-start | bytes 393224 | tf_op jit(solution)/shard_map/ppermute | solution.py:593
  50.9 7.4 %collective-permute-start.10 = (f32[32,8,128]{2,1,0:T(8,128)S(1)}, f32[32,8,128]{2,1,0:T(8,128)S(1)}, u32[]{:S(2)}, u32[]{:S(2)}) collective-permute-start(f32[32,8,128]{2,1,0:T(8,128)S(1)} %get-tuple-element.68), channel_id=1, source_target_pairs={{0,24},{8,32},{16,40},{24,48},{32,56},{40,0},{48,8},{56,16},{1,25}... | collective-permute-start | bytes 393224 | tf_op jit(solution)/shard_map/ppermute | solution.py:593
  50.9 12.7 %collective-permute-start.9 = (f32[32,8,128]{2,1,0:T(8,128)S(1)}, f32[32,8,128]{2,1,0:T(8,128)S(1)}, u32[]{:S(2)}, u32[]{:S(2)}) collective-permute-start(f32[32,8,128]{2,1,0:T(8,128)S(1)} %get-tuple-element.69), channel_id=1, source_target_pairs={{0,16},{8,24},{16,32},{24,40},{32,48},{40,56},{48,0},{56,8},{1,17}... | collective-permute-start | bytes 393224 | tf_op jit(solution)/shard_map/ppermute | solution.py:593
  53.5 10.2 %collective-permute-start.8 = (f32[32,8,128]{2,1,0:T(8,128)S(1)}, f32[32,8,128]{2,1,0:T(8,128)S(1)}, u32[]{:S(2)}, u32[]{:S(2)}) collective-permute-start(f32[32,8,128]{2,1,0:T(8,128)S(1)} %get-tuple-element.70), channel_id=1, source_target_pairs={{0,8},{8,16},{16,24},{24,32},{32,40},{40,48},{48,56},{56,0},{1,9},... | collective-permute-start | bytes 393224 | tf_op jit(solution)/shard_map/ppermute | solution.py:593

commit v4 on v3

--- a/solution.py
+++ b/solution.py
@@ -16,7 +16,7 @@
 RX = NX + TILE
 PR, PI, PX, PY, PZ, EP = range(6)
 EARLY = ()
-LATE = (4, 3, 5, 2, 6, 1, 7)
+LATE = (4, 2, 6, 3, 5, 1, 7)
 
 SIN = (1.0, -0.16666658222675323, 0.008333050645887852, -0.00019809069635812193, 2.6052216526295524e-06)
 COS = (-0.5, 0.0416666604578495, -0.0013888651737943292, 2.4774621124379337e-05, -2.6298400257473986e-07)
@@ -100,13 +100,21 @@
     return copies
 
 
-def pack_x(levels_in, pr, pi, px, py, pz, mat, up, down, levels, top, low, top_mat, low_mat, sems):
+def pack_first(levels_in, pr, pi, px, py, pz, mat, up, down, zup, zdown,
+               levels, top, low, top_mat, low_mat, far, end_mat, sems):
     fields = (pr, pi, px, py, pz)
     pairs = [(levels_in, levels)]
     pairs += [(q.at[:, pl.ds(NX - TILE, TILE), :], top.at[k]) for k, q in enumerate(fields)]
     pairs += [(q.at[:, pl.ds(0, TILE), :], low.at[k]) for k, q in enumerate(fields)]
     pairs += [(mat.at[:, pl.ds(NX - TILE, TILE), :], top_mat), (mat.at[:, pl.ds(0, TILE), :], low_mat)]
-    for copy in start_copies(pairs, sems):
+    ready = len(pairs)
+    pairs += [(q.at[14], far.at[k]) for k, q in enumerate((pr, pi, pz))]
+    pairs += [(mat.at[0], end_mat.at[0]), (mat.at[15], end_mat.at[1])]
+    pairs += [(q.at[15], zup.at[2 + k]) for k, q in enumerate(fields)]
+    pairs += [(q.at[0], zdown.at[2 + k]) for k, q in enumerate(fields)]
+    pairs += [(pr.at[1], zdown.at[0]), (pi.at[1], zdown.at[1])]
+    copies = start_copies(pairs, sems)
+    for copy in copies[:ready]:
         copy.wait()
     row = iota((TILE, LANES), 0)
     values = scaled_levels(levels)
@@ -118,10 +126,16 @@
         down[z, TILE:, :] = second
         return carry
 
-    lax.fori_loop(0, NZ, body, 0, unroll=2)
-
-
-def prepare(levels_in, pr_in, pi_in, px_in, py_in, pz_in, mat_in, pr, pi, ep, trig, own, up, down,
+    lax.fori_loop(0, NZ, body, 0, unroll=4)
+    for copy in copies[ready:]:
+        copy.wait()
+    c, s = sincos(far[2])
+    zup[0], zup[1] = turned_back(c, s, far[0], far[1])
+    zdown[7] = material_gain(end_mat[0], values)
+    zup[7] = material_gain(end_mat[1], values)
+
+
+def prepare(levels_in, pr_in, pi_in, px_in, py_in, pz_in, mat_in, pr, pi, ep, trig, own,
             levels, px, py, pz, mat, sems):
     pairs = [(levels_in, levels), (mat_in, mat), (pz_in, pz), (px_in, px), (py_in, py), (pr_in, pr), (pi_in, pi)]
     copies = start_copies(pairs, sems)
@@ -144,18 +158,18 @@
         lax.fori_loop(0, NZ, angles, 0)
     copies[5].wait()
     copies[6].wait()
-    group = iota((NX, LANES), 1) // 8
-    for k, q in enumerate((pr, pi, px, py, pz, ep)):
-        acc = jnp.zeros((NX, LANES), F32)
-        for z in range(NZ):
-            acc = jnp.where(group == z, roll(q[z], 8 * z - 126, 1), acc)
-        own[k] = acc
-    up[0], up[1] = turned_back(trig[0, 14], trig[1, 14], pr[14], pi[14])
-    down[0] = pr[1]
-    down[1] = pi[1]
-    for k, q in enumerate((pr, pi, px, py, pz, ep)):
-        up[2 + k] = q[15]
-        down[2 + k] = q[0]
+    group = iota((TILE, LANES), 1) // 8
+
+    def columns(t, carry):
+        rows = pl.ds(pl.multiple_of(t * TILE, TILE), TILE)
+        for k, q in enumerate((pr, pi, px, py, pz, ep)):
+            acc = roll(q[0, rows, :], -126, 1)
+            for z in range(1, NZ):
+                acc = jnp.where(group == z, roll(q[z, rows, :], 8 * z - 126, 1), acc)
+            own[k, rows, :] = acc
+        return carry
+
+    lax.fori_loop(0, NX // TILE, columns, 0)
 
 
 def pack_y(own_in, lo, hi, halo, own, up, down):
@@ -222,13 +236,13 @@
     if above is not None:
         t = turned(cz, sz, *above)
         sum_r, sum_i = sum_r + t[0], sum_i + t[1]
-    fr, fi = r, i
     wr, wi = turned_back(cy, sy, r, i)
+    fr, fi, wr, wi = roll(r, -1, 1), roll(i, -1, 1), roll(wr, 1, 1), roll(wi, 1, 1)
     if edge is not None:
-        fr, fi = jnp.where(lane == 0, edge[0], r), jnp.where(lane == 0, edge[1], i)
-        wr, wi = jnp.where(lane == 127, edge[0], wr), jnp.where(lane == 127, edge[1], wi)
-    t = turned(cy, sy, roll(fr, -1, 1), roll(fi, -1, 1))
-    sum_r, sum_i = sum_r + t[0] + roll(wr, 1, 1), sum_i + t[1] + roll(wi, 1, 1)
+        fr, fi = jnp.where(lane == 127, edge[0], fr), jnp.where(lane == 127, edge[1], fi)
+        wr, wi = jnp.where(lane == 0, edge[0], wr), jnp.where(lane == 0, edge[1], wi)
+    t = turned(cy, sy, fr, fi)
+    sum_r, sum_i = sum_r + t[0] + wr, sum_i + t[1] + wi
     gain = gain - time_step * (r * r + i * i)
     return gain * r + time_step * sum_r, gain * i + time_step * sum_i
 
@@ -313,7 +327,7 @@
 
 
 def shift_of(group):
-    return (126 - 8 * group) % 128
+    return (125 - 8 * group) % 128
 
 
 def on(test):
@@ -332,24 +346,45 @@
 
 def edge_columns(slot, ntrig, r, i):
     wr, wi = turned_back(ntrig[4], ntrig[5], r, i)
-    return jnp.where(slot == 1, roll(wr, -5, 1), r), jnp.where(slot == 1, roll(wi, -5, 1), i)
-
-
-def analyse(z, r, i, trig_x, trig_y, columns, jx_column, lane, triangle, out, spot, gap):
+    return jnp.where(slot == 3, roll(wr, -3, 1), r), jnp.where(slot == 3, roll(wi, -3, 1), i)
+
+
+def masked_rows(v, keep_tile):
+    return jnp.concatenate([v[:NX], jnp.where(keep_tile > 0, v[NX:], 0.0)], axis=0)
+
+
+def analyse(z, r, i, trig_x, trig_y, columns, jx_column, lane, rows, out, spot):
     shift = shift_of(z)
-    t = turned(*trig_x, ahead_x(r), ahead_x(i))
-    jx = r * t[1] - i * t[0]
-    fr = jnp.where(lane == 0, roll_by(columns[0], shift), r)
-    fi = jnp.where(lane == 0, roll_by(columns[1], shift), i)
-    t = turned(*trig_y, roll(fr, -1, 1), roll(fi, -1, 1))
+    own_r, own_i = r[:NX], i[:NX]
+    t = turned(trig_x[0][:NX], trig_x[1][:NX], ahead_x(r)[:NX], ahead_x(i)[:NX])
+    jx = own_r * t[1] - own_i * t[0]
+    last = lane == 127
+    fr = jnp.where(last, roll_by(columns[0], shift), roll(r, -1, 1))
+    fi = jnp.where(last, roll_by(columns[1], shift), roll(i, -1, 1))
+    t = turned(*trig_y, fr, fi)
     jy = r * t[1] - i * t[0]
-    jx_next = roll(jnp.where(lane == 0, roll_by(jx_column, shift), jx), -1, 1)
-    circulation = (jx + ahead_x(jy) - jx_next - jy)[:NX]
-    sums = jnp.dot(jx[:NX], triangle, precision=lax.Precision.HIGHEST, preferred_element_type=F32)
+    jx_next = jnp.where(last[:NX], roll_by(jx_column[:NX], shift), roll(jx, -1, 1))
+    circulation = jx + ahead_x(jy)[:NX] - jx_next - jy[:NX]
+    rows[pl.ds(spot * NX, NX), :] = jx
     for j in range(NX // TILE):
         away = (j + out.shape[0] - lax.axis_index("gy")) % out.shape[0]
         out[away, spot] = circulation[j * TILE:(j + 1) * TILE]
-        out[away, spot + gap] = sums[j * TILE:(j + 1) * TILE]
+
+
+def prefix(rows, out, spots, gap):
+    triangle = triangle_of().astype(jnp.bfloat16)
+    v = rows[spots.start * NX:spots.stop * NX, :]
+    a = v.astype(jnp.bfloat16)
+    v = v - a.astype(F32)
+    b = v.astype(jnp.bfloat16)
+    c = (v - b.astype(F32)).astype(jnp.bfloat16)
+    sums = jnp.dot(jnp.concatenate([c, b, a], axis=0), triangle, preferred_element_type=F32)
+    n = a.shape[0]
+    sums = sums[:n] + sums[n:2 * n] + sums[2 * n:]
+    for k, spot in enumerate(spots):
+        for j in range(NX // TILE):
+            away = (j + out.shape[0] - lax.axis_index("gy")) % out.shape[0]
+            out[away, gap + spot] = sums[k * NX + j * TILE:k * NX + (j + 1) * TILE]
 
 
 def roll_by(v, shift):
@@ -361,10 +396,11 @@
 
 
 def interior(pr_in, pi_in, ep, trig, halo, trig_halo, strip, ntrig, cr, ci, final_r, final_i, out,
-             er, ei, nr, ni, jx_edge):
+             er, ei, nr, ni, jx_edge, rows):
     lane = iota((RX, LANES), 1)
     slot = lane % 8
     keep_x, keep_xy = inside_masks()
+    keep_tile = keep_x[NX:]
     zero = jnp.zeros((RX, LANES), F32)
     for n, k in enumerate((PZ, PX, PY)):
         ntrig[2 * n], ntrig[2 * n + 1] = sincos(strip[k])
@@ -374,13 +410,11 @@
     def fix(z, carry):
         shift = shift_of(z)
         xr, xi = roll_by(er[...], shift), roll_by(ei[...], shift)
-        cy, sy = angles_at(trig, trig_halo, 4, z), angles_at(trig, trig_halo, 5, z)
-        hr, hi = turned(cy, sy, roll(xr, -1, 1), roll(xi, -1, 1))
-        lr, li = roll(xr, 1, 1), roll(xi, 1, 1)
-        r = pr_in[z] + time_step * jnp.where(lane == 127, hr, jnp.where(lane == 0, lr, zero))
-        i = pi_in[z] + time_step * jnp.where(lane == 127, hi, jnp.where(lane == 0, li, zero))
-        cr[z] = jnp.where(keep_x > 0, r, zero)
-        ci[z] = jnp.where(keep_x > 0, i, zero)
+        cy = jnp.where(lane == 127, angles_at(trig, trig_halo, 4, z), jnp.where(lane == 0, 1.0, 0.0)) * time_step
+        sy = jnp.where(lane == 127, angles_at(trig, trig_halo, 5, z), 0.0) * time_step
+        hr, hi = turned(cy, sy, xr, xi)
+        cr[z] = masked_rows(pr_in[z] + hr, keep_tile)
+        ci[z] = masked_rows(pi_in[z] + hi, keep_tile)
         return carry
 
     for z in range(NZ):
@@ -399,36 +433,36 @@
     ni[...] = i
     t = turned(ntrig[2], ntrig[3], ahead_x(r), ahead_x(i))
     jx_edge[...] = r * t[1] - i * t[0]
-    triangle = triangle_of()
 
     def second(z, carry):
         last_layer(z, (cr[z], ci[z]), (cr[z + 1], ci[z + 1]), (cr[z - 1], ci[z - 1]), ep, trig, halo, trig_halo,
-                   (er[...], ei[...]), (nr[...], ni[...]), jx_edge[...], keep_x, lane, triangle,
-                   final_r, final_i, out, None, z - 2, NZ - 4)
+                   (er[...], ei[...]), (nr[...], ni[...]), jx_edge[...], keep_x, lane, rows,
+                   final_r, final_i, out, None, z - 2)
         return carry
 
     for z in range(2, NZ - 2):
         second(z, 0)
+        if z % 4 == 1:
+            prefix(rows, out, range(z - 5, z - 1), NZ - 4)
 
 
 def last_layer(z, centre, above, below, ep, trig, halo, trig_halo, edges, columns, jx_column, keep_x, lane,
-               triangle, final_r, final_i, out, below_turned, spot, gap):
+               rows, final_r, final_i, out, below_turned, spot):
     t = [angles_at(trig, trig_halo, n, z) for n in range(6)]
     if below_turned is None:
         below_turned = turned_back(angles_at(trig, trig_halo, 0, z - 1), angles_at(trig, trig_halo, 1, z - 1), *below)
     shift = shift_of(z)
     edge = roll_by(edges[0], shift), roll_by(edges[1], shift)
     r, i = advance(centre, above, below_turned, t, edge, tall(ep, halo.at[EP], z), lane)
-    zero = jnp.zeros((RX, LANES), F32)
-    r = jnp.where(keep_x > 0, r, zero)
-    i = jnp.where(keep_x > 0, i, zero)
-    final_r[z] = r[:NX]
-    final_i[z] = i[:NX]
-    analyse(z, r, i, t[2:4], t[4:6], columns, jx_column, lane, triangle, out, spot, gap)
-
-
-def boundary(pr, pi, ep, trig, halo, trig_halo, strip, ntrig0, cr, ci, some_r, some_i, middle_out,
-             zlo, zhi, elo, ehi, final_r, final_i, out, ntrig1):
+    r = masked_rows(r, keep_x[NX:])
+    i = masked_rows(i, keep_x[NX:])
+    final_r[spot] = r[:NX]
+    final_i[spot] = i[:NX]
+    analyse(z, r, i, t[2:4], t[4:6], columns, jx_column, lane, rows, out, spot)
+
+
+def boundary(pr, pi, ep, trig, halo, trig_halo, strip, ntrig0, cr, ci, middle_out,
+             zlo, zhi, elo, ehi, final_r, final_i, out, ntrig1, rows):
     lane = iota((RX, LANES), 1)
     slot = lane % 8
     group = lane // 8
@@ -439,8 +473,6 @@
     zero = jnp.zeros((RX, LANES), F32)
     for away in range(out.shape[0]):
         out[away, 8:] = middle_out[away]
-    final_r[2:NZ - 2] = some_r[2:NZ - 2]
-    final_i[2:NZ - 2] = some_i[2:NZ - 2]
     lo8 = jnp.concatenate([elo[8 + t] for t in range(RX // TILE)], axis=0)
     hi8 = jnp.concatenate([ehi[8 + t] for t in range(RX // TILE)], axis=0)
 
@@ -509,10 +541,9 @@
     w = turned_back(t_lo[0], t_lo[1], *inner)
     first = masked(keep_x > 0, (cr[0] + time_step * w[0], ci[0] + time_step * w[1]))
     below = turned_back(t_lo[0], t_lo[1], *v)
-    triangle = triangle_of()
-    common = (ep, trig, halo, trig_halo, edges, columns, jx_column, keep_x, lane, triangle, final_r, final_i, out)
-    last_layer(0, first, (cr[1], ci[1]), None, *common, below, 0, 4)
-    last_layer(1, (cr[1], ci[1]), (cr[2], ci[2]), first, *common, None, 1, 4)
+    common = (ep, trig, halo, trig_halo, edges, columns, jx_column, keep_x, lane, rows, final_r, final_i, out)
+    last_layer(0, first, (cr[1], ci[1]), None, *common, below, 0)
+    last_layer(1, (cr[1], ci[1]), (cr[2], ci[2]), first, *common, None, 1)
     t_hi = angles(zhi, ehi)
     outer = masked(ok_hi, (got(zhi, ehi, 0), got(zhi, ehi, 1)))
     inner = masked(ok_hi, (got(zhi, ehi, 2), got(zhi, ehi, 3)))
@@ -521,8 +552,18 @@
     v = masked(ok_hi & (keep_x > 0), advance(inner, outer, below, t_hi, edge, got(zhi, ehi, 2 + EP), lane))
     w = turned(at(15, 0), at(15, 1), *inner)
     final = masked(keep_x > 0, (cr[15] + time_step * w[0], ci[15] + time_step * w[1]))
-    last_layer(14, (cr[14], ci[14]), final, (cr[13], ci[13]), *common, None, 2, 4)
-    last_layer(15, final, v, (cr[14], ci[14]), *common, None, 3, 4)
+    last_layer(14, (cr[14], ci[14]), final, (cr[13], ci[13]), *common, None, 2)
+    last_layer(15, final, v, (cr[14], ci[14]), *common, None, 3)
+    prefix(rows, out, range(4), 4)
+
+
+def store(some_r, some_i, ends_r, ends_i, final_r, final_i, sems):
+    pairs = []
+    for some, ends, final in ((some_r, ends_r, final_r), (some_i, ends_i, final_i)):
+        pairs += [(some, final.at[pl.ds(2, NZ - 4)]), (ends.at[pl.ds(0, 2)], final.at[pl.ds(0, 2)]),
+                  (ends.at[pl.ds(2, 2)], final.at[pl.ds(NZ - 2, 2)])]
+    for copy in start_copies(pairs, sems):
+        copy.wait()
 
 
 ENDS = (0, 1, NZ - 2, NZ - 1)
@@ -600,15 +641,17 @@
     edge = spec(NZ, TILE, LANES)
     block, tall_block, strip_like = spec(NZ, NX, NY), spec(NZ, RX, LANES), spec(RX, LANES)
     scratch = lambda s, dtype=F32: pltpu.VMEM(s.shape, dtype)
-    up, down = call(pack_x, (edge, spec(NZ, 2 * TILE, LANES)), *raw, hbm=7, scratch=[
+    layers = spec(8, NX, NY)
+    up, down, zup, zdown = call(pack_first, (edge, spec(NZ, 2 * TILE, LANES), layers, layers), *raw, hbm=7, scratch=[
         pltpu.SMEM((LEVELS,), F32), pltpu.VMEM((5, NZ, TILE, LANES), F32), pltpu.VMEM((5, NZ, TILE, LANES), F32),
-        scratch(edge, jnp.int32), scratch(edge, jnp.int32), pltpu.SemaphoreType.DMA((13,))])
+        scratch(edge, jnp.int32), scratch(edge, jnp.int32), pltpu.VMEM((3, NX, NY), F32),
+        pltpu.VMEM((2, NX, NY), jnp.int32), pltpu.SemaphoreType.DMA((30,))])
     lo, hi = exchange(up, down, "gx")
-    pr, pi, ep, trig, own, zup, zdown = call(
-        prepare, (block, block, block, spec(6, NZ, NX, NY), spec(6, NX, LANES), spec(8, NX, NY), spec(8, NX, NY)),
+    zlo, zhi = exchange(zup, zdown, "gz")
+    pr, pi, ep, trig, own = call(
+        prepare, (block, block, block, spec(6, NZ, NX, NY), spec(6, NX, LANES)),
         *raw, hbm=7, scratch=[pltpu.SMEM((LEVELS,), F32), scratch(block), scratch(block), scratch(block),
                               scratch(block, jnp.int32), pltpu.SemaphoreType.DMA((7,))])
-    zlo, zhi = exchange(zup, zdown, "gz")
     halo, own, up, down = call(
         pack_y, (spec(6, NZ, TILE, LANES), spec(6, RX, LANES), strip_like, spec(2, RX, LANES)), own, lo, hi)
     lo, hi = exchange(up, down, "gy")
@@ -616,14 +659,20 @@
     strip, up, down = call(pack_edges, (spec(6, RX, LANES), spec(17, TILE, LANES), spec(17, TILE, LANES)),
                            trig_halo, halo, own, lo, hi)
     elo, ehi = exchange(up, down, "gz")
+    middle_block, ends_block = spec(NZ - 4, NX, NY), spec(4, NX, NY)
     ntrig, cr, ci, some_r, some_i, out = call(
-        interior, (spec(6, RX, LANES), tall_block, tall_block, block, block, spec(parts, 2 * NZ - 8, TILE, LANES)),
-        br, bi, ep, trig, halo, trig_halo, strip, scratch=[scratch(strip_like)] * 5)
+        interior, (spec(6, RX, LANES), tall_block, tall_block, middle_block, middle_block,
+                   spec(parts, 2 * NZ - 8, TILE, LANES)),
+        br, bi, ep, trig, halo, trig_halo, strip,
+        scratch=[scratch(strip_like)] * 5 + [pltpu.VMEM(((NZ - 4) * NX, NY), F32)])
     got = [ahead(out[k], k) for k in EARLY]
-    final_r, final_i, out = call(
-        boundary, (block, block, spec(parts, 2 * NZ, TILE, LANES)), pr, pi, ep, trig, halo, trig_halo, strip, ntrig, cr, ci,
-        some_r, some_i, out, zlo, zhi, elo, ehi, scratch=[pltpu.VMEM((6, RX, LANES), F32)])
+    ends_r, ends_i, out = call(
+        boundary, (ends_block, ends_block, spec(parts, 2 * NZ, TILE, LANES)), pr, pi, ep, trig, halo, trig_halo, strip,
+        ntrig, cr, ci, out, zlo, zhi, elo, ehi,
+        scratch=[pltpu.VMEM((6, RX, LANES), F32), pltpu.VMEM((4 * NX, NY), F32)])
     late = {k: ahead(out[k, :8] if k in EARLY else out[k], k) for k in LATE}
+    final_r, final_i = call(store, (block, block), some_r, some_i, ends_r, ends_i, hbm_out=True,
+                            scratch=[pltpu.SemaphoreType.DMA((6,))])
     got += [out[0]] + [late[k] for k in range(1, parts)]
     slab = spec(NZ, TILE, parts * LANES)
     circulation, flux = call(finish, (slab, slab), *got, hbm_out=True, scratch=[

time: 65.2 us -> 62.1 us (0.952)
  the two profiles are of different devices: /device:TPU:8 before, /device:TPU:1 now
where the time goes in v4:
time: 62.1 us; the launch traced here: 61.9 us
  starting transfers between devices  26.5 us (43%)
  waiting for transfers between devices  18.6 us (30%)
  Pallas kernels  16 us (26%)
  between operations  0.79 us (1%)
    pallas_call x9, Pallas kernels, call(): pl.pallas_call(body, out_shape=outs, in_specs=memory, scratch_shapes=list...  16 us
    ppermute x4, starting transfers between devices, exchange(): hi = lax.ppermute(down, axis, [(b, a) for a, b in forward])  15.4 us
    ppermute x7, waiting for transfers between devices, ahead(): return lax.ppermute(value, 'gy', [(i, (i + k) % size) for i in range(size)])  11 us
    ppermute x7, starting transfers between devices, ahead(): return lax.ppermute(value, 'gy', [(i, (i + k) % size) for i in range(size)])  9.08 us
    ppermute x4, waiting for transfers between devices, exchange(): lo = lax.ppermute(up, axis, forward)  7.5 us
    ppermute x4, starting transfers between devices, exchange(): lo = lax.ppermute(up, axis, forward)  1.94 us
  transfers between devices with their start and end apart: 15, of which 3 were waited for; matrix products, arithmetic and copies ran while one was open for 0% of the time, Pallas kernels for 18%

profile of v4, /device:TPU:1, one launch (start us, length us, event | category | flops | bytes accessed | tf_op | source)
XLA Modules:
  0.0 61.9 jit_solution(13278434925240013219)
XLA Ops:
  0.6 1.8 %shard_map.103 = (f32[16,8,128]{2,1,0:T(8,128)S(1)}, f32[16,16,128]{2,1,0:T(8,128)S(1)}, f32[8,64,128]{2,1,0:T(8,128)S(1)}, f32[8,64,128]{2,1,0:T(8,128)S(1)}) custom-call(f32[8]{0:T(128)} %levels_in.3, f32[16,64,128]{2,1,0:T(8,128)} %pr.1, f32[16,64,128]{2,1,0:T(8,128)} %pi.1, f32[16,64,128]{2,1,0:T(8,128)} %px.1, f32[16,64,128]{2,1,0:T(8,128)} %py.1, ...), custom_call_target="tpu_custom_call" | custom-call | tf_op jit(solution)/shard_map/pallas_call | solution.py:617
  2.4 6.9 %collective-permute-start.1 = (f32[16,16,128]{2,1,0:T(8,128)S(1)}, f32[16,16,128]{2,1,0:T(8,128)S(1)}, u32[]{:S(2)}, u32[]{:S(2)}) collective-permute-start(f32[16,16,128]{2,1,0:T(8,128)S(1)} %get-tuple-element.42), channel_id=1, source_target_pairs={{64,0},{128,64},{192,128},{0,192},{65,1},{129,65},{193,129},{1,193... | collective-permute-start | bytes 393224 | tf_op jit(solution)/shard_map/ppermute | solution.py:628
  9.3 0.7 %collective-permute-start.4 = (f32[8,64,128]{2,1,0:T(8,128)S(1)}, f32[8,64,128]{2,1,0:T(8,128)S(1)}, u32[]{:S(2)}, u32[]{:S(2)}) collective-permute-start(f32[8,64,128]{2,1,0:T(8,128)S(1)} %get-tuple-element.57), channel_id=1, source_target_pairs={{0,1},{1,2},{2,3},{3,4},{4,5},{5,6},{6,7},{7,0},{8,9},{9,10},{10,1... | collective-permute-start | bytes 786440 | tf_op jit(solution)/shard_map/ppermute | solution.py:627
  10.0 2.8 %collective-permute-start.5 = (f32[8,64,128]{2,1,0:T(8,128)S(1)}, f32[8,64,128]{2,1,0:T(8,128)S(1)}, u32[]{:S(2)}, u32[]{:S(2)}) collective-permute-start(f32[8,64,128]{2,1,0:T(8,128)S(1)} %get-tuple-element.58), channel_id=1, source_target_pairs={{1,0},{2,1},{3,2},{4,3},{5,4},{6,5},{7,6},{0,7},{9,8},{10,9},{11,1... | collective-permute-start | bytes 786440 | tf_op jit(solution)/shard_map/ppermute | solution.py:628
  12.9 4.4 %shard_map.102 = (f32[16,64,128]{2,1,0:T(8,128)S(1)}, f32[16,64,128]{2,1,0:T(8,128)S(1)}, f32[16,64,128]{2,1,0:T(8,128)S(1)}, f32[6,16,64,128]{3,2,1,0:T(8,128)S(1)}, f32[6,64,128]{2,1,0:T(8,128)S(1)}) custom-call(f32[8]{0:T(128)} %levels_in.3, f32[16,64,128]{2,1,0:T(8,128)} %pr.1, f32[16,64,128]{2,1,0:T(8,128)} %pi.1, f32[16,64,128]{2,1,0:T(8,128)} %px.1, ...), custom_call_target="tpu_custom_call" | custom-call | tf_op jit(solution)/shard_map/pallas_call | solution.py:617
  17.3 7.5 %collective-permute-done.lo = f32[16,8,128]{2,1,0:T(8,128)S(1)} collective-permute-done((f32[16,8,128]{2,1,0:T(8,128)S(1)}, f32[16,8,128]{2,1,0:T(8,128)S(1)}, u32[]{:S(2)}, u32[]{:S(2)}) %collective-permute-start) | collective-permute-done | bytes 65568 | tf_op jit(solution)/shard_map/ppermute | solution.py:627
  24.8 0.3 shard_map.104
  25.1 2.1 %collective-permute-start.3 = (f32[2,72,128]{2,1,0:T(8,128)S(1)}, f32[2,72,128]{2,1,0:T(8,128)S(1)}, u32[]{:S(2)}, u32[]{:S(2)}) collective-permute-start(f32[2,72,128]{2,1,0:T(8,128)S(1)} %get-tuple-element.49), channel_id=1, source_target_pairs={{8,0},{16,8},{24,16},{32,24},{40,32},{48,40},{56,48},{0,56},{9,1},... | collective-permute-start | bytes 221192 | tf_op jit(solution)/shard_map/ppermute | solution.py:628
  27.3 1.1 %collective-permute-start.2 = (f32[72,128]{1,0:T(8,128)S(1)}, f32[72,128]{1,0:T(8,128)S(1)}, u32[]{:S(2)}, u32[]{:S(2)}) collective-permute-start(f32[72,128]{1,0:T(8,128)S(1)} %get-tuple-element.48), channel_id=1, source_target_pairs={{0,8},{8,16},{16,24},{24,32},{32,40},{40,48},{48,56},{56,0},{1,9},... | collective-permute-start | bytes 110600 | tf_op jit(solution)/shard_map/ppermute | solution.py:627
  28.4 2.1 %shard_map.105 = (f32[6,16,8,128]{3,2,1,0:T(8,128)S(1)}, f32[16,72,128]{2,1,0:T(8,128)S(1)}, f32[16,72,128]{2,1,0:T(8,128)S(1)}) custom-call(f32[16,64,128]{2,1,0:T(8,128)S(1)} %get-tuple-element.36.pr, f32[16,64,128]{2,1,0:T(8,128)S(1)} %get-tuple-element.37.pi, f32[16,64,128]{2,1,0:T(8,128)S(1)} %get-tuple-element.38.ep, ...), custom_call_target="tpu_custom_call" | custom-call | tf_op jit(solution)/shard_map/pallas_call | solution.py:617
  30.5 0.4 shard_map.106
  30.9 0.1 collective-permute-start.6
  31.0 3.6 %collective-permute-start.7 = (f32[17,8,128]{2,1,0:T(8,128)S(1)}, f32[17,8,128]{2,1,0:T(8,128)S(1)}, u32[]{:S(2)}, u32[]{:S(2)}) collective-permute-start(f32[17,8,128]{2,1,0:T(8,128)S(1)} %get-tuple-element.60), channel_id=1, source_target_pairs={{1,0},{2,1},{3,2},{4,3},{5,4},{6,5},{7,6},{0,7},{9,8},{10,9},{11,1... | collective-permute-start | bytes 208904 | tf_op jit(solution)/shard_map/ppermute | solution.py:628
  34.6 3.0 %shard_map.107 = (f32[6,72,128]{2,1,0:T(8,128)S(1)}, f32[16,72,128]{2,1,0:T(8,128)S(1)}, f32[16,72,128]{2,1,0:T(8,128)S(1)}, f32[12,64,128]{2,1,0:T(8,128)S(1)},...) custom-call(f32[16,72,128]{2,1,0:T(8,128)S(1)} %get-tuple-element.44.pr_in, ...), custom_call_target="tpu_custom_call" | custom-call | tf_op jit(solution)/shard_map/pallas_call | solution.py:617
  37.7 1.8 %shard_map.108 = (f32[4,64,128]{2,1,0:T(8,128)S(1)}, f32[4,64,128]{2,1,0:T(8,128)S(1)}, f32[8,32,8,128]{3,2,1,0:T(8,128)S(1)}) custom-call(f32[16,64,128]{2,1,0:T(8,128)S(1)} %get-tuple-element.36.pr, f32[16,64,128]{2,1,0:T(8,128)S(1)} %get-tuple-element.37.pi, f32[16,64,128]{2,1,0:T(8,128)S(1)} %get-tuple-element.38.ep, ...), custom_call_target="tpu_custom_call" | custom-call | tf_op jit(solution)/shard_map/pallas_call | solution.py:617
  39.6 1.8 %collective-permute-start.8 = (f32[32,8,128]{2,1,0:T(8,128)S(1)}, f32[32,8,128]{2,1,0:T(8,128)S(1)}, u32[]{:S(2)}, u32[]{:S(2)}) collective-permute-start(f32[32,8,128]{2,1,0:T(8,128)S(1)} %get-tuple-element.74), channel_id=1, source_target_pairs={{0,8},{8,16},{16,24},{24,32},{32,40},{40,48},{48,56},{56,0},{1,9},... | collective-permute-start | bytes 393224 | tf_op jit(solution)/shard_map/ppermute | solution.py:634
  41.4 1.2 %collective-permute-start.9 = (f32[32,8,128]{2,1,0:T(8,128)S(1)}, f32[32,8,128]{2,1,0:T(8,128)S(1)}, u32[]{:S(2)}, u32[]{:S(2)}) collective-permute-start(f32[32,8,128]{2,1,0:T(8,128)S(1)} %get-tuple-element.73), channel_id=1, source_target_pairs={{0,16},{8,24},{16,32},{24,40},{32,48},{40,56},{48,0},{56,8},{1,17}... | collective-permute-start | bytes 393224 | tf_op jit(solution)/shard_map/ppermute | solution.py:634
  42.6 1.6 %collective-permute-start.10 = (f32[32,8,128]{2,1,0:T(8,128)S(1)}, f32[32,8,128]{2,1,0:T(8,128)S(1)}, u32[]{:S(2)}, u32[]{:S(2)}) collective-permute-start(f32[32,8,128]{2,1,0:T(8,128)S(1)} %get-tuple-element.72), channel_id=1, source_target_pairs={{0,24},{8,32},{16,40},{24,48},{32,56},{40,0},{48,8},{56,16},{1,25}... | collective-permute-start | bytes 393224 | tf_op jit(solution)/shard_map/ppermute | solution.py:634
  44.3 1.8 %collective-permute-start.11 = (f32[32,8,128]{2,1,0:T(8,128)S(1)}, f32[32,8,128]{2,1,0:T(8,128)S(1)}, u32[]{:S(2)}, u32[]{:S(2)}) collective-permute-start(f32[32,8,128]{2,1,0:T(8,128)S(1)} %get-tuple-element.71), channel_id=1, source_target_pairs={{0,32},{8,40},{16,48},{24,56},{32,0},{40,8},{48,16},{56,24},{1,33}... | collective-permute-start | bytes 393224 | tf_op jit(solution)/shard_map/ppermute | solution.py:634
  46.0 2.6 %collective-permute-start.12 = (f32[32,8,128]{2,1,0:T(8,128)S(1)}, f32[32,8,128]{2,1,0:T(8,128)S(1)}, u32[]{:S(2)}, u32[]{:S(2)}) collective-permute-start(f32[32,8,128]{2,1,0:T(8,128)S(1)} %get-tuple-element.70), channel_id=1, source_target_pairs={{0,40},{8,48},{16,56},{24,0},{32,8},{40,16},{48,24},{56,32},{1,41}... | collective-permute-start | bytes 393224 | tf_op jit(solution)/shard_map/ppermute | solution.py:634
  48.7 7.7 %collective-permute-done.9.refs_2_ = f32[32,8,128]{2,1,0:T(8,128)S(1)} collective-permute-done((f32[32,8,128]{2,1,0:T(8,128)S(1)}, f32[32,8,128]{2,1,0:T(8,128)S(1)}, u32[]{:S(2)}, u32[]{:S(2)}) %collective-permute-start.9) | collective-permute-done | bytes 131104 | tf_op jit(solution)/shard_map/ppermute | solution.py:634
  56.4 1.0 %shard_map.109 = (f32[16,64,128]{2,1,0:T(8,128)}, f32[16,64,128]{2,1,0:T(8,128)}) custom-call(f32[12,64,128]{2,1,0:T(8,128)S(1)} %get-tuple-element.51.some_r, f32[12,64,128]{2,1,0:T(8,128)S(1)} %get-tuple-element.52.some_i, f32[4,64,128]{2,1,0:T(8,128)S(1)} %get-tuple-element.61.ends_r, f32[4,64,128]{2,1,0:T(8,128)S(1)} %get-tuple-element.62.ends_i), custom_call_target="tpu_custom_call" | custom-call | tf_op jit(solution)/shard_map/pallas_call | solution.py:617
  57.4 3.3 %collective-permute-done.14.refs_7_ = f32[32,8,128]{2,1,0:T(8,128)S(1)} collective-permute-done((f32[32,8,128]{2,1,0:T(8,128)S(1)}, f32[32,8,128]{2,1,0:T(8,128)S(1)}, u32[]{:S(2)}, u32[]{:S(2)}) %collective-permute-start.14) | collective-permute-done | bytes 131104 | tf_op jit(solution)/shard_map/ppermute | solution.py:634
  60.8 1.2 %shard_map.110 = (f32[16,8,1024]{2,1,0:T(8,128)}, f32[16,8,1024]{2,1,0:T(8,128)}) custom-call(f32[32,8,128]{2,1,0:T(8,128)S(1)} %get-tuple-element.75.refs_0_, f32[32,8,128]{2,1,0:T(8,128)S(1)} %collective-permute-done.8.refs_1_, f32[32,8,128]{2,1,0:T(8,128)S(1)} %collective-permute-done.9.refs_2_, f32[32,8,128]{2,1,0:T(8,128)S(1)} %collective-permute-done.10.refs_3_, ...), custom_call_target="tpu_custom_call" | custom-call | tf_op jit(solution)/shard_map/pallas_call | solution.py:617
  (16 shorter events, 0.1 us)
Async XLA Ops:
  2.4 22.4 %collective-permute-start.1 = (f32[16,16,128]{2,1,0:T(8,128)S(1)}, f32[16,16,128]{2,1,0:T(8,128)S(1)}, u32[]{:S(2)}, u32[]{:S(2)}) collective-permute-start(f32[16,16,128]{2,1,0:T(8,128)S(1)} %get-tuple-element.42), channel_id=1, source_target_pairs={{64,0},{128,64},{192,128},{0,192},{65,1},{129,65},{193,129},{1,193... | collective-permute-start | bytes 393224 | tf_op jit(solution)/shard_map/ppermute | solution.py:628
  9.3 28.3 %collective-permute-start.4 = (f32[8,64,128]{2,1,0:T(8,128)S(1)}, f32[8,64,128]{2,1,0:T(8,128)S(1)}, u32[]{:S(2)}, u32[]{:S(2)}) collective-permute-start(f32[8,64,128]{2,1,0:T(8,128)S(1)} %get-tuple-element.57), channel_id=1, source_target_pairs={{0,1},{1,2},{2,3},{3,4},{4,5},{5,6},{6,7},{7,0},{8,9},{9,10},{10,1... | collective-permute-start | bytes 786440 | tf_op jit(solution)/shard_map/ppermute | solution.py:627
  10.0 27.6 %collective-permute-start.5 = (f32[8,64,128]{2,1,0:T(8,128)S(1)}, f32[8,64,128]{2,1,0:T(8,128)S(1)}, u32[]{:S(2)}, u32[]{:S(2)}) collective-permute-start(f32[8,64,128]{2,1,0:T(8,128)S(1)} %get-tuple-element.58), channel_id=1, source_target_pairs={{1,0},{2,1},{3,2},{4,3},{5,4},{6,5},{7,6},{0,7},{9,8},{10,9},{11,1... | collective-permute-start | bytes 786440 | tf_op jit(solution)/shard_map/ppermute | solution.py:628
  12.9 11.9 %collective-permute-start = (f32[16,8,128]{2,1,0:T(8,128)S(1)}, f32[16,8,128]{2,1,0:T(8,128)S(1)}, u32[]{:S(2)}, u32[]{:S(2)}) collective-permute-start(f32[16,8,128]{2,1,0:T(8,128)S(1)} %get-tuple-element.41), channel_id=1, source_target_pairs={{0,64},{64,128},{128,192},{192,0},{1,65},{65,129},{129,193},{193,1... | collective-permute-start | bytes 196616 | tf_op jit(solution)/shard_map/ppermute | solution.py:627
  25.1 5.3 %collective-permute-start.3 = (f32[2,72,128]{2,1,0:T(8,128)S(1)}, f32[2,72,128]{2,1,0:T(8,128)S(1)}, u32[]{:S(2)}, u32[]{:S(2)}) collective-permute-start(f32[2,72,128]{2,1,0:T(8,128)S(1)} %get-tuple-element.49), channel_id=1, source_target_pairs={{8,0},{16,8},{24,16},{32,24},{40,32},{48,40},{56,48},{0,56},{9,1},... | collective-permute-start | bytes 221192 | tf_op jit(solution)/shard_map/ppermute | solution.py:628
  27.3 3.2 %collective-permute-start.2 = (f32[72,128]{1,0:T(8,128)S(1)}, f32[72,128]{1,0:T(8,128)S(1)}, u32[]{:S(2)}, u32[]{:S(2)}) collective-permute-start(f32[72,128]{1,0:T(8,128)S(1)} %get-tuple-element.48), channel_id=1, source_target_pairs={{0,8},{8,16},{16,24},{24,32},{32,40},{40,48},{48,56},{56,0},{1,9},... | collective-permute-start | bytes 110600 | tf_op jit(solution)/shard_map/ppermute | solution.py:627
  30.9 6.7 %collective-permute-start.6 = (f32[17,8,128]{2,1,0:T(8,128)S(1)}, f32[17,8,128]{2,1,0:T(8,128)S(1)}, u32[]{:S(2)}, u32[]{:S(2)}) collective-permute-start(f32[17,8,128]{2,1,0:T(8,128)S(1)} %get-tuple-element.59), channel_id=1, source_target_pairs={{0,1},{1,2},{2,3},{3,4},{4,5},{5,6},{6,7},{7,0},{8,9},{9,10},{10,1... | collective-permute-start | bytes 208904 | tf_op jit(solution)/shard_map/ppermute | solution.py:627
  31.0 6.7 %collective-permute-start.7 = (f32[17,8,128]{2,1,0:T(8,128)S(1)}, f32[17,8,128]{2,1,0:T(8,128)S(1)}, u32[]{:S(2)}, u32[]{:S(2)}) collective-permute-start(f32[17,8,128]{2,1,0:T(8,128)S(1)} %get-tuple-element.60), channel_id=1, source_target_pairs={{1,0},{2,1},{3,2},{4,3},{5,4},{6,5},{7,6},{0,7},{9,8},{10,9},{11,1... | collective-permute-start | bytes 208904 | tf_op jit(solution)/shard_map/ppermute | solution.py:628
  39.6 9.1 %collective-permute-start.8 = (f32[32,8,128]{2,1,0:T(8,128)S(1)}, f32[32,8,128]{2,1,0:T(8,128)S(1)}, u32[]{:S(2)}, u32[]{:S(2)}) collective-permute-start(f32[32,8,128]{2,1,0:T(8,128)S(1)} %get-tuple-element.74), channel_id=1, source_target_pairs={{0,8},{8,16},{16,24},{24,32},{32,40},{40,48},{48,56},{56,0},{1,9},... | collective-permute-start | bytes 393224 | tf_op jit(solution)/shard_map/ppermute | solution.py:634
  41.4 14.9 %collective-permute-start.9 = (f32[32,8,128]{2,1,0:T(8,128)S(1)}, f32[32,8,128]{2,1,0:T(8,128)S(1)}, u32[]{:S(2)}, u32[]{:S(2)}) collective-permute-start(f32[32,8,128]{2,1,0:T(8,128)S(1)} %get-tuple-element.73), channel_id=1, source_target_pairs={{0,16},{8,24},{16,32},{24,40},{32,48},{40,56},{48,0},{56,8},{1,17}... | collective-permute-start | bytes 393224 | tf_op jit(solution)/shard_map/ppermute | solution.py:634
  42.6 14.7 %collective-permute-start.10 = (f32[32,8,128]{2,1,0:T(8,128)S(1)}, f32[32,8,128]{2,1,0:T(8,128)S(1)}, u32[]{:S(2)}, u32[]{:S(2)}) collective-permute-start(f32[32,8,128]{2,1,0:T(8,128)S(1)} %get-tuple-element.72), channel_id=1, source_target_pairs={{0,24},{8,32},{16,40},{24,48},{32,56},{40,0},{48,8},{56,16},{1,25}... | collective-permute-start | bytes 393224 | tf_op jit(solution)/shard_map/ppermute | solution.py:634
  44.3 13.1 %collective-permute-start.11 = (f32[32,8,128]{2,1,0:T(8,128)S(1)}, f32[32,8,128]{2,1,0:T(8,128)S(1)}, u32[]{:S(2)}, u32[]{:S(2)}) collective-permute-start(f32[32,8,128]{2,1,0:T(8,128)S(1)} %get-tuple-element.71), channel_id=1, source_target_pairs={{0,32},{8,40},{16,48},{24,56},{32,0},{40,8},{48,16},{56,24},{1,33}... | collective-permute-start | bytes 393224 | tf_op jit(solution)/shard_map/ppermute | solution.py:634
  46.0 11.4 %collective-permute-start.12 = (f32[32,8,128]{2,1,0:T(8,128)S(1)}, f32[32,8,128]{2,1,0:T(8,128)S(1)}, u32[]{:S(2)}, u32[]{:S(2)}) collective-permute-start(f32[32,8,128]{2,1,0:T(8,128)S(1)} %get-tuple-element.70), channel_id=1, source_target_pairs={{0,40},{8,48},{16,56},{24,0},{32,8},{40,16},{48,24},{56,32},{1,41}... | collective-permute-start | bytes 393224 | tf_op jit(solution)/shard_map/ppermute | solution.py:634
  48.7 8.7 %collective-permute-start.13 = (f32[32,8,128]{2,1,0:T(8,128)S(1)}, f32[32,8,128]{2,1,0:T(8,128)S(1)}, u32[]{:S(2)}, u32[]{:S(2)}) collective-permute-start(f32[32,8,128]{2,1,0:T(8,128)S(1)} %get-tuple-element.69), channel_id=1, source_target_pairs={{0,48},{8,56},{16,0},{24,8},{32,16},{40,24},{48,32},{56,40},{1,49}... | collective-permute-start | bytes 393224 | tf_op jit(solution)/shard_map/ppermute | solution.py:634
  56.4 4.4 %collective-permute-start.14 = (f32[32,8,128]{2,1,0:T(8,128)S(1)}, f32[32,8,128]{2,1,0:T(8,128)S(1)}, u32[]{:S(2)}, u32[]{:S(2)}) collective-permute-start(f32[32,8,128]{2,1,0:T(8,128)S(1)} %get-tuple-element.68), channel_id=1, source_target_pairs={{0,56},{8,0},{16,8},{24,16},{32,24},{40,32},{48,40},{56,48},{1,57}... | collective-permute-start | bytes 393224 | tf_op jit(solution)/shard_map/ppermute | solution.py:634

commit v5 on v4

--- a/solution.py
+++ b/solution.py
@@ -60,28 +60,6 @@
     return c * r + s * i, c * i - s * r
 
 
-def row_up(a, row):
-    pr, pi, px, py, pz, ep = a
-    c, s = sincos(px)
-    wr, wi = turned_back(c, s, pr, pi)
-    last = row == 6
-    pr = jnp.where(last, wr, pr)
-    pi = jnp.where(last, wi, pi)
-    out = roll(pr, 2, 0)
-    out = jnp.where(row >= 2, roll(pi, 4, 0), out)
-    out = jnp.where(row == 4, roll(px, 5, 0), out)
-    out = jnp.where(row == 5, roll(py, 6, 0), out)
-    out = jnp.where(row == 6, roll(pz, 7, 0), out)
-    return jnp.where(row == 7, ep, out)
-
-
-def row_down(a, row):
-    pr, pi, px, py, pz, ep = a
-    first = jnp.where(row < 3, pr, jnp.where(row < 6, roll(pi, 3, 0), roll(px, 6, 0)))
-    second = jnp.where(row < 2, py, jnp.where(row < 4, roll(pz, 2, 0), roll(ep, 4, 0)))
-    return first, second
-
-
 def scaled_levels(levels):
     return [1.0 + time_step * (levels[k] - 6.0) for k in range(LEVELS)]
 
@@ -101,98 +79,70 @@
 
 
 def pack_first(levels_in, pr, pi, px, py, pz, mat, up, down, zup, zdown,
-               levels, top, low, top_mat, low_mat, far, end_mat, sems):
+               levels, outer, row_mat, far, sems):
     fields = (pr, pi, px, py, pz)
     pairs = [(levels_in, levels)]
-    pairs += [(q.at[:, pl.ds(NX - TILE, TILE), :], top.at[k]) for k, q in enumerate(fields)]
-    pairs += [(q.at[:, pl.ds(0, TILE), :], low.at[k]) for k, q in enumerate(fields)]
-    pairs += [(mat.at[:, pl.ds(NX - TILE, TILE), :], top_mat), (mat.at[:, pl.ds(0, TILE), :], low_mat)]
-    ready = len(pairs)
-    pairs += [(q.at[14], far.at[k]) for k, q in enumerate((pr, pi, pz))]
-    pairs += [(mat.at[0], end_mat.at[0]), (mat.at[15], end_mat.at[1])]
-    pairs += [(q.at[15], zup.at[2 + k]) for k, q in enumerate(fields)]
-    pairs += [(q.at[0], zdown.at[2 + k]) for k, q in enumerate(fields)]
-    pairs += [(pr.at[1], zdown.at[0]), (pi.at[1], zdown.at[1])]
-    copies = start_copies(pairs, sems)
-    for copy in copies[:ready]:
+    pairs += [(q.at[:, NX - 2, :], outer.at[k]) for k, q in enumerate((pr, pi, px))]
+    pairs += [(mat.at[:, row, :], row_mat.at[k]) for k, row in enumerate((0, 1, NX - 1))]
+    pairs += [(q.at[:, NX - 1, :], up.at[2 + k]) for k, q in enumerate(fields)]
+    pairs += [(q.at[:, row, :], down.at[3 * k + row]) for k, q in enumerate((pr, pi)) for row in range(3)]
+    pairs += [(q.at[:, row, :], down.at[6 + 2 * k + row]) for k, q in enumerate((px, py, pz)) for row in range(2)]
+    pairs += [(q.at[NZ - 1], far.at[k]) for k, q in enumerate((pr, pi, pz))]
+    pairs += [(pr.at[0], zdown.at[0]), (pi.at[0], zdown.at[1])]
+    for copy in start_copies(pairs, sems):
         copy.wait()
-    row = iota((TILE, LANES), 0)
     values = scaled_levels(levels)
-
-    def body(z, carry):
-        up[z] = row_up([top[k, z] for k in range(5)] + [material_gain(top_mat[z], values)], row)
-        first, second = row_down([low[k, z] for k in range(5)] + [material_gain(low_mat[z], values)], row)
-        down[z, :TILE, :] = first
-        down[z, TILE:, :] = second
-        return carry
-
-    lax.fori_loop(0, NZ, body, 0, unroll=4)
-    for copy in copies[ready:]:
-        copy.wait()
+    c, s = sincos(outer[2])
+    up[0], up[1] = turned_back(c, s, outer[0], outer[1])
+    up[7] = material_gain(row_mat[2], values)
+    down[12] = material_gain(row_mat[0], values)
+    down[13] = material_gain(row_mat[1], values)
     c, s = sincos(far[2])
     zup[0], zup[1] = turned_back(c, s, far[0], far[1])
-    zdown[7] = material_gain(end_mat[0], values)
-    zup[7] = material_gain(end_mat[1], values)
-
-
-def prepare(levels_in, pr_in, pi_in, px_in, py_in, pz_in, mat_in, pr, pi, ep, trig, own,
-            levels, px, py, pz, mat, sems):
-    pairs = [(levels_in, levels), (mat_in, mat), (pz_in, pz), (px_in, px), (py_in, py), (pr_in, pr), (pi_in, pi)]
-    copies = start_copies(pairs, sems)
-    copies[0].wait()
-    copies[1].wait()
+
+
+def columns(levels, pr, pi, px, py, pz, mat, own):
+    group = iota((TILE, LANES), 1) // 8
     values = scaled_levels(levels)
-
-    def gains(z, carry):
-        ep[z] = material_gain(mat[z], values)
-        return carry
-
-    lax.fori_loop(0, NZ, gains, 0)
-    for n, q in enumerate((pz, px, py)):
-        copies[2 + n].wait()
-
-        def angles(z, carry):
-            trig[2 * n, z], trig[2 * n + 1, z] = sincos(q[z])
-            return carry
-
-        lax.fori_loop(0, NZ, angles, 0)
-    copies[5].wait()
-    copies[6].wait()
-    group = iota((TILE, LANES), 1) // 8
-
-    def columns(t, carry):
-        rows = pl.ds(pl.multiple_of(t * TILE, TILE), TILE)
-        for k, q in enumerate((pr, pi, px, py, pz, ep)):
+    for k, q in enumerate((pr, pi, px, py, pz, mat)):
+        for t in range(NX // TILE):
+            rows = slice(t * TILE, (t + 1) * TILE)
             acc = roll(q[0, rows, :], -126, 1)
             for z in range(1, NZ):
                 acc = jnp.where(group == z, roll(q[z, rows, :], 8 * z - 126, 1), acc)
-            own[k, rows, :] = acc
+            own[k, rows, :] = material_gain(acc, values) if k == EP else acc
+
+
+def angles(levels, px, py, pz, mat, ep, trig):
+    values = scaled_levels(levels)
+
+    def body(z, carry):
+        ep[z] = material_gain(mat[z], values)
+        for n, q in enumerate((pz, px, py)):
+            trig[2 * n, z], trig[2 * n + 1, z] = sincos(q[z])
         return carry
 
-    lax.fori_loop(0, NX // TILE, columns, 0)
+    lax.fori_loop(0, NZ, body, 0)
 
 
 def pack_y(own_in, lo, hi, halo, own, up, down):
     row = iota((TILE, LANES), 0)
     gx = lax.axis_index("gx")
     keep = jnp.where(row < 4, jnp.where(gx < lax.axis_size("gx") - 1, 1, 0), jnp.where(gx > 0, 1, 0)) > 0
-    low_rows = row >= 6
-    last = row == 7
     group = iota((TILE, LANES), 1) // 8
     acc = [jnp.zeros((TILE, LANES), F32) for _ in range(6)]
+    zero = jnp.zeros((TILE, LANES), F32)
+
+    def rows_at(z, placed):
+        out = zero
+        for at, (ref, k) in placed.items():
+            out = jnp.where(row == at, jnp.broadcast_to(ref[k, z:z + 1, :], (TILE, LANES)), out)
+        return out
+
     for z in range(NZ):
-        l = lo[z]
-        a = hi[z, :TILE, :]
-        b = hi[z, TILE:, :]
-        zero = jnp.zeros_like(l)
-        tiles = (
-            jnp.where(keep, jnp.where(low_rows, roll(l, 6, 0), a), zero),
-            jnp.where(keep, jnp.where(low_rows, roll(l, 4, 0), roll(a, -3, 0)), zero),
-            jnp.where(last, roll(l, 3, 0), jnp.where(row < 2, roll(a, -6, 0), zero)),
-            jnp.where(last, roll(l, 2, 0), jnp.where(row < 2, b, zero)),
-            jnp.where(last, roll(l, 1, 0), jnp.where(row < 2, roll(b, -2, 0), zero)),
-            jnp.where(last, l, jnp.where(row < 2, roll(b, -4, 0), zero)),
-        )
+        tiles = [jnp.where(keep, rows_at(z, {0: (hi, 3 * k), 1: (hi, 3 * k + 1), 2: (hi, 3 * k + 2),
+                                             6: (lo, k), 7: (lo, 2 + k)}), zero) for k in range(2)]
+        tiles += [rows_at(z, {0: (hi, 6 + 2 * k), 1: (hi, 7 + 2 * k), 7: (lo, 4 + k)}) for k in range(4)]
         for k, tile in enumerate(tiles):
             halo[k, z] = tile
             acc[k] = jnp.where(group == z, roll(tile, 8 * z - 126, 1), acc[k])
@@ -271,17 +221,14 @@
             above = layer(above)
         br[z], bi[z] = advance(layer(z), above, below, t, none, tall(ep, halo.at[EP], z), lane)
 
-    one(0, 1, None)
-
     def body(z, carry):
         one(z, z + 1, z - 1)
         return carry
 
     lax.fori_loop(1, NZ - 1, body, 0)
-    one(NZ - 1, None, NZ - 2)
-
-
-def pack_edges(trig_halo, halo, own, lo, hi, strip, up, down):
+
+
+def pack_edges(pr, pi, ep, trig, halo, own, lo, hi, strip, ntrig, part, strip_part, up, down):
     lane = iota((RX, LANES), 1)
     slot = lane % 8
     group = lane // 8
@@ -306,24 +253,57 @@
     strip[PY] = join(PY, roll(b, 2, 1), jnp.where(one, roll(l, 1, 1), zero))
     strip[PZ] = join(PZ, b, jnp.where(one, l, zero))
     strip[EP] = join(EP, roll(b, -2, 1), jnp.where(one, roll(l, -1, 1), zero))
-    up[0], up[1] = turned_back(trig_halo[0, 14], trig_halo[1, 14], halo[PR, 14], halo[PI, 14])
-    down[0] = halo[PR, 1]
-    down[1] = halo[PI, 1]
-    for k in range(6):
-        up[2 + k] = halo[k, 15]
-        down[2 + k] = halo[k, 0]
-    c, s = sincos(strip[PZ])
-    wr, wi = turned_back(c, s, strip[PR], strip[PI])
-    out = jnp.where(group == 0, roll(wr, -8 * 14, 1), roll(wi, -8 * 13, 1))
-    for k in range(6):
-        out = jnp.where(group == 2 + k, roll(strip[k], 8 * (2 + k - 15), 1), out)
-    for t in range(RX // TILE):
-        up[8 + t] = out[t * TILE:(t + 1) * TILE]
-    out = jnp.where(group == 0, roll(strip[PR], -8, 1), strip[PI])
-    for k in range(6):
-        out = jnp.where(group == 2 + k, roll(strip[k], 8 * (2 + k), 1), out)
-    for t in range(RX // TILE):
-        down[8 + t] = out[t * TILE:(t + 1) * TILE]
+    for n, k in enumerate((PZ, PX, PY)):
+        ntrig[2 * n], ntrig[2 * n + 1] = sincos(strip[k])
+    keep_x, keep_xy = inside_masks()
+    keep_tile = keep_x[NX:]
+    sr, si = strip[PR], strip[PI]
+    nt = [ntrig[n] for n in range(6)]
+    w = turned_back(nt[0], nt[1], sr, si)
+    below = [jnp.where(group > 0, roll(v, 8, 1), zero) for v in w]
+    above = [jnp.where(group < NZ - 1, roll(v, -8, 1), zero) for v in (sr, si)]
+    qr, qi = [jnp.where(keep_xy > 0, v, zero) for v in advance((sr, si), above, below, nt, None, strip[EP], lane)]
+    strip_part[0] = qr
+    strip_part[1] = qi
+    er, ei = edge_columns(slot, ntrig, sr, si)
+
+    def layer(z):
+        return tall(pr, halo.at[PR], z), tall(pi, halo.at[PI], z)
+
+    def angles_of(z):
+        found = []
+        for n, k in enumerate((PZ, PX, PY)):
+            c, s = sincos(halo[k, z])
+            found += [jnp.concatenate([trig[2 * n, z], c], axis=0), jnp.concatenate([trig[2 * n + 1, z], s], axis=0)]
+        return found
+
+    def first_step(z, above, below, t):
+        edge = roll_by(er, shift_of(z)), roll_by(ei, shift_of(z))
+        v = advance(layer(z), above, below, t, edge, tall(ep, halo.at[EP], z), lane)
+        return masked_rows(v[0], keep_tile), masked_rows(v[1], keep_tile)
+
+    def send(message, tiles, layers, strips):
+        message[0], message[1] = tiles
+        packed = strips[3]
+        for k in range(3):
+            packed = jnp.where(group == k, strips[k], packed)
+        for k, v in enumerate((*layers, packed)):
+            for t in range(RX // TILE):
+                message[2 + 9 * k + t] = v[t * TILE:(t + 1) * TILE]
+
+    low = first_step(0, layer(1), None, angles_of(0))
+    t = angles_of(NZ - 1)
+    c, s = sincos(halo[PZ, NZ - 2])
+    below = turned_back(jnp.concatenate([trig[0, NZ - 2], c], axis=0), jnp.concatenate([trig[1, NZ - 2], s], axis=0),
+                        *layer(NZ - 2))
+    high = first_step(NZ - 1, None, below, t)
+    part[0], part[1] = low
+    part[2], part[3] = high
+    turned_strips = (*w, *turned_back(nt[0], nt[1], qr, qi))
+    send(up, turned_back(t[0][NX:], t[1][NX:], halo[PR, NZ - 1], halo[PI, NZ - 1]), turned_back(t[0], t[1], *high),
+         [roll(v, 8 * (k - 15), 1) for k, v in enumerate(turned_strips)])
+    send(down, (halo[PR, 0], halo[PI, 0]), low,
+         [roll(v, 8 * k, 1) for k, v in enumerate((sr, si, qr, qi))])
 
 
 def shift_of(group):
@@ -395,15 +375,13 @@
     return jnp.where(iota((LANES, LANES), 0) <= iota((LANES, LANES), 1), 1.0, 0.0).astype(F32)
 
 
-def interior(pr_in, pi_in, ep, trig, halo, trig_halo, strip, ntrig, cr, ci, final_r, final_i, out,
+def interior(pr_in, pi_in, ep, trig, halo, trig_halo, strip, ntrig, part, strip_part, cr, ci, final_r, final_i, out,
              er, ei, nr, ni, jx_edge, rows):
     lane = iota((RX, LANES), 1)
     slot = lane % 8
     keep_x, keep_xy = inside_masks()
     keep_tile = keep_x[NX:]
     zero = jnp.zeros((RX, LANES), F32)
-    for n, k in enumerate((PZ, PX, PY)):
-        ntrig[2 * n], ntrig[2 * n + 1] = sincos(strip[k])
     nt = lambda: [ntrig[n] for n in range(6)]
     er[...], ei[...] = edge_columns(slot, ntrig, strip[PR], strip[PI])
 
@@ -417,8 +395,9 @@
         ci[z] = masked_rows(pi_in[z] + hi, keep_tile)
         return carry
 
-    for z in range(NZ):
+    for z in range(1, NZ - 1):
         fix(z, 0)
+    cr[0], ci[0], cr[NZ - 1], ci[NZ - 1] = part[0], part[1], part[2], part[3]
 
     def strips(r, i):
         w = turned_back(ntrig[0], ntrig[1], r, i)
@@ -426,7 +405,7 @@
                     strip[EP], lane)
         return jnp.where(keep_xy > 0, v[0], zero), jnp.where(keep_xy > 0, v[1], zero)
 
-    mr, mi = strips(strip[PR], strip[PI])
+    mr, mi = strip_part[0], strip_part[1]
     er[...], ei[...] = edge_columns(slot, ntrig, mr, mi)
     r, i = strips(mr, mi)
     nr[...] = r
@@ -461,99 +440,63 @@
     analyse(z, r, i, t[2:4], t[4:6], columns, jx_column, lane, rows, out, spot)
 
 
-def boundary(pr, pi, ep, trig, halo, trig_halo, strip, ntrig0, cr, ci, middle_out,
-             zlo, zhi, elo, ehi, final_r, final_i, out, ntrig1, rows):
+def boundary(pr, pi, ep, trig, halo, trig_halo, strip, ntrig, strip_part, cr, ci, middle_out,
+             zlo, zhi, elo, ehi, final_r, final_i, out, rows):
     lane = iota((RX, LANES), 1)
     slot = lane % 8
     group = lane // 8
     keep_x, keep_xy = inside_masks()
     gz = lax.axis_index("gz")
-    z_hi, z_lo = on(gz < lax.axis_size("gz") - 1), on(gz > 0)
-    keep_z = jnp.where(group < 8, z_hi, z_lo)
+    ok_hi = jnp.broadcast_to(on(gz < lax.axis_size("gz") - 1), (RX, LANES)) > 0
+    ok_lo = jnp.broadcast_to(on(gz > 0), (RX, LANES)) > 0
     zero = jnp.zeros((RX, LANES), F32)
     for away in range(out.shape[0]):
         out[away, 8:] = middle_out[away]
-    lo8 = jnp.concatenate([elo[8 + t] for t in range(RX // TILE)], axis=0)
-    hi8 = jnp.concatenate([ehi[8 + t] for t in range(RX // TILE)], axis=0)
-
-    def beyond(k, outer):
-        v = jnp.where(group == 0, roll(hi8, -8 * (2 + k), 1), roll(lo8, 8 * (15 - 2 - k), 1))
-        if outer is not None:
-            v = jnp.where(group == 1, roll(hi8, 8 * (1 - outer), 1), v)
-            v = jnp.where(group == 14, roll(lo8, 8 * (14 - outer), 1), v)
-        return v
-
-    for n, k in enumerate((PZ, PX, PY)):
-        v = beyond(k, None)
-        if k == PZ:
-            v = jnp.where(group == 14, zero, v)
-        ntrig1[2 * n], ntrig1[2 * n + 1] = sincos(v)
-    trigs = (ntrig0, ntrig1)
-    gains = (strip[EP], beyond(EP, None))
-
-    def step_strips(halves, wanted):
-        w = [turned_back(trigs[h][0], trigs[h][1], *halves[h]) for h in range(2)]
-        results = []
-        for h in wanted:
-            g = 1 - h
-            below = [jnp.where(group == 0, roll(w[g][n], 8, 1), roll(w[h][n], 8, 1)) for n in range(2)]
-            above = [jnp.where(group == 15, roll(halves[g][n], -8, 1), roll(halves[h][n], -8, 1)) for n in range(2)]
-            v = advance(halves[h], above, below, [trigs[h][n] for n in range(6)], None, gains[h], lane)
-            keep = keep_xy if h == 0 else keep_xy * keep_z
-            results.append([jnp.where(keep > 0, u, zero) for u in v])
-        return results
-
-    halves = ((strip[PR], strip[PI]),
-              (jnp.where(keep_z > 0, beyond(PR, 0), zero), jnp.where(keep_z > 0, beyond(PI, 1), zero)))
-    beyond_edge = edge_columns(slot, ntrig1, *halves[1])
-    middle = step_strips(halves, (0, 1))
-    edges = edge_columns(slot, ntrig0, *middle[0])
-    (columns,) = step_strips(middle, (0,))
-    t = turned(ntrig0[2], ntrig0[3], ahead_x(columns[0]), ahead_x(columns[1]))
-    jx_column = columns[0] * t[1] - columns[1] * t[0]
-
-    ok_lo = jnp.broadcast_to(z_lo, (RX, LANES)) > 0
-    ok_hi = jnp.broadcast_to(z_hi, (RX, LANES)) > 0
-
-    def got(main, tiles, n):
-        return jnp.concatenate([main[n], tiles[n]], axis=0)
-
-    def angles(main, tiles):
-        found = []
-        for k in (PZ, PX, PY):
-            found += list(sincos(got(main, tiles, 2 + k)))
-        return found
-
-    def own(z):
-        return tall(pr, halo.at[PR], z), tall(pi, halo.at[PI], z)
+
+    def piece(message, k):
+        return jnp.concatenate([message[2 + 9 * k + t] for t in range(RX // TILE)], axis=0)
+
+    def added(v, w):
+        return tuple(a + time_step * b for a, b in zip(v, w))
 
     def masked(ok, v):
         return tuple(jnp.where(ok, u, zero) for u in v)
 
-    def at(z, n):
-        return angles_at(trig, trig_halo, n, z)
-
-    t_lo = angles(zlo, elo)
-    outer = masked(ok_lo, (got(zlo, elo, 0), got(zlo, elo, 1)))
-    inner = masked(ok_lo, (got(zlo, elo, 2), got(zlo, elo, 3)))
-    edge = roll_by(beyond_edge[0], shift_of(15)), roll_by(beyond_edge[1], shift_of(15))
-    v = masked(ok_lo & (keep_x > 0), advance(inner, own(0), outer, t_lo, edge, got(zlo, elo, 2 + EP), lane))
-    w = turned_back(t_lo[0], t_lo[1], *inner)
-    first = masked(keep_x > 0, (cr[0] + time_step * w[0], ci[0] + time_step * w[1]))
-    below = turned_back(t_lo[0], t_lo[1], *v)
+    lo_strip, hi_strip = piece(elo, 2), piece(ehi, 2)
+    own = strip[PR], strip[PI]
+    nt = [ntrig[n] for n in range(6)]
+    from_lo = [roll(lo_strip, -8 * k, 1) for k in range(4)]
+    from_hi = [roll(hi_strip, 8 * (15 - k), 1) for k in range(4)]
+    at_lo, at_hi = ok_lo & (group == 0), ok_hi & (group == NZ - 1)
+    beyond = turned(nt[0], nt[1], *from_hi[:2])
+    middle = added((strip_part[0], strip_part[1]),
+                   [jnp.where(at_lo, a, jnp.where(at_hi, b, zero)) for a, b in zip(from_lo, beyond)])
+    lower = masked(ok_lo, added(from_lo[2:], own))
+    upper = masked(ok_hi, added(from_hi[2:], turned_back(nt[0], nt[1], *own)))
+    w = turned_back(nt[0], nt[1], *middle)
+    below = [jnp.where(group == 0, a, roll(b, 8, 1)) for a, b in zip(lower, w)]
+    above = [jnp.where(group == NZ - 1, a, roll(b, -8, 1)) for a, b in zip(upper, middle)]
+    columns = masked(keep_xy > 0, advance(middle, above, below, nt, None, strip[EP], lane))
+    edges = edge_columns(slot, ntrig, *middle)
+    t = turned(nt[2], nt[3], ahead_x(columns[0]), ahead_x(columns[1]))
+    jx_column = columns[0] * t[1] - columns[1] * t[0]
+
+    def layer(z):
+        return tall(pr, halo.at[PR], z), tall(pi, halo.at[PI], z)
+
+    def got(main, tiles):
+        return tuple(jnp.concatenate([main[n], tiles[n]], axis=0) for n in range(2))
+
     common = (ep, trig, halo, trig_halo, edges, columns, jx_column, keep_x, lane, rows, final_r, final_i, out)
+    first = added((cr[0], ci[0]), masked(ok_lo, got(zlo, elo)))
+    below = masked(ok_lo, added((piece(elo, 0), piece(elo, 1)), layer(0)))
     last_layer(0, first, (cr[1], ci[1]), None, *common, below, 0)
     last_layer(1, (cr[1], ci[1]), (cr[2], ci[2]), first, *common, None, 1)
-    t_hi = angles(zhi, ehi)
-    outer = masked(ok_hi, (got(zhi, ehi, 0), got(zhi, ehi, 1)))
-    inner = masked(ok_hi, (got(zhi, ehi, 2), got(zhi, ehi, 3)))
-    edge = roll_by(beyond_edge[0], shift_of(0)), roll_by(beyond_edge[1], shift_of(0))
-    below = turned_back(at(15, 0), at(15, 1), *own(15))
-    v = masked(ok_hi & (keep_x > 0), advance(inner, outer, below, t_hi, edge, got(zhi, ehi, 2 + EP), lane))
-    w = turned(at(15, 0), at(15, 1), *inner)
-    final = masked(keep_x > 0, (cr[15] + time_step * w[0], ci[15] + time_step * w[1]))
+    c, s = angles_at(trig, trig_halo, 0, NZ - 1), angles_at(trig, trig_halo, 1, NZ - 1)
+    final = added((cr[15], ci[15]), turned(c, s, *masked(ok_hi, got(zhi, ehi))))
+    above = masked(ok_hi, added((piece(ehi, 0), piece(ehi, 1)), turned_back(c, s, *layer(NZ - 1))))
     last_layer(14, (cr[14], ci[14]), final, (cr[13], ci[13]), *common, None, 2)
-    last_layer(15, final, v, (cr[14], ci[14]), *common, None, 3)
+    last_layer(15, final, above, (cr[14], ci[14]), *common, None, 3)
     prefix(rows, out, range(4), 4)
 
 
@@ -612,8 +555,9 @@
     return jax.ShapeDtypeStruct(shape, F32)
 
 
-def call(body, outs, *args, scratch=(), hbm=0, hbm_out=False):
-    memory = [pl.BlockSpec(memory_space=pltpu.HBM if k < hbm else pltpu.VMEM) for k in range(len(args))]
+def call(body, outs, *args, scratch=(), hbm=0, smem=0, hbm_out=False):
+    memory = [pl.BlockSpec(memory_space=pltpu.HBM if k < hbm else pltpu.SMEM if k < smem else pltpu.VMEM)
+              for k in range(len(args))]
     return pl.pallas_call(
         body, out_shape=outs, in_specs=memory, scratch_shapes=list(scratch),
         out_specs=jax.tree.map(lambda _: pl.BlockSpec(memory_space=pltpu.HBM if hbm_out else pltpu.VMEM), outs),
@@ -636,40 +580,37 @@
 
 def program(pr_in, pi_in, pz_in, px_in, py_in, material, levels):
     parts = lax.axis_size("gy")
-    raw = (levels, pr_in, pi_in, px_in, py_in, pz_in, material)
+    pr, pi, px, py, pz = pr_in, pi_in, px_in, py_in, pz_in
+    raw = (levels, pr, pi, px, py, pz, material)
     raw = tuple(pltpu.with_memory_space_constraint(a, pltpu.HBM) for a in raw)
-    edge = spec(NZ, TILE, LANES)
     block, tall_block, strip_like = spec(NZ, NX, NY), spec(NZ, RX, LANES), spec(RX, LANES)
     scratch = lambda s, dtype=F32: pltpu.VMEM(s.shape, dtype)
-    layers = spec(8, NX, NY)
-    up, down, zup, zdown = call(pack_first, (edge, spec(NZ, 2 * TILE, LANES), layers, layers), *raw, hbm=7, scratch=[
-        pltpu.SMEM((LEVELS,), F32), pltpu.VMEM((5, NZ, TILE, LANES), F32), pltpu.VMEM((5, NZ, TILE, LANES), F32),
-        scratch(edge, jnp.int32), scratch(edge, jnp.int32), pltpu.VMEM((3, NX, NY), F32),
-        pltpu.VMEM((2, NX, NY), jnp.int32), pltpu.SemaphoreType.DMA((30,))])
+    layers = spec(2, NX, NY)
+    up, down, zup, zdown = call(pack_first, (spec(8, NZ, NY), spec(14, NZ, NY), layers, layers), *raw, hbm=7, scratch=[
+        pltpu.SMEM((LEVELS,), F32), pltpu.VMEM((3, NZ, NY), F32), pltpu.VMEM((3, NZ, NY), jnp.int32),
+        pltpu.VMEM((3, NX, NY), F32), pltpu.SemaphoreType.DMA((29,))])
     lo, hi = exchange(up, down, "gx")
     zlo, zhi = exchange(zup, zdown, "gz")
-    pr, pi, ep, trig, own = call(
-        prepare, (block, block, block, spec(6, NZ, NX, NY), spec(6, NX, LANES)),
-        *raw, hbm=7, scratch=[pltpu.SMEM((LEVELS,), F32), scratch(block), scratch(block), scratch(block),
-                              scratch(block, jnp.int32), pltpu.SemaphoreType.DMA((7,))])
+    own = call(columns, spec(6, NX, LANES), levels, pr, pi, px, py, pz, material, smem=1)
     halo, own, up, down = call(
         pack_y, (spec(6, NZ, TILE, LANES), spec(6, RX, LANES), strip_like, spec(2, RX, LANES)), own, lo, hi)
     lo, hi = exchange(up, down, "gy")
+    ep, trig = call(angles, (block, spec(6, NZ, NX, NY)), levels, px, py, pz, material, smem=1)
+    message = spec(2 + 3 * RX // TILE, TILE, LANES)
+    strip, ntrig, part, strip_part, up, down = call(
+        pack_edges, (spec(6, RX, LANES), spec(6, RX, LANES), spec(4, RX, LANES), spec(2, RX, LANES), message, message),
+        pr, pi, ep, trig, halo, own, lo, hi)
+    elo, ehi = exchange(up, down, "gz")
     trig_halo, br, bi = call(begin, (spec(6, NZ, TILE, LANES), tall_block, tall_block), pr, pi, ep, trig, halo)
-    strip, up, down = call(pack_edges, (spec(6, RX, LANES), spec(17, TILE, LANES), spec(17, TILE, LANES)),
-                           trig_halo, halo, own, lo, hi)
-    elo, ehi = exchange(up, down, "gz")
     middle_block, ends_block = spec(NZ - 4, NX, NY), spec(4, NX, NY)
-    ntrig, cr, ci, some_r, some_i, out = call(
-        interior, (spec(6, RX, LANES), tall_block, tall_block, middle_block, middle_block,
-                   spec(parts, 2 * NZ - 8, TILE, LANES)),
-        br, bi, ep, trig, halo, trig_halo, strip,
+    cr, ci, some_r, some_i, out = call(
+        interior, (tall_block, tall_block, middle_block, middle_block, spec(parts, 2 * NZ - 8, TILE, LANES)),
+        br, bi, ep, trig, halo, trig_halo, strip, ntrig, part, strip_part,
         scratch=[scratch(strip_like)] * 5 + [pltpu.VMEM(((NZ - 4) * NX, NY), F32)])
     got = [ahead(out[k], k) for k in EARLY]
     ends_r, ends_i, out = call(
         boundary, (ends_block, ends_block, spec(parts, 2 * NZ, TILE, LANES)), pr, pi, ep, trig, halo, trig_halo, strip,
-        ntrig, cr, ci, out, zlo, zhi, elo, ehi,
-        scratch=[pltpu.VMEM((6, RX, LANES), F32), pltpu.VMEM((4 * NX, NY), F32)])
+        ntrig, strip_part, cr, ci, out, zlo, zhi, elo, ehi, scratch=[pltpu.VMEM((4 * NX, NY), F32)])
     late = {k: ahead(out[k, :8] if k in EARLY else out[k], k) for k in LATE}
     final_r, final_i = call(store, (block, block), some_r, some_i, ends_r, ends_i, hbm_out=True,
                             scratch=[pltpu.SemaphoreType.DMA((6,))])

time: 62.1 us -> 55 us (0.89)
  the two profiles are of different devices: /device:TPU:1 before, /device:TPU:6 now
where the time goes in v5:
time: 55 us; the launch traced here: 54.9 us
  starting transfers between devices  22.1 us (40%)
  waiting for transfers between devices  17.8 us (32%)
  Pallas kernels  14 us (25%)
  between operations  0.89 us (2%)
    pallas_call x10, Pallas kernels, call(): pl.pallas_call(body, out_shape=outs, in_specs=memory, scratch_shapes=list...  14 us
    ppermute x4, starting transfers between devices, exchange(): hi = lax.ppermute(down, axis, [(b, a) for a, b in forward])  13.1 us
    ppermute x7, waiting for transfers between devices, ahead(): return lax.ppermute(value, 'gy', [(i, (i + k) % size) for i in range(size)])  12.1 us
    ppermute x7, starting transfers between devices, ahead(): return lax.ppermute(value, 'gy', [(i, (i + k) % size) for i in range(size)])  6.79 us
    ppermute x4, waiting for transfers between devices, exchange(): lo = lax.ppermute(up, axis, forward)  5.71 us
    ppermute x4, starting transfers between devices, exchange(): lo = lax.ppermute(up, axis, forward)  2.26 us
  transfers between devices with their start and end apart: 15, of which 4 were waited for; matrix products, arithmetic and copies ran while one was open for 0% of the time, Pallas kernels for 17%

profile of v5, /device:TPU:6, one launch (start us, length us, event | category | flops | bytes accessed | tf_op | source)
XLA Modules:
  0.0 54.9 jit_solution(16343254774989601552)
XLA Ops:
  0.7 1.4 %shard_map.104 = (f32[8,16,128]{2,1,0:T(8,128)S(1)}, f32[14,16,128]{2,1,0:T(8,128)S(1)}, f32[2,64,128]{2,1,0:T(8,128)S(1)}, f32[2,64,128]{2,1,0:T(8,128)S(1)}) custom-call(f32[8]{0:T(128)} %levels_in.1, f32[16,64,128]{2,1,0:T(8,128)} %pr.9, f32[16,64,128]{2,1,0:T(8,128)} %pi.9, f32[16,64,128]{2,1,0:T(8,128)} %px.5, f32[16,64,128]{2,1,0:T(8,128)} %py.5, ...), custom_call_target="tpu_custom_call" | custom-call | tf_op jit(solution)/shard_map/pallas_call | solution.py:561
  2.1 6.4 %collective-permute-start.1 = (f32[14,16,128]{2,1,0:T(8,128)S(1)}, f32[14,16,128]{2,1,0:T(8,128)S(1)}, u32[]{:S(2)}, u32[]{:S(2)}) collective-permute-start(f32[14,16,128]{2,1,0:T(8,128)S(1)} %get-tuple-element.38), channel_id=1, source_target_pairs={{64,0},{128,64},{192,128},{0,192},{65,1},{129,65},{193,129},{1,193... | collective-permute-start | bytes 344072 | tf_op jit(solution)/shard_map/ppermute | solution.py:572
  8.5 1.4 %shard_map.103.own_in = f32[6,64,128]{2,1,0:T(8,128)S(1)} custom-call(f32[8]{0:T(128)S(1)} %copy-done.6, f32[16,64,128]{2,1,0:T(8,128)S(1)} %copy-done, f32[16,64,128]{2,1,0:T(8,128)S(1)} %copy-done.1, f32[16,64,128]{2,1,0:T(8,128)S(1)} %copy-done.2, f32[16,64,128]{2,1,0:T(8,128)S(1)} %copy-done.3, f32[16,64,128]{2,1,0:T(8,128)S(1)} %copy-done.4, ...), custom_call_target="tpu_custom_call" | custom-call | tf_op jit(solution)/shard_map/pallas_call | solution.py:561
  10.0 5.0 %collective-permute-done.lo = f32[8,16,128]{2,1,0:T(8,128)S(1)} collective-permute-done((f32[8,16,128]{2,1,0:T(8,128)S(1)}, f32[8,16,128]{2,1,0:T(8,128)S(1)}, u32[]{:S(2)}, u32[]{:S(2)}) %collective-permute-start) | collective-permute-done | bytes 65568 | tf_op jit(solution)/shard_map/ppermute | solution.py:571
  15.0 0.4 shard_map.105
  15.4 0.5 collective-permute-start.2
  15.9 2.2 %shard_map.102 = (f32[16,64,128]{2,1,0:T(8,128)S(1)}, f32[6,16,64,128]{3,2,1,0:T(8,128)S(1)}) custom-call(f32[8]{0:T(128)S(1)} %copy-done.6, f32[16,64,128]{2,1,0:T(8,128)S(1)} %copy-done.2, f32[16,64,128]{2,1,0:T(8,128)S(1)} %copy-done.3, f32[16,64,128]{2,1,0:T(8,128)S(1)} %copy-done.4, s32[16,64,128]{2,1,0:T(8,128)S(1)} %copy-done.5), custom_call_target="tpu_custom_call" | custom-call | tf_op jit(solution)/shard_map/pallas_call | solution.py:561
  18.1 0.7 %collective-permute-done.2.lo = f32[72,128]{1,0:T(8,128)S(1)} collective-permute-done((f32[72,128]{1,0:T(8,128)S(1)}, f32[72,128]{1,0:T(8,128)S(1)}, u32[]{:S(2)}, u32[]{:S(2)}) %collective-permute-start.2) | collective-permute-done | bytes 36896 | tf_op jit(solution)/shard_map/ppermute | solution.py:571
  18.8 0.7 %shard_map.107 = (f32[6,72,128]{2,1,0:T(8,128)S(1)}, f32[6,72,128]{2,1,0:T(8,128)S(1)}, f32[4,72,128]{2,1,0:T(8,128)S(1)}, f32[2,72,128]{2,1,0:T(8,128)S(1)}, f3...) custom-call(f32[16,64,128]{2,1,0:T(8,128)S(1)} %copy-done, f32[16,64,128]{2,1,0:T(8,128)S(1)} %copy-done.1, ...), custom_call_target="tpu_custom_call" | custom-call | tf_op jit(solution)/shard_map/pallas_call | solution.py:561
  19.5 1.8 %collective-permute-start.6 = (f32[29,8,128]{2,1,0:T(8,128)S(1)}, f32[29,8,128]{2,1,0:T(8,128)S(1)}, u32[]{:S(2)}, u32[]{:S(2)}) collective-permute-start(f32[29,8,128]{2,1,0:T(8,128)S(1)} %get-tuple-element.57), channel_id=1, source_target_pairs={{0,1},{1,2},{2,3},{3,4},{4,5},{5,6},{6,7},{7,0},{8,9},{9,10},{10,1... | collective-permute-start | bytes 356360 | tf_op jit(solution)/shard_map/ppermute | solution.py:571
  21.2 2.5 %collective-permute-start.7 = (f32[29,8,128]{2,1,0:T(8,128)S(1)}, f32[29,8,128]{2,1,0:T(8,128)S(1)}, u32[]{:S(2)}, u32[]{:S(2)}) collective-permute-start(f32[29,8,128]{2,1,0:T(8,128)S(1)} %get-tuple-element.58), channel_id=1, source_target_pairs={{1,0},{2,1},{3,2},{4,3},{5,4},{6,5},{7,6},{0,7},{9,8},{10,9},{11,1... | collective-permute-start | bytes 356360 | tf_op jit(solution)/shard_map/ppermute | solution.py:572
  23.8 4.1 %collective-permute-start.5 = (f32[2,64,128]{2,1,0:T(8,128)S(1)}, f32[2,64,128]{2,1,0:T(8,128)S(1)}, u32[]{:S(2)}, u32[]{:S(2)}) collective-permute-start(f32[2,64,128]{2,1,0:T(8,128)S(1)} %get-tuple-element.56), channel_id=1, source_target_pairs={{1,0},{2,1},{3,2},{4,3},{5,4},{6,5},{7,6},{0,7},{9,8},{10,9},{11,1... | collective-permute-start | bytes 196616 | tf_op jit(solution)/shard_map/ppermute | solution.py:572
  27.9 1.9 %shard_map.106 = (f32[6,16,8,128]{3,2,1,0:T(8,128)S(1)}, f32[16,72,128]{2,1,0:T(8,128)S(1)}, f32[16,72,128]{2,1,0:T(8,128)S(1)}) custom-call(f32[16,64,128]{2,1,0:T(8,128)S(1)} %copy-done, f32[16,64,128]{2,1,0:T(8,128)S(1)} %copy-done.1, f32[16,64,128]{2,1,0:T(8,128)S(1)} %get-tuple-element.35.ep, f32[6,16,64,128]{3,2,1,0:T(8,128)S(1)} %get-tuple-element.36.trig, ...), custom_call_target="tpu_custom_call" | custom-call | tf_op jit(solution)/shard_map/pallas_call | solution.py:561
  29.9 2.7 %shard_map.108 = (f32[16,72,128]{2,1,0:T(8,128)S(1)}, f32[16,72,128]{2,1,0:T(8,128)S(1)}, f32[12,64,128]{2,1,0:T(8,128)S(1)}, f32[12,64,128]{2,1,0:T(8,128)S(1)}, f32[8,24,8,128]{3,2,1,0:T(8,128)S(1)}) custom-call(f32[16,72,128]{2,1,0:T(8,128)S(1)} %get-tuple-element.40.pr_in, f32[16,72,128]{2,1,0:T(8,128)S(1)} %get-tuple-element.41.pi_in, ...), custom_call_target="tpu_custom_call" | custom-call | tf_op jit(solution)/shard_map/pallas_call | solution.py:561
  32.6 1.1 %shard_map.109 = (f32[4,64,128]{2,1,0:T(8,128)S(1)}, f32[4,64,128]{2,1,0:T(8,128)S(1)}, f32[8,32,8,128]{3,2,1,0:T(8,128)S(1)}) custom-call(f32[16,64,128]{2,1,0:T(8,128)S(1)} %copy-done, f32[16,64,128]{2,1,0:T(8,128)S(1)} %copy-done.1, f32[16,64,128]{2,1,0:T(8,128)S(1)} %get-tuple-element.35.ep, f32[6,16,64,128]{3,2,1,0:T(8,128)S(1)} %get-tuple-element.36.trig, ...), custom_call_target="tpu_custom_call" | custom-call | tf_op jit(solution)/shard_map/pallas_call | solution.py:561
  33.8 0.9 %collective-permute-start.13 = (f32[32,8,128]{2,1,0:T(8,128)S(1)}, f32[32,8,128]{2,1,0:T(8,128)S(1)}, u32[]{:S(2)}, u32[]{:S(2)}) collective-permute-start(f32[32,8,128]{2,1,0:T(8,128)S(1)} %get-tuple-element.67), channel_id=1, source_target_pairs={{0,48},{8,56},{16,0},{24,8},{32,16},{40,24},{48,32},{56,40},{1,49}... | collective-permute-start | bytes 393224 | tf_op jit(solution)/shard_map/ppermute | solution.py:578
  34.7 3.3 %collective-permute-start.12 = (f32[32,8,128]{2,1,0:T(8,128)S(1)}, f32[32,8,128]{2,1,0:T(8,128)S(1)}, u32[]{:S(2)}, u32[]{:S(2)}) collective-permute-start(f32[32,8,128]{2,1,0:T(8,128)S(1)} %get-tuple-element.68), channel_id=1, source_target_pairs={{0,40},{8,48},{16,56},{24,0},{32,8},{40,16},{48,24},{56,32},{1,41}... | collective-permute-start | bytes 393224 | tf_op jit(solution)/shard_map/ppermute | solution.py:578
  38.0 0.3 collective-permute-start.11
  38.2 2.1 %collective-permute-start.10 = (f32[32,8,128]{2,1,0:T(8,128)S(1)}, f32[32,8,128]{2,1,0:T(8,128)S(1)}, u32[]{:S(2)}, u32[]{:S(2)}) collective-permute-start(f32[32,8,128]{2,1,0:T(8,128)S(1)} %get-tuple-element.70), channel_id=1, source_target_pairs={{0,24},{8,32},{16,40},{24,48},{32,56},{40,0},{48,8},{56,16},{1,25}... | collective-permute-start | bytes 393224 | tf_op jit(solution)/shard_map/ppermute | solution.py:578
  40.3 0.3 collective-permute-start.9
  40.6 8.8 %collective-permute-done.13.refs_6_ = f32[32,8,128]{2,1,0:T(8,128)S(1)} collective-permute-done((f32[32,8,128]{2,1,0:T(8,128)S(1)}, f32[32,8,128]{2,1,0:T(8,128)S(1)}, u32[]{:S(2)}, u32[]{:S(2)}) %collective-permute-start.13) | collective-permute-done | bytes 131104 | tf_op jit(solution)/shard_map/ppermute | solution.py:578
  49.3 1.0 %shard_map.110 = (f32[16,64,128]{2,1,0:T(8,128)}, f32[16,64,128]{2,1,0:T(8,128)}) custom-call(f32[12,64,128]{2,1,0:T(8,128)S(1)} %get-tuple-element.50.some_r, f32[12,64,128]{2,1,0:T(8,128)S(1)} %get-tuple-element.51.some_i, f32[4,64,128]{2,1,0:T(8,128)S(1)} %get-tuple-element.59.ends_r, f32[4,64,128]{2,1,0:T(8,128)S(1)} %get-tuple-element.60.ends_i), custom_call_target="tpu_custom_call" | custom-call | tf_op jit(solution)/shard_map/pallas_call | solution.py:561
  50.4 3.3 %collective-permute-done.8.refs_1_ = f32[32,8,128]{2,1,0:T(8,128)S(1)} collective-permute-done((f32[32,8,128]{2,1,0:T(8,128)S(1)}, f32[32,8,128]{2,1,0:T(8,128)S(1)}, u32[]{:S(2)}, u32[]{:S(2)}) %collective-permute-start.8) | collective-permute-done | bytes 131104 | tf_op jit(solution)/shard_map/ppermute | solution.py:578
  53.7 1.2 %shard_map.111 = (f32[16,8,1024]{2,1,0:T(8,128)}, f32[16,8,1024]{2,1,0:T(8,128)}) custom-call(f32[32,8,128]{2,1,0:T(8,128)S(1)} %get-tuple-element.73.refs_0_, f32[32,8,128]{2,1,0:T(8,128)S(1)} %collective-permute-done.8.refs_1_, f32[32,8,128]{2,1,0:T(8,128)S(1)} %collective-permute-done.9.refs_2_, f32[32,8,128]{2,1,0:T(8,128)S(1)} %collective-permute-done.10.refs_3_, ...), custom_call_target="tpu_custom_call" | custom-call | tf_op jit(solution)/shard_map/pallas_call | solution.py:561
  (31 shorter events, 0.2 us)
Async XLA Ops:
  0.6 7.8 %copy-start.1 = (f32[16,64,128]{2,1,0:T(8,128)S(1)}, f32[16,64,128]{2,1,0:T(8,128)}, u32[]{:S(2)}) copy-start(f32[16,64,128]{2,1,0:T(8,128)} %pi.9) | copy-start | bytes 1572868
  0.6 7.8 %copy-start = (f32[16,64,128]{2,1,0:T(8,128)S(1)}, f32[16,64,128]{2,1,0:T(8,128)}, u32[]{:S(2)}) copy-start(f32[16,64,128]{2,1,0:T(8,128)} %pr.9) | copy-start | bytes 1572868
  0.7 7.8 %copy-start.6 = (f32[8]{0:T(128)S(1)}, f32[8]{0:T(128)}, u32[]{:S(2)}) copy-start(f32[8]{0:T(128)} %levels_in.1) | copy-start | bytes 100
  0.7 7.8 %copy-start.5 = (s32[16,64,128]{2,1,0:T(8,128)S(1)}, s32[16,64,128]{2,1,0:T(8,128)}, u32[]{:S(2)}) copy-start(s32[16,64,128]{2,1,0:T(8,128)} %mat.5) | copy-start | bytes 1572868
  0.7 7.8 %copy-start.3 = (f32[16,64,128]{2,1,0:T(8,128)S(1)}, f32[16,64,128]{2,1,0:T(8,128)}, u32[]{:S(2)}) copy-start(f32[16,64,128]{2,1,0:T(8,128)} %py.5) | copy-start | bytes 1572868
  0.7 7.8 %copy-start.2 = (f32[16,64,128]{2,1,0:T(8,128)S(1)}, f32[16,64,128]{2,1,0:T(8,128)}, u32[]{:S(2)}) copy-start(f32[16,64,128]{2,1,0:T(8,128)} %px.5) | copy-start | bytes 1572868
  0.7 7.8 %copy-start.4 = (f32[16,64,128]{2,1,0:T(8,128)S(1)}, f32[16,64,128]{2,1,0:T(8,128)}, u32[]{:S(2)}) copy-start(f32[16,64,128]{2,1,0:T(8,128)} %pz.5) | copy-start | bytes 1572868
  2.1 12.9 %collective-permute-start.1 = (f32[14,16,128]{2,1,0:T(8,128)S(1)}, f32[14,16,128]{2,1,0:T(8,128)S(1)}, u32[]{:S(2)}, u32[]{:S(2)}) collective-permute-start(f32[14,16,128]{2,1,0:T(8,128)S(1)} %get-tuple-element.38), channel_id=1, source_target_pairs={{64,0},{128,64},{192,128},{0,192},{65,1},{129,65},{193,129},{1,193... | collective-permute-start | bytes 344072 | tf_op jit(solution)/shard_map/ppermute | solution.py:572
  8.5 6.5 %collective-permute-start = (f32[8,16,128]{2,1,0:T(8,128)S(1)}, f32[8,16,128]{2,1,0:T(8,128)S(1)}, u32[]{:S(2)}, u32[]{:S(2)}) collective-permute-start(f32[8,16,128]{2,1,0:T(8,128)S(1)} %get-tuple-element.37), channel_id=1, source_target_pairs={{0,64},{64,128},{128,192},{192,0},{1,65},{65,129},{129,193},{193,1... | collective-permute-start | bytes 196616 | tf_op jit(solution)/shard_map/ppermute | solution.py:571
  15.4 3.4 %collective-permute-start.3 = (f32[2,72,128]{2,1,0:T(8,128)S(1)}, f32[2,72,128]{2,1,0:T(8,128)S(1)}, u32[]{:S(2)}, u32[]{:S(2)}) collective-permute-start(f32[2,72,128]{2,1,0:T(8,128)S(1)} %get-tuple-element.45), channel_id=1, source_target_pairs={{8,0},{16,8},{24,16},{32,24},{40,32},{48,40},{56,48},{0,56},{9,1},... | collective-permute-start | bytes 221192 | tf_op jit(solution)/shard_map/ppermute | solution.py:572
  15.4 3.4 %collective-permute-start.2 = (f32[72,128]{1,0:T(8,128)S(1)}, f32[72,128]{1,0:T(8,128)S(1)}, u32[]{:S(2)}, u32[]{:S(2)}) collective-permute-start(f32[72,128]{1,0:T(8,128)S(1)} %get-tuple-element.44), channel_id=1, source_target_pairs={{0,8},{8,16},{16,24},{24,32},{32,40},{40,48},{48,56},{56,0},{1,9},... | collective-permute-start | bytes 110600 | tf_op jit(solution)/shard_map/ppermute | solution.py:571
  19.5 13.1 %collective-permute-start.6 = (f32[29,8,128]{2,1,0:T(8,128)S(1)}, f32[29,8,128]{2,1,0:T(8,128)S(1)}, u32[]{:S(2)}, u32[]{:S(2)}) collective-permute-start(f32[29,8,128]{2,1,0:T(8,128)S(1)} %get-tuple-element.57), channel_id=1, source_target_pairs={{0,1},{1,2},{2,3},{3,4},{4,5},{5,6},{6,7},{7,0},{8,9},{9,10},{10,1... | collective-permute-start | bytes 356360 | tf_op jit(solution)/shard_map/ppermute | solution.py:571
  21.2 11.3 %collective-permute-start.7 = (f32[29,8,128]{2,1,0:T(8,128)S(1)}, f32[29,8,128]{2,1,0:T(8,128)S(1)}, u32[]{:S(2)}, u32[]{:S(2)}) collective-permute-start(f32[29,8,128]{2,1,0:T(8,128)S(1)} %get-tuple-element.58), channel_id=1, source_target_pairs={{1,0},{2,1},{3,2},{4,3},{5,4},{6,5},{7,6},{0,7},{9,8},{10,9},{11,1... | collective-permute-start | bytes 356360 | tf_op jit(solution)/shard_map/ppermute | solution.py:572
  23.8 8.8 %collective-permute-start.4 = (f32[2,64,128]{2,1,0:T(8,128)S(1)}, f32[2,64,128]{2,1,0:T(8,128)S(1)}, u32[]{:S(2)}, u32[]{:S(2)}) collective-permute-start(f32[2,64,128]{2,1,0:T(8,128)S(1)} %get-tuple-element.55), channel_id=1, source_target_pairs={{0,1},{1,2},{2,3},{3,4},{4,5},{5,6},{6,7},{7,0},{8,9},{9,10},{10,1... | collective-permute-start | bytes 196616 | tf_op jit(solution)/shard_map/ppermute | solution.py:571
  23.8 8.8 %collective-permute-start.5 = (f32[2,64,128]{2,1,0:T(8,128)S(1)}, f32[2,64,128]{2,1,0:T(8,128)S(1)}, u32[]{:S(2)}, u32[]{:S(2)}) collective-permute-start(f32[2,64,128]{2,1,0:T(8,128)S(1)} %get-tuple-element.56), channel_id=1, source_target_pairs={{1,0},{2,1},{3,2},{4,3},{5,4},{6,5},{7,6},{0,7},{9,8},{10,9},{11,1... | collective-permute-start | bytes 196616 | tf_op jit(solution)/shard_map/ppermute | solution.py:572
  33.8 6.5 %collective-permute-start.14 = (f32[32,8,128]{2,1,0:T(8,128)S(1)}, f32[32,8,128]{2,1,0:T(8,128)S(1)}, u32[]{:S(2)}, u32[]{:S(2)}) collective-permute-start(f32[32,8,128]{2,1,0:T(8,128)S(1)} %get-tuple-element.66), channel_id=1, source_target_pairs={{0,56},{8,0},{16,8},{24,16},{32,24},{40,32},{48,40},{56,48},{1,57}... | collective-permute-start | bytes 393224 | tf_op jit(solution)/shard_map/ppermute | solution.py:578
  33.8 15.5 %collective-permute-start.13 = (f32[32,8,128]{2,1,0:T(8,128)S(1)}, f32[32,8,128]{2,1,0:T(8,128)S(1)}, u32[]{:S(2)}, u32[]{:S(2)}) collective-permute-start(f32[32,8,128]{2,1,0:T(8,128)S(1)} %get-tuple-element.67), channel_id=1, source_target_pairs={{0,48},{8,56},{16,0},{24,8},{32,16},{40,24},{48,32},{56,40},{1,49}... | collective-permute-start | bytes 393224 | tf_op jit(solution)/shard_map/ppermute | solution.py:578
  34.7 15.6 %collective-permute-start.12 = (f32[32,8,128]{2,1,0:T(8,128)S(1)}, f32[32,8,128]{2,1,0:T(8,128)S(1)}, u32[]{:S(2)}, u32[]{:S(2)}) collective-permute-start(f32[32,8,128]{2,1,0:T(8,128)S(1)} %get-tuple-element.68), channel_id=1, source_target_pairs={{0,40},{8,48},{16,56},{24,0},{32,8},{40,16},{48,24},{56,32},{1,41}... | collective-permute-start | bytes 393224 | tf_op jit(solution)/shard_map/ppermute | solution.py:578
  38.0 12.4 %collective-permute-start.11 = (f32[32,8,128]{2,1,0:T(8,128)S(1)}, f32[32,8,128]{2,1,0:T(8,128)S(1)}, u32[]{:S(2)}, u32[]{:S(2)}) collective-permute-start(f32[32,8,128]{2,1,0:T(8,128)S(1)} %get-tuple-element.69), channel_id=1, source_target_pairs={{0,32},{8,40},{16,48},{24,56},{32,0},{40,8},{48,16},{56,24},{1,33}... | collective-permute-start | bytes 393224 | tf_op jit(solution)/shard_map/ppermute | solution.py:578
  38.2 12.1 %collective-permute-start.10 = (f32[32,8,128]{2,1,0:T(8,128)S(1)}, f32[32,8,128]{2,1,0:T(8,128)S(1)}, u32[]{:S(2)}, u32[]{:S(2)}) collective-permute-start(f32[32,8,128]{2,1,0:T(8,128)S(1)} %get-tuple-element.70), channel_id=1, source_target_pairs={{0,24},{8,32},{16,40},{24,48},{32,56},{40,0},{48,8},{56,16},{1,25}... | collective-permute-start | bytes 393224 | tf_op jit(solution)/shard_map/ppermute | solution.py:578
  40.3 10.1 %collective-permute-start.9 = (f32[32,8,128]{2,1,0:T(8,128)S(1)}, f32[32,8,128]{2,1,0:T(8,128)S(1)}, u32[]{:S(2)}, u32[]{:S(2)}) collective-permute-start(f32[32,8,128]{2,1,0:T(8,128)S(1)} %get-tuple-element.71), channel_id=1, source_target_pairs={{0,16},{8,24},{16,32},{24,40},{32,48},{40,56},{48,0},{56,8},{1,17}... | collective-permute-start | bytes 393224 | tf_op jit(solution)/shard_map/ppermute | solution.py:578
  49.3 4.4 %collective-permute-start.8 = (f32[32,8,128]{2,1,0:T(8,128)S(1)}, f32[32,8,128]{2,1,0:T(8,128)S(1)}, u32[]{:S(2)}, u32[]{:S(2)}) collective-permute-start(f32[32,8,128]{2,1,0:T(8,128)S(1)} %get-tuple-element.72), channel_id=1, source_target_pairs={{0,8},{8,16},{16,24},{24,32},{32,40},{40,48},{48,56},{56,0},{1,9},... | collective-permute-start | bytes 393224 | tf_op jit(solution)/shard_map/ppermute | solution.py:578
